TPU v7x, 32 devices: a whole 2x2x4 slice. The times are simulated.
32 devices in a mesh: gz: 4 (over y, x), gx: 8 (over z, core).
Axes of the slice: x: 2, y: 2, z: 4, core: 2. Of those that a mesh axis runs over, the one named last changes fastest.
Arguments:
- substrate: float32 [64, 256, 1024], P('gz', 'gx'), may hold values from 0 to 1
- catalyst: float32 [64, 256, 1024], P('gz', 'gx'), may hold values from 0 to 1
- extinction: float32 [2], replicated, may hold values from 0.25 to 1
- emission: float32 [3, 2], replicated, may hold values from 0.5 to 2
Outputs:
- substrate_next: float32 [64, 256, 1024], P('gz', 'gx')
- catalyst_next: float32 [64, 256, 1024], P('gz', 'gx')
- image: float32 [4, 256, 1024], P(None, 'gx', 'gz')
All inputs are finite; a program needn't handle non-finite values.
Results may differ from a plain program's by a relative error of at most 0.00004.
Values sent between devices are 32-bit elements; how exact they have to be, the bound alone decides.
No kernel may reach another device: no remote copies, remote signals or barrier semaphores. Data moves between devices by JAX's collectives and lax.ppermute only.
A program may use at most 64 MiB of HBM per device.

v0:
```python
import functools

import jax
import jax.numpy as jnp
from jax import lax
from jax.experimental import pallas as pl
from jax.experimental.pallas import tpu as pltpu
from jax.sharding import PartitionSpec as P


RATES = (0.16, 0.08)
FEED = 0.037
KILL = 0.06
OPTICAL = 4.0
ROWS = 8

HBM = pl.BlockSpec(memory_space=pltpu.HBM)
VMEM = pl.BlockSpec(memory_space=pltpu.VMEM)
SMEM = pl.BlockSpec(memory_space=pltpu.SMEM)


def f32(*shape):
    return jax.ShapeDtypeStruct(shape, jnp.float32)


def hbm(x):
    return pltpu.with_memory_space_constraint(x, pltpu.HBM)


def lanes(x):
    return pltpu.roll(x, 1, axis=x.ndim - 1) + pltpu.roll(x, x.shape[-1] - 1, axis=x.ndim - 1)


def react(sub, cat, around_sub, around_cat):
    growth = sub * cat * cat
    sub_new = (1.0 - 6.0 * RATES[0] - FEED) * sub + RATES[0] * around_sub - growth + FEED
    cat_new = (1.0 - 6.0 * RATES[1] - FEED - KILL) * cat + RATES[1] * around_cat + growth
    return sub_new, cat_new


def plane_step(load, low_rows, high_rows, across, store):
    first = low_rows[0].shape[-1]
    index = lax.broadcasted_iota(jnp.int32, (ROWS, first), 0)
    top, bottom = index == 0, index == ROWS - 1
    for tile in range(load.tiles):
        sums, olds = [], []
        for s in range(2):
            old = load(s, tile)
            above = low_rows[s] if tile == 0 else load(s, tile - 1)[ROWS - 1 :]
            below = high_rows[s] if tile == load.tiles - 1 else load(s, tile + 1)[:1]
            up = jnp.where(top, jnp.broadcast_to(above, old.shape), pltpu.roll(old, 1, axis=0))
            down = jnp.where(bottom, jnp.broadcast_to(below, old.shape), pltpu.roll(old, ROWS - 1, axis=0))
            around = lanes(old) + (up + down)
            beside = across(s, tile)
            sums.append(around if beside is None else around + beside)
            olds.append(old)
        store(tile, *react(olds[0], olds[1], sums[0], sums[1]))


class Tiles:
    def __init__(self, sub, cat):
        self.refs = (sub, cat)
        self.tiles = sub.shape[0] // ROWS

    def __call__(self, s, tile):
        return self.refs[s][pl.ds(tile * ROWS, ROWS), :]


def planes_kernel(sub, cat, front, back, sems):
    depth = sub.shape[0]
    copies = []
    for s, field in enumerate((sub, cat)):
        for plane, out in ((0, front), (depth - 1, back)):
            copies.append(pltpu.make_async_copy(field.at[plane], out.at[s], sems.at[len(copies)]))
    for copy in copies:
        copy.start()
    for copy in copies:
        copy.wait()


def rows_kernel(sub, cat, low, high, second, penult, heads, tails, sems):
    depth, rows, _ = sub.shape
    copies = []
    for s, field in enumerate((sub, cat)):
        for source, out in (
            (field.at[:, :ROWS], heads.at[s]),
            (field.at[:, rows - ROWS :], tails.at[s]),
            (field.at[1], second.at[s]),
            (field.at[depth - 2], penult.at[s]),
        ):
            copies.append(pltpu.make_async_copy(source, out, sems.at[len(copies)]))
    for copy in copies:
        copy.start()
    for copy in copies:
        copy.wait()
    for s in range(2):
        for row in range(2):
            for plane in range(depth):
                low[s, row, plane : plane + 1] = heads[s, plane, row : row + 1]
                high[s, row, plane : plane + 1] = tails[s, plane, ROWS - 2 + row : ROWS - 1 + row]


def edge_kernel(front, back, second, penult, from_low, from_high, q_low, q_high):
    depth = from_low.shape[2]
    for plane, outer, inner, out in ((0, front, second, q_low), (depth - 1, back, penult, q_high)):
        load = Tiles(outer.at[0], outer.at[1])
        inside = Tiles(inner.at[0], inner.at[1])

        def store(tile, sub, cat, out=out):
            out[0, pl.ds(tile * ROWS, ROWS), :] = sub
            out[1, pl.ds(tile * ROWS, ROWS), :] = cat

        plane_step(
            load,
            [from_low[s, 1, plane : plane + 1] for s in range(2)],
            [from_high[s, 0, plane : plane + 1] for s in range(2)],
            inside,
            store,
        )


def composite(sub, cat, scale_sub, scale_cat, clear):
    keep = jnp.exp(-(scale_sub * sub + scale_cat * cat))
    weight = clear * (1.0 - keep)
    return weight * sub, weight * cat, clear * keep


def inner_kernel(
    share, scale, emission, me, sub_hbm, cat_hbm, from_low, from_high, own_low, own_high,
    sub_out, cat_out, seen, near, far, rows_low, rows_high,
    old, mid, new, sem_in, sem_out,
):
    del emission, me
    depth, rows, columns = sub_hbm.shape
    chunk = 2
    chunks = depth // chunk
    inputs = (sub_hbm, cat_hbm)
    outputs = (sub_out, cat_out)

    def fetch(s, c):
        return pltpu.make_async_copy(
            inputs[s].at[pl.ds(c * chunk, chunk)], old.at[s, pl.ds(c * chunk, chunk)], sem_in.at[s, c]
        )

    def put(s, c):
        return pltpu.make_async_copy(
            new.at[s, pl.ds(c * chunk, chunk)], outputs[s].at[pl.ds(c * chunk, chunk)], sem_out.at[s, c]
        )

    for c in range(chunks):
        for s in range(2):
            fetch(s, c).start()

    which = lax.broadcasted_iota(jnp.int32, (depth, columns), 0)
    for got, at, own, at_own, out in (
        (from_low, 1, own_low, 0, rows_low),
        (from_high, 0, own_high, 1, rows_high),
    ):
        sums, olds = [], []
        for s in range(2):
            here = got[s, at]
            ahead = jnp.where(which == 0, 0.0, pltpu.roll(here, 1, axis=0))
            behind = jnp.where(which == depth - 1, 0.0, pltpu.roll(here, depth - 1, axis=0))
            sums.append(lanes(here) + (got[s, 1 - at] + own[s, at_own]) + (ahead + behind))
            olds.append(here)
        sub, cat = react(olds[0], olds[1], sums[0], sums[1])
        out[0] = sub
        out[1] = cat

    def first(k):
        def store(tile, sub, cat):
            mid[0, k, pl.ds(tile * ROWS, ROWS), :] = sub
            mid[1, k, pl.ds(tile * ROWS, ROWS), :] = cat

        def across(s, tile):
            span = pl.ds(tile * ROWS, ROWS)
            return old[s, k - 1, span, :] + old[s, k + 1, span, :]

        plane_step(
            Tiles(old.at[0, k], old.at[1, k]),
            [from_low[s, 1, pl.ds(k, 1)] for s in range(2)],
            [from_high[s, 0, pl.ds(k, 1)] for s in range(2)],
            across,
            store,
        )

    scale_sub, scale_cat = scale[0] * share, scale[1] * share
    seen[0] = jnp.zeros((rows, columns), jnp.float32)
    seen[1] = jnp.zeros((rows, columns), jnp.float32)
    seen[2] = jnp.ones((rows, columns), jnp.float32)

    def second(k):
        def store(tile, sub, cat):
            span = pl.ds(tile * ROWS, ROWS)
            new[0, k, span, :] = sub
            new[1, k, span, :] = cat
            one, two, clear = composite(sub, cat, scale_sub, scale_cat, seen[2, span, :])
            seen[0, span, :] += one
            seen[1, span, :] += two
            seen[2, span, :] = clear

        def across(s, tile):
            span = pl.ds(tile * ROWS, ROWS)
            return mid[s, k - 1, span, :] + mid[s, k + 1, span, :]

        plane_step(
            Tiles(mid.at[0, k], mid.at[1, k]),
            [rows_low[s, pl.ds(k, 1)] for s in range(2)],
            [rows_high[s, pl.ds(k, 1)] for s in range(2)],
            across,
            store,
        )

    for s in range(2):
        fetch(s, 0).wait()

    @pl.loop(1, chunks)
    def _(c):
        for s in range(2):
            fetch(s, c).wait()
        for j in range(chunk):
            first(c * chunk + j - 1)

    @pl.loop(1, chunks - 1)
    def _(c):
        for j in range(chunk):
            second(c * chunk + j)
        for s in range(2):
            put(s, c).start()

    for s in range(2):
        for j in range(2):
            near[s, j] = mid[s, 1 + j]
            far[s, j] = mid[s, depth - 3 + j]

    @pl.loop(1, chunks - 1)
    def _(c):
        for s in range(2):
            put(s, c).wait()


def corner_kernel(p_low, p_high, first, last):
    rows = p_low.shape[1]
    for side, p in enumerate((p_low, p_high)):
        for s in range(2):
            first[side, s : s + 1] = p[s, :1]
            last[side, s : s + 1] = p[s, rows - 1 :]


def rim_kernel(
    share, scale, q_low, q_high, p_low, p_high, front, back, near, far, rows_low, rows_high, corner_low, corner_high, inner,
    ring, known, seen, mid,
):
    depth = rows_low.shape[1]
    rows, _ = q_low.shape[1:]
    scale_sub, scale_cat = scale[0] * share, scale[1] * share
    for side, q, p, own, inside in ((0, q_low, p_low, front, near), (1, q_high, p_high, back, far)):
        outer = 0 if side == 0 else depth - 1
        inner_plane = 1 if side == 0 else depth - 2
        one, two = (0, 1) if side == 0 else (1, 0)
        for s in range(2):
            mid[side, s] = q[s] + RATES[s] * p[s]

        def store_known(tile, sub, cat, side=side, own=own):
            span = pl.ds(tile * ROWS, ROWS)
            known[side, 0, span, :] = sub + (RATES[0] * RATES[0]) * own[0, span, :]
            known[side, 1, span, :] = cat + (RATES[1] * RATES[1]) * own[1, span, :]

        def across_known(s, tile, inside=inside, one=one):
            return inside[s, one, pl.ds(tile * ROWS, ROWS), :]

        plane_step(
            Tiles(mid.at[side, 0], mid.at[side, 1]),
            [rows_low[s, outer : outer + 1] + RATES[s] * corner_low[side, s : s + 1] for s in range(2)],
            [rows_high[s, outer : outer + 1] + RATES[s] * corner_high[side, s : s + 1] for s in range(2)],
            across_known,
            store_known,
        )

        def store_ring(tile, sub, cat, side=side):
            span = pl.ds(tile * ROWS, ROWS)
            ring[0, side, span, :] = sub
            ring[1, side, span, :] = cat

        def across_ring(s, tile, side=side, inside=inside, two=two):
            span = pl.ds(tile * ROWS, ROWS)
            return inside[s, two, span, :] + mid[side, s, span, :]

        plane_step(
            Tiles(inside.at[0, one], inside.at[1, one]),
            [rows_low[s, inner_plane : inner_plane + 1] for s in range(2)],
            [rows_high[s, inner_plane : inner_plane + 1] for s in range(2)],
            across_ring,
            store_ring,
        )

    for tile in range(rows // ROWS):
        span = pl.ds(tile * ROWS, ROWS)
        one, two, clear = composite(ring[0, 0, span, :], ring[1, 0, span, :], scale_sub, scale_cat, 1.0)
        sub = one + clear * inner[0, span, :]
        cat = two + clear * inner[1, span, :]
        clear = clear * inner[2, span, :]
        one, two, clear = composite(ring[0, 1, span, :], ring[1, 1, span, :], scale_sub, scale_cat, clear)
        seen[0, span, :] = sub + one
        seen[1, span, :] = cat + two
        seen[2, span, :] = clear


def last_kernel(share, scale, me, known, q_low, q_high, seen, *outs_and_scratch):
    *pieces, outer, whole = outs_and_scratch
    rows, columns = seen.shape[1:]
    count = len(pieces)
    wide = columns // count
    scale_sub, scale_cat = scale[0] * share, scale[1] * share
    for tile in range(rows // ROWS):
        span = pl.ds(tile * ROWS, ROWS)
        low = [known[0, s, span, :] + RATES[s] * q_low[s, span, :] for s in range(2)]
        high = [known[1, s, span, :] + RATES[s] * q_high[s, span, :] for s in range(2)]
        for s in range(2):
            outer[s, 0, span, :] = low[s]
            outer[s, 1, span, :] = high[s]
        one, two, clear = composite(low[0], low[1], scale_sub, scale_cat, 1.0)
        sub = one + clear * seen[0, span, :]
        cat = two + clear * seen[1, span, :]
        clear = clear * seen[2, span, :]
        one, two, clear = composite(high[0], high[1], scale_sub, scale_cat, clear)
        whole[0, span, :] = sub + one
        whole[1, span, :] = cat + two
        whole[2, span, :] = clear
    for shift, piece in enumerate(pieces):
        target = lax.rem(me[0] + shift, count)
        if wide % 128 == 0:
            piece[...] = whole[:, :, pl.ds(pl.multiple_of(target * wide, 128), wide)]
        else:
            for other in range(count):

                @pl.when(target == other)
                def _(piece=piece, other=other):
                    piece[...] = whole[:, :, other * wide : (other + 1) * wide]


def shade_kernel(emission, me, *pieces_and_rest):
    *pieces, image, slabs = pieces_and_rest
    count = len(pieces)
    for shift, piece in enumerate(pieces):
        slabs[lax.rem(me[0] + count - shift, count)] = piece[...]
    sub, cat, clear = slabs[0, 0], slabs[0, 1], slabs[0, 2]
    for slab in range(1, count):
        sub = sub + clear * slabs[slab, 0]
        cat = cat + clear * slabs[slab, 1]
        clear = clear * slabs[slab, 2]
    for channel in range(3):
        image[channel] = emission[channel, 0] * sub + emission[channel, 1] * cat
    image[3] = 1.0 - clear


def place_kernel(ring, outer, sub_in, cat_in, sub_out, cat_out, sems):
    del sub_in, cat_in
    depth = sub_out.shape[0]
    outputs = (sub_out, cat_out)
    copies = []
    for s in range(2):
        for side in range(2):
            for at, source in ((side * (depth - 1), outer), (1 + side * (depth - 3), ring)):
                copies.append(pltpu.make_async_copy(source.at[s, side], outputs[s].at[at], sems.at[len(copies)]))
    for copy in copies:
        copy.start()
    for copy in copies:
        copy.wait()


def call(kernel, flops, room, **kwargs):
    return pl.pallas_call(
        kernel,
        cost_estimate=pl.CostEstimate(flops=flops, bytes_accessed=1 << 16, transcendentals=0),
        compiler_params=pltpu.CompilerParams(vmem_limit_bytes=room << 20),
        **kwargs,
    )


def body(substrate, catalyst, extinction, emission):
    depth, rows, columns = substrate.shape
    count = lax.axis_size("gz")
    wide = columns // count
    me = lax.axis_index("gz").astype(jnp.int32)[None]
    share = OPTICAL / (depth * count)

    def ring(size, shift):
        return [(i, (i + shift) % size) for i in range(size)]

    def up(x, axis):
        return lax.ppermute(x, axis, ring(lax.axis_size(axis), 1))

    def down(x, axis):
        return lax.ppermute(x, axis, ring(lax.axis_size(axis), -1))

    front, back = call(
        planes_kernel,
        1 << 20,
        2,
        name="planes",
        out_shape=(f32(2, rows, columns), f32(2, rows, columns)),
        in_specs=[HBM, HBM],
        out_specs=(VMEM, VMEM),
        scratch_shapes=[pltpu.SemaphoreType.DMA((4,))],
    )(hbm(substrate), hbm(catalyst))
    p_low = up(back, "gz")
    p_high = down(front, "gz")
    own_low, own_high, second, penult = call(
        rows_kernel,
        1 << 20,
        8,
        name="rows",
        out_shape=(
            f32(2, 2, depth, columns),
            f32(2, 2, depth, columns),
            f32(2, rows, columns),
            f32(2, rows, columns),
        ),
        in_specs=[HBM, HBM],
        out_specs=(VMEM, VMEM, VMEM, VMEM),
        scratch_shapes=[
            pltpu.VMEM((2, depth, ROWS, columns), jnp.float32),
            pltpu.VMEM((2, depth, ROWS, columns), jnp.float32),
            pltpu.SemaphoreType.DMA((8,)),
        ],
    )(hbm(substrate), hbm(catalyst))
    from_low = up(own_high, "gx")
    from_high = down(own_low, "gx")

    q_low, q_high = call(
        edge_kernel,
        1 << 22,
        8,
        name="edge",
        out_shape=(f32(2, rows, columns), f32(2, rows, columns)),
        in_specs=[VMEM] * 6,
        out_specs=(VMEM, VMEM),
    )(front, back, second, penult, from_low, from_high)
    q_from_low = up(q_high, "gz")
    q_from_high = down(q_low, "gz")

    sub_part, cat_part, inner, near, far, rows_low, rows_high = call(
        functools.partial(inner_kernel, share),
        1 << 26,
        24,
        name="inner",
        out_shape=(
            f32(depth, rows, columns),
            f32(depth, rows, columns),
            f32(3, rows, columns),
            f32(2, 2, rows, columns),
            f32(2, 2, rows, columns),
            f32(2, depth, columns),
            f32(2, depth, columns),
        ),
        in_specs=[SMEM, SMEM, SMEM, HBM, HBM, VMEM, VMEM, VMEM, VMEM],
        out_specs=(HBM, HBM, VMEM, VMEM, VMEM, VMEM, VMEM),
        scratch_shapes=[
            pltpu.VMEM((2, depth, rows, columns), jnp.float32),
            pltpu.VMEM((2, depth, rows, columns), jnp.float32),
            pltpu.VMEM((2, depth, rows, columns), jnp.float32),
            pltpu.SemaphoreType.DMA((2, depth // 2)),
            pltpu.SemaphoreType.DMA((2, depth // 2)),
        ],
    )(extinction, emission, me, hbm(substrate), hbm(catalyst), from_low, from_high, own_low, own_high)

    p_low, p_high, inner = lax.optimization_barrier((p_low, p_high, inner))
    first_rows, last_rows = call(
        corner_kernel,
        1 << 18,
        2,
        name="corner",
        out_shape=(f32(2, 2, columns), f32(2, 2, columns)),
        in_specs=[VMEM, VMEM],
        out_specs=(VMEM, VMEM),
    )(p_low, p_high)
    corner_low = up(last_rows, "gx")
    corner_high = down(first_rows, "gx")

    ring_planes, known, seen = call(
        functools.partial(rim_kernel, share),
        1 << 23,
        12,
        name="rim",
        out_shape=(f32(2, 2, rows, columns), f32(2, 2, rows, columns), f32(3, rows, columns)),
        in_specs=[SMEM] + [VMEM] * 13,
        out_specs=(VMEM, VMEM, VMEM),
        scratch_shapes=[pltpu.VMEM((2, 2, rows, columns), jnp.float32)],
    )(
        extinction, q_low, q_high, p_low, p_high, front, back, near, far, rows_low, rows_high, corner_low, corner_high, inner
    )

    *pieces, outer = call(
        functools.partial(last_kernel, share),
        1 << 22,
        8,
        name="last",
        out_shape=(*[f32(3, rows, wide)] * count, f32(2, 2, rows, columns)),
        in_specs=[SMEM, SMEM] + [VMEM] * 4,
        out_specs=tuple([VMEM] * (count + 1)),
        scratch_shapes=[pltpu.VMEM((3, rows, columns), jnp.float32)],
    )(extinction, me, known, q_from_low, q_from_high, seen)

    received = [pieces[0]]
    for shift in range(1, count):
        received.append(lax.ppermute(pieces[shift], "gz", ring(count, shift)))

    sub_final, cat_final = call(
        place_kernel,
        1 << 22,
        4,
        name="place",
        out_shape=(f32(depth, rows, columns), f32(depth, rows, columns)),
        in_specs=[VMEM, VMEM, HBM, HBM],
        out_specs=(HBM, HBM),
        input_output_aliases={2: 0, 3: 1},
        scratch_shapes=[pltpu.SemaphoreType.DMA((8,))],
    )(ring_planes, outer, sub_part, cat_part)

    image = call(
        shade_kernel,
        1 << 20,
        8,
        name="shade",
        out_shape=f32(4, rows, wide),
        in_specs=[SMEM, SMEM] + [VMEM] * count,
        out_specs=VMEM,
        scratch_shapes=[pltpu.VMEM((count, 3, rows, wide), jnp.float32)],
    )(emission, me, *received)
    return sub_final, cat_final, image


def solution(mesh):
    placed = (P("gz", "gx", None), P("gz", "gx", None), P(), P())

    return jax.shard_map(
        body,
        mesh=mesh,
        in_specs=placed,
        out_specs=(P("gz", "gx", None), P("gz", "gx", None), P(None, "gx", "gz")),
        check_vma=False,
    )
```

profile of v0, /device:TPU:0, one launch (start us, length us, event | category | flops | bytes accessed | tf_op | source)
XLA Modules:
  0.0 42.7 jit_solution(9941999832661951481)
XLA Ops:
  0.6 1.9 %rows.1 = (f32[2,2,16,1024]{3,2,1,0:T(8,128)S(1)}, f32[2,2,16,1024]{3,2,1,0:T(8,128)S(1)}, f32[2,32,1024]{2,1,0:T(8,128)S(1)}, f32[2,32,1024]{2,1,0:T(8,128)S(1)}) custom-call(f32[16,32,1024]{2,1,0:T(8,128)} %sub_hbm.1, f32[16,32,1024]{2,1,0:T(8,128)} %cat_hbm.1), custom_call_target="tpu_custom_call" | custom-call | flops 1048576 | bytes 65536 | tf_op jit(solution)/shard_map/rows/pallas_call | solution.py:409
  2.5 0.5 %collective-permute-start = (f32[2,2,16,1024]{3,2,1,0:T(8,128)S(1)}, f32[2,2,16,1024]{3,2,1,0:T(8,128)S(1)}, u32[]{:S(2)}, u32[]{:S(2)}) collective-permute-start(f32[2,2,16,1024]{3,2,1,0:T(8,128)S(1)} %get-tuple-element.37.own_high), channel_id=1, source_target_pairs={{0,1},{1,2},{2,3},{3,4},{4,5},{5,6},{6,7},{7,0},{8,9},{9,10},{10,1... | collective-permute-start | bytes 786440 | tf_op jit(solution)/shard_map/ppermute | solution.py:392
  3.0 0.0 copy-start.1
  3.0 0.0 copy-start
  3.1 4.1 %collective-permute-start.1 = (f32[2,2,16,1024]{3,2,1,0:T(8,128)S(1)}, f32[2,2,16,1024]{3,2,1,0:T(8,128)S(1)}, u32[]{:S(2)}, u32[]{:S(2)}) collective-permute-start(f32[2,2,16,1024]{3,2,1,0:T(8,128)S(1)} %get-tuple-element.38.own_low), channel_id=1, source_target_pairs={{0,7},{1,0},{2,1},{3,2},{4,3},{5,4},{6,5},{7,6},{8,15},{9,8},{10,9... | collective-permute-start | bytes 786440 | tf_op jit(solution)/shard_map/ppermute | solution.py:395
  7.2 1.1 %planes.1 = (f32[2,32,1024]{2,1,0:T(8,128)S(1)}, f32[2,32,1024]{2,1,0:T(8,128)S(1)}) custom-call(f32[16,32,1024]{2,1,0:T(8,128)} %sub_hbm.1, f32[16,32,1024]{2,1,0:T(8,128)} %cat_hbm.1), custom_call_target="tpu_custom_call" | custom-call | flops 1048576 | bytes 65536 | tf_op jit(solution)/shard_map/planes/pallas_call | solution.py:397
  8.3 2.0 %collective-permute-start.2 = (f32[2,32,1024]{2,1,0:T(8,128)S(1)}, f32[2,32,1024]{2,1,0:T(8,128)S(1)}, u32[]{:S(2)}, u32[]{:S(2)}) collective-permute-start(f32[2,32,1024]{2,1,0:T(8,128)S(1)} %get-tuple-element.34.back), channel_id=1, source_target_pairs={{0,8},{8,16},{16,24},{24,0},{1,9},{9,17},{17,25},{25,1},{2,10},{10... | collective-permute-start | bytes 786440 | tf_op jit(solution)/shard_map/ppermute | solution.py:392
  10.3 1.0 %collective-permute-start.3 = (f32[2,32,1024]{2,1,0:T(8,128)S(1)}, f32[2,32,1024]{2,1,0:T(8,128)S(1)}, u32[]{:S(2)}, u32[]{:S(2)}) collective-permute-start(f32[2,32,1024]{2,1,0:T(8,128)S(1)} %get-tuple-element.33.front), channel_id=1, source_target_pairs={{0,24},{8,0},{16,8},{24,16},{1,25},{9,1},{17,9},{25,17},{2,26},{10... | collective-permute-start | bytes 786440 | tf_op jit(solution)/shard_map/ppermute | solution.py:395
  11.3 0.1 collective-permute-done.from_low
  11.3 0.4 %collective-permute-done.1.from_high = f32[2,2,16,1024]{3,2,1,0:T(8,128)S(1)} collective-permute-done((f32[2,2,16,1024]{3,2,1,0:T(8,128)S(1)}, f32[2,2,16,1024]{3,2,1,0:T(8,128)S(1)}, u32[]{:S(2)}, u32[]{:S(2)}) %collective-permute-start.1) | collective-permute-done | bytes 262176 | tf_op jit(solution)/shard_map/ppermute | solution.py:395
  11.8 0.3 edge.1
  12.1 2.1 %collective-permute-start.6 = (f32[2,32,1024]{2,1,0:T(8,128)S(1)}, f32[2,32,1024]{2,1,0:T(8,128)S(1)}, u32[]{:S(2)}, u32[]{:S(2)}) collective-permute-start(f32[2,32,1024]{2,1,0:T(8,128)S(1)} %get-tuple-element.40.q_high), channel_id=1, source_target_pairs={{0,8},{8,16},{16,24},{24,0},{1,9},{9,17},{17,25},{25,1},{2,10},{10... | collective-permute-start | bytes 786440 | tf_op jit(solution)/shard_map/ppermute | solution.py:392
  14.2 1.0 %collective-permute-start.7 = (f32[2,32,1024]{2,1,0:T(8,128)S(1)}, f32[2,32,1024]{2,1,0:T(8,128)S(1)}, u32[]{:S(2)}, u32[]{:S(2)}) collective-permute-start(f32[2,32,1024]{2,1,0:T(8,128)S(1)} %get-tuple-element.39.q_low), channel_id=1, source_target_pairs={{0,24},{8,0},{16,8},{24,16},{1,25},{9,1},{17,9},{25,17},{2,26},{10... | collective-permute-start | bytes 786440 | tf_op jit(solution)/shard_map/ppermute | solution.py:395
  15.2 0.0 copy-done.1
  15.3 0.1 copy.9.emission
  15.3 0.0 copy-done
  15.3 8.3 %inner.1 = (f32[16,32,1024]{2,1,0:T(8,128)}, f32[16,32,1024]{2,1,0:T(8,128)}, f32[3,32,1024]{2,1,0:T(8,128)S(1)}, f32[2,2,32,1024]{3,2,1,0:T(8,128)S(1)}, f32[2,...) custom-call(f32[2]{0:T(128)S(1)} %copy-done, f32[3,2]{1,0:T(4,128)S(1)} %copy.9.emission, ...), custom_call_target="tpu_custom_call" | custom-call | flops 67108864 | bytes 65536 | tf_op jit(solution)/shard_map/inner/pallas_call | solution.py:443
  23.7 0.0 collective-permute-done.2.p_low
  23.7 0.8 %collective-permute-done.3.p_high = f32[2,32,1024]{2,1,0:T(8,128)S(1)} collective-permute-done((f32[2,32,1024]{2,1,0:T(8,128)S(1)}, f32[2,32,1024]{2,1,0:T(8,128)S(1)}, u32[]{:S(2)}, u32[]{:S(2)}) %collective-permute-start.3) | collective-permute-done | bytes 262176 | tf_op jit(solution)/shard_map/ppermute | solution.py:395
  24.5 1.2 %collective-permute-start.4 = (f32[2,2,1024]{2,1,0:T(2,128)S(1)}, f32[2,2,1024]{2,1,0:T(2,128)S(1)}, u32[]{:S(2)}, u32[]{:S(2)}) collective-permute-start(f32[2,2,1024]{2,1,0:T(2,128)S(1)} %get-tuple-element.48), channel_id=1, source_target_pairs={{0,1},{1,2},{2,3},{3,4},{4,5},{5,6},{6,7},{7,0},{8,9},{9,10},{10,1... | collective-permute-start | bytes 49160 | tf_op jit(solution)/shard_map/ppermute | solution.py:392
  25.7 2.4 %collective-permute-start.5 = (f32[2,2,1024]{2,1,0:T(2,128)S(1)}, f32[2,2,1024]{2,1,0:T(2,128)S(1)}, u32[]{:S(2)}, u32[]{:S(2)}) collective-permute-start(f32[2,2,1024]{2,1,0:T(2,128)S(1)} %get-tuple-element.49), channel_id=1, source_target_pairs={{0,7},{1,0},{2,1},{3,2},{4,3},{5,4},{6,5},{7,6},{8,15},{9,8},{10,9... | collective-permute-start | bytes 49160 | tf_op jit(solution)/shard_map/ppermute | solution.py:395
  28.1 1.4 %collective-permute-done.4.corner_low = f32[2,2,1024]{2,1,0:T(2,128)S(1)} collective-permute-done((f32[2,2,1024]{2,1,0:T(2,128)S(1)}, f32[2,2,1024]{2,1,0:T(2,128)S(1)}, u32[]{:S(2)}, u32[]{:S(2)}) %collective-permute-start.4) | collective-permute-done | bytes 16416 | tf_op jit(solution)/shard_map/ppermute | solution.py:392
  29.5 0.0 collective-permute-done.5.corner_high
  29.6 1.4 %rim.1 = (f32[2,2,32,1024]{3,2,1,0:T(8,128)S(1)}, f32[2,2,32,1024]{3,2,1,0:T(8,128)S(1)}, f32[3,32,1024]{2,1,0:T(8,128)S(1)}) custom-call(f32[2]{0:T(128)S(1)} %copy-done, f32[2,32,1024]{2,1,0:T(8,128)S(1)} %get-tuple-element.39.q_low, f32[2,32,1024]{2,1,0:T(8,128)S(1)} %get-tuple-element.40.q_high, f32[2,32,1024]{2,1,0:T(8,128)S(1)} %collective-permute-done.2.p_low, ...), custom_call_target="tpu_custom_call" | custom-call | flops 8388608 | bytes 65536 | tf_op jit(solution)/shard_map/rim/pallas_call | solution.py:481
  31.0 0.0 collective-permute-done.6.q_low
  31.0 2.0 %collective-permute-done.7.q_high = f32[2,32,1024]{2,1,0:T(8,128)S(1)} collective-permute-done((f32[2,32,1024]{2,1,0:T(8,128)S(1)}, f32[2,32,1024]{2,1,0:T(8,128)S(1)}, u32[]{:S(2)}, u32[]{:S(2)}) %collective-permute-start.7) | collective-permute-done | bytes 262176 | tf_op jit(solution)/shard_map/ppermute | solution.py:395
  33.0 0.7 %last.1 = (f32[3,32,256]{2,1,0:T(8,128)S(1)}, f32[3,32,256]{2,1,0:T(8,128)S(1)}, f32[3,32,256]{2,1,0:T(8,128)S(1)}, f32[3,32,256]{2,1,0:T(8,128)S(1)}, f32[2,2,32,1024]{3,2,1,0:T(8,128)S(1)}) custom-call(f32[2]{0:T(128)S(1)} %copy-done, s32[1]{0:T(128)} %bitcast.me, f32[2,2,32,1024]{3,2,1,0:T(8,128)S(1)} %get-tuple-element.52.known, ...), custom_call_target="tpu_custom_call" | custom-call | flops 4194304 | bytes 65536 | tf_op jit(solution)/shard_map/last/pallas_call | solution.py:494
  33.7 1.5 %collective-permute-start.10 = (f32[3,32,256]{2,1,0:T(8,128)S(1)}, f32[3,32,256]{2,1,0:T(8,128)S(1)}, u32[]{:S(2)}, u32[]{:S(2)}) collective-permute-start(f32[3,32,256]{2,1,0:T(8,128)S(1)} %get-tuple-element.62), channel_id=1, source_target_pairs={{0,24},{8,0},{16,8},{24,16},{1,25},{9,1},{17,9},{25,17},{2,26},{10... | collective-permute-start | bytes 294920 | tf_op jit(solution)/shard_map/ppermute | solution.py:507
  35.2 0.6 %collective-permute-start.8 = (f32[3,32,256]{2,1,0:T(8,128)S(1)}, f32[3,32,256]{2,1,0:T(8,128)S(1)}, u32[]{:S(2)}, u32[]{:S(2)}) collective-permute-start(f32[3,32,256]{2,1,0:T(8,128)S(1)} %get-tuple-element.60), channel_id=1, source_target_pairs={{0,8},{8,16},{16,24},{24,0},{1,9},{9,17},{17,25},{25,1},{2,10},{10... | collective-permute-start | bytes 294920 | tf_op jit(solution)/shard_map/ppermute | solution.py:507
  35.8 0.9 %collective-permute-start.9 = (f32[3,32,256]{2,1,0:T(8,128)S(1)}, f32[3,32,256]{2,1,0:T(8,128)S(1)}, u32[]{:S(2)}, u32[]{:S(2)}) collective-permute-start(f32[3,32,256]{2,1,0:T(8,128)S(1)} %get-tuple-element.61), channel_id=1, source_target_pairs={{0,16},{8,24},{16,0},{24,8},{1,17},{9,25},{17,1},{25,9},{2,18},{10... | collective-permute-start | bytes 294920 | tf_op jit(solution)/shard_map/ppermute | solution.py:507
  36.7 1.0 %place.1 = (f32[16,32,1024]{2,1,0:T(8,128)}, f32[16,32,1024]{2,1,0:T(8,128)}) custom-call(f32[2,2,32,1024]{3,2,1,0:T(8,128)S(1)} %get-tuple-element.51.ring, f32[2,2,32,1024]{3,2,1,0:T(8,128)S(1)} %get-tuple-element.54.outer, f32[16,32,1024]{2,1,0:T(8,128)} %get-tuple-element.55.sub_in, ...), custom_call_target="tpu_custom_call", output_to_operand_aliasing={{0}: (2, {}), {1}: (3, {})} | custom-call | flops 4194304 | bytes 65536 | tf_op jit(solution)/shard_map/place/pallas_call | solution.py:509
  37.7 0.6 %collective-permute-done.10.pieces_and_rest_3_ = f32[3,32,256]{2,1,0:T(8,128)S(1)} collective-permute-done((f32[3,32,256]{2,1,0:T(8,128)S(1)}, f32[3,32,256]{2,1,0:T(8,128)S(1)}, u32[]{:S(2)}, u32[]{:S(2)}) %collective-permute-start.10) | collective-permute-done | bytes 98336 | tf_op jit(solution)/shard_map/ppermute | solution.py:507
  38.4 2.4 %collective-permute-done.8.pieces_and_rest_1_ = f32[3,32,256]{2,1,0:T(8,128)S(1)} collective-permute-done((f32[3,32,256]{2,1,0:T(8,128)S(1)}, f32[3,32,256]{2,1,0:T(8,128)S(1)}, u32[]{:S(2)}, u32[]{:S(2)}) %collective-permute-start.8) | collective-permute-done | bytes 98336 | tf_op jit(solution)/shard_map/ppermute | solution.py:507
  40.8 0.6 %collective-permute-done.9.pieces_and_rest_2_ = f32[3,32,256]{2,1,0:T(8,128)S(1)} collective-permute-done((f32[3,32,256]{2,1,0:T(8,128)S(1)}, f32[3,32,256]{2,1,0:T(8,128)S(1)}, u32[]{:S(2)}, u32[]{:S(2)}) %collective-permute-start.9) | collective-permute-done | bytes 98336 | tf_op jit(solution)/shard_map/ppermute | solution.py:507
  41.5 1.3 %shade.1 = f32[4,32,256]{2,1,0:T(8,128)} custom-call(f32[3,2]{1,0:T(4,128)S(1)} %copy.9.emission, s32[1]{0:T(128)} %bitcast.me, f32[3,32,256]{2,1,0:T(8,128)S(1)} %get-tuple-element.59.pieces_and_rest_0_, f32[3,32,256]{2,1,0:T(8,128)S(1)} %collective-permute-done.8.pieces_and_rest_1_, f32[3,32,256]{2,1,0:T(8,128)S(1)} %collective-permute-done.9.pieces_and_rest_2_, ...), custom_call_target="tpu_custom_call" | custom-call | flops 1048576 | bytes 65536 | tf_op jit(solution)/shard_map/shade/pallas_call | solution.py:521
  (1 shorter events, 0.0 us)
Async XLA Ops:
  2.5 8.8 %collective-permute-start = (f32[2,2,16,1024]{3,2,1,0:T(8,128)S(1)}, f32[2,2,16,1024]{3,2,1,0:T(8,128)S(1)}, u32[]{:S(2)}, u32[]{:S(2)}) collective-permute-start(f32[2,2,16,1024]{3,2,1,0:T(8,128)S(1)} %get-tuple-element.37.own_high), channel_id=1, source_target_pairs={{0,1},{1,2},{2,3},{3,4},{4,5},{5,6},{6,7},{7,0},{8,9},{9,10},{10,1... | collective-permute-start | bytes 786440 | tf_op jit(solution)/shard_map/ppermute | solution.py:392
  3.0 12.2 %copy-start.1 = (f32[3,2]{0,1:T(2,128)S(1)}, f32[3,2]{0,1:T(2,128)}, u32[]{:S(2)}) copy-start(f32[3,2]{0,1:T(2,128)} %param.7) | copy-start | bytes 76
  3.0 12.3 %copy-start = (f32[2]{0:T(128)S(1)}, f32[2]{0:T(128)}, u32[]{:S(2)}) copy-start(f32[2]{0:T(128)} %scale.5) | copy-start | bytes 28
  3.1 8.7 %collective-permute-start.1 = (f32[2,2,16,1024]{3,2,1,0:T(8,128)S(1)}, f32[2,2,16,1024]{3,2,1,0:T(8,128)S(1)}, u32[]{:S(2)}, u32[]{:S(2)}) collective-permute-start(f32[2,2,16,1024]{3,2,1,0:T(8,128)S(1)} %get-tuple-element.38.own_low), channel_id=1, source_target_pairs={{0,7},{1,0},{2,1},{3,2},{4,3},{5,4},{6,5},{7,6},{8,15},{9,8},{10,9... | collective-permute-start | bytes 786440 | tf_op jit(solution)/shard_map/ppermute | solution.py:395
  8.3 15.4 %collective-permute-start.2 = (f32[2,32,1024]{2,1,0:T(8,128)S(1)}, f32[2,32,1024]{2,1,0:T(8,128)S(1)}, u32[]{:S(2)}, u32[]{:S(2)}) collective-permute-start(f32[2,32,1024]{2,1,0:T(8,128)S(1)} %get-tuple-element.34.back), channel_id=1, source_target_pairs={{0,8},{8,16},{16,24},{24,0},{1,9},{9,17},{17,25},{25,1},{2,10},{10... | collective-permute-start | bytes 786440 | tf_op jit(solution)/shard_map/ppermute | solution.py:392
  10.3 14.3 %collective-permute-start.3 = (f32[2,32,1024]{2,1,0:T(8,128)S(1)}, f32[2,32,1024]{2,1,0:T(8,128)S(1)}, u32[]{:S(2)}, u32[]{:S(2)}) collective-permute-start(f32[2,32,1024]{2,1,0:T(8,128)S(1)} %get-tuple-element.33.front), channel_id=1, source_target_pairs={{0,24},{8,0},{16,8},{24,16},{1,25},{9,1},{17,9},{25,17},{2,26},{10... | collective-permute-start | bytes 786440 | tf_op jit(solution)/shard_map/ppermute | solution.py:395
  12.1 18.8 %collective-permute-start.6 = (f32[2,32,1024]{2,1,0:T(8,128)S(1)}, f32[2,32,1024]{2,1,0:T(8,128)S(1)}, u32[]{:S(2)}, u32[]{:S(2)}) collective-permute-start(f32[2,32,1024]{2,1,0:T(8,128)S(1)} %get-tuple-element.40.q_high), channel_id=1, source_target_pairs={{0,8},{8,16},{16,24},{24,0},{1,9},{9,17},{17,25},{25,1},{2,10},{10... | collective-permute-start | bytes 786440 | tf_op jit(solution)/shard_map/ppermute | solution.py:392
  14.2 18.7 %collective-permute-start.7 = (f32[2,32,1024]{2,1,0:T(8,128)S(1)}, f32[2,32,1024]{2,1,0:T(8,128)S(1)}, u32[]{:S(2)}, u32[]{:S(2)}) collective-permute-start(f32[2,32,1024]{2,1,0:T(8,128)S(1)} %get-tuple-element.39.q_low), channel_id=1, source_target_pairs={{0,24},{8,0},{16,8},{24,16},{1,25},{9,1},{17,9},{25,17},{2,26},{10... | collective-permute-start | bytes 786440 | tf_op jit(solution)/shard_map/ppermute | solution.py:395
  24.5 5.0 %collective-permute-start.4 = (f32[2,2,1024]{2,1,0:T(2,128)S(1)}, f32[2,2,1024]{2,1,0:T(2,128)S(1)}, u32[]{:S(2)}, u32[]{:S(2)}) collective-permute-start(f32[2,2,1024]{2,1,0:T(2,128)S(1)} %get-tuple-element.48), channel_id=1, source_target_pairs={{0,1},{1,2},{2,3},{3,4},{4,5},{5,6},{6,7},{7,0},{8,9},{9,10},{10,1... | collective-permute-start | bytes 49160 | tf_op jit(solution)/shard_map/ppermute | solution.py:392
  25.7 3.9 %collective-permute-start.5 = (f32[2,2,1024]{2,1,0:T(2,128)S(1)}, f32[2,2,1024]{2,1,0:T(2,128)S(1)}, u32[]{:S(2)}, u32[]{:S(2)}) collective-permute-start(f32[2,2,1024]{2,1,0:T(2,128)S(1)} %get-tuple-element.49), channel_id=1, source_target_pairs={{0,7},{1,0},{2,1},{3,2},{4,3},{5,4},{6,5},{7,6},{8,15},{9,8},{10,9... | collective-permute-start | bytes 49160 | tf_op jit(solution)/shard_map/ppermute | solution.py:395
  33.7 4.7 %collective-permute-start.10 = (f32[3,32,256]{2,1,0:T(8,128)S(1)}, f32[3,32,256]{2,1,0:T(8,128)S(1)}, u32[]{:S(2)}, u32[]{:S(2)}) collective-permute-start(f32[3,32,256]{2,1,0:T(8,128)S(1)} %get-tuple-element.62), channel_id=1, source_target_pairs={{0,24},{8,0},{16,8},{24,16},{1,25},{9,1},{17,9},{25,17},{2,26},{10... | collective-permute-start | bytes 294920 | tf_op jit(solution)/shard_map/ppermute | solution.py:507
  35.2 5.6 %collective-permute-start.8 = (f32[3,32,256]{2,1,0:T(8,128)S(1)}, f32[3,32,256]{2,1,0:T(8,128)S(1)}, u32[]{:S(2)}, u32[]{:S(2)}) collective-permute-start(f32[3,32,256]{2,1,0:T(8,128)S(1)} %get-tuple-element.60), channel_id=1, source_target_pairs={{0,8},{8,16},{16,24},{24,0},{1,9},{9,17},{17,25},{25,1},{2,10},{10... | collective-permute-start | bytes 294920 | tf_op jit(solution)/shard_map/ppermute | solution.py:507
  35.8 5.7 %collective-permute-start.9 = (f32[3,32,256]{2,1,0:T(8,128)S(1)}, f32[3,32,256]{2,1,0:T(8,128)S(1)}, u32[]{:S(2)}, u32[]{:S(2)}) collective-permute-start(f32[3,32,256]{2,1,0:T(8,128)S(1)} %get-tuple-element.61), channel_id=1, source_target_pairs={{0,16},{8,24},{16,0},{24,8},{1,17},{9,25},{17,1},{25,9},{2,18},{10... | collective-permute-start | bytes 294920 | tf_op jit(solution)/shard_map/ppermute | solution.py:507
where the time goes:
time: 42.9 us; the launch traced here: 42.7 us
  starting transfers between devices  17.4 us (41%)
  Pallas kernels  16.1 us (38%)
  waiting for transfers between devices  8.49 us (20%)
  between operations  0.71 us (2%)
    ppermute x4, starting transfers between devices, down(): return lax.ppermute(x, axis, ring(lax.axis_size(axis), -1))  8.59 us
    pallas_call x1, Pallas kernels, body(): call(functools.partial(inner_kernel, share), 1 << 26, 24, name='inner', o...  8.31 us
    ppermute x4, starting transfers between devices, up(): return lax.ppermute(x, axis, ring(lax.axis_size(axis), 1))  5.76 us
    ppermute x3, waiting for transfers between devices, body(): received.append(lax.ppermute(pieces[shift], 'gz', ring(count, shift)))  3.71 us
    ppermute x4, waiting for transfers between devices, down(): return lax.ppermute(x, axis, ring(lax.axis_size(axis), -1))  3.3 us
    ppermute x3, starting transfers between devices, body(): received.append(lax.ppermute(pieces[shift], 'gz', ring(count, shift)))  3.01 us
    pallas_call x1, Pallas kernels, body(): call(rows_kernel, 1 << 20, 8, name='rows', out_shape=(f32(2, 2, depth, co...  1.87 us
    ppermute x4, waiting for transfers between devices, up(): return lax.ppermute(x, axis, ring(lax.axis_size(axis), 1))  1.48 us
  transfers between devices with their start and end apart: 11, of which 8 were waited for; matrix products, arithmetic and copies ran while one was open for 0% of the time, Pallas kernels for 29%

commit v1 on v0

v1 whole, which is shorter than its diff:
```python
import functools

import jax
import jax.numpy as jnp
from jax import lax
from jax.experimental import pallas as pl
from jax.experimental.pallas import tpu as pltpu
from jax.sharding import PartitionSpec as P


RATES = (0.16, 0.08)
FEED = 0.037
KILL = 0.06
OPTICAL = 4.0
ROWS = 8

HBM = pl.BlockSpec(memory_space=pltpu.HBM)
VMEM = pl.BlockSpec(memory_space=pltpu.VMEM)
SMEM = pl.BlockSpec(memory_space=pltpu.SMEM)


def f32(*shape):
    return jax.ShapeDtypeStruct(shape, jnp.float32)


def hbm(x):
    return pltpu.with_memory_space_constraint(x, pltpu.HBM)


def lanes(x):
    return pltpu.roll(x, 1, axis=x.ndim - 1) + pltpu.roll(x, x.shape[-1] - 1, axis=x.ndim - 1)


def react(sub, cat, around_sub, around_cat):
    growth = sub * cat * cat
    sub_new = (1.0 - 6.0 * RATES[0] - FEED) * sub + RATES[0] * around_sub - growth + FEED
    cat_new = (1.0 - 6.0 * RATES[1] - FEED - KILL) * cat + RATES[1] * around_cat + growth
    return sub_new, cat_new


def plane_step(load, tiles, low_rows, high_rows, across, store):
    for tile in range(tiles):
        sums, olds = [], []
        for s in range(2):
            old = load(s, tile)
            index = lax.broadcasted_iota(jnp.int32, old.shape, 0)
            above = load(s, tile - 1)[ROWS - 1 :] if tile else low_rows and low_rows[s]
            below = load(s, tile + 1)[:1] if tile < tiles - 1 else high_rows and high_rows[s]
            above = 0.0 if above is None else jnp.broadcast_to(above, old.shape)
            below = 0.0 if below is None else jnp.broadcast_to(below, old.shape)
            up = jnp.where(index == 0, above, pltpu.roll(old, 1, axis=0))
            down = jnp.where(index == ROWS - 1, below, pltpu.roll(old, ROWS - 1, axis=0))
            sums.append(lanes(old) + (up + down) + across(s, tile))
            olds.append(old)
        store(tile, *react(olds[0], olds[1], sums[0], sums[1]))


def span(tile):
    return pl.ds(tile * ROWS, ROWS)


def planes_kernel(sub, cat, front, back, sems):
    depth = sub.shape[0]
    copies = []
    for s, field in enumerate((sub, cat)):
        for plane, out in ((0, front), (depth - 1, back)):
            copies.append(pltpu.make_async_copy(field.at[plane], out.at[s], sems.at[len(copies)]))
    for copy in copies:
        copy.start()
    for copy in copies:
        copy.wait()


def prepare_kernel(sub, cat, front, back, low, high, q_low, q_high, heads, tails, second, penult, sems):
    depth, rows, _ = sub.shape
    copies = []
    for s, field in enumerate((sub, cat)):
        for source, out in (
            (field.at[1], second.at[s]),
            (field.at[depth - 2], penult.at[s]),
            (field.at[:, :ROWS], heads.at[s]),
            (field.at[:, rows - ROWS :], tails.at[s]),
        ):
            copies.append(pltpu.make_async_copy(source, out, sems.at[len(copies)]))
    for copy in copies:
        copy.start()
    for at in (0, 1, 4, 5):
        copies[at].wait()
    for outer, inner, out in ((front, second, q_low), (back, penult, q_high)):

        def store(tile, sub, cat, out=out):
            out[0, span(tile), :] = sub
            out[1, span(tile), :] = cat

        plane_step(
            lambda s, tile, outer=outer: outer[s, span(tile), :],
            rows // ROWS,
            None,
            None,
            lambda s, tile, inner=inner: inner[s, span(tile), :],
            store,
        )
    for at in (2, 3, 6, 7):
        copies[at].wait()
    for s in range(2):
        for row in range(2):
            for plane in range(depth):
                low[s, row, plane : plane + 1] = heads[s, plane, row : row + 1]
                high[s, row, plane : plane + 1] = tails[s, plane, ROWS - 2 + row : ROWS - 1 + row]


def composite(sub, cat, scale_sub, scale_cat, clear):
    keep = jnp.exp(-(scale_sub * sub + scale_cat * cat))
    weight = clear * (1.0 - keep)
    return weight * sub, weight * cat, clear * keep


def first_kernel(emission, me, sub, cat, mid, old, sems):
    del emission, me
    depth, rows, _ = sub.shape
    fields = (sub, cat)

    def fetch(s, k):
        return pltpu.make_async_copy(fields[s].at[k], old.at[s, k], sems.at[s, k])

    for k in range(depth):
        for s in range(2):
            fetch(s, k).start()
    for k in range(2):
        for s in range(2):
            fetch(s, k).wait()

    @pl.loop(1, depth - 1)
    def _(k):
        for s in range(2):
            fetch(s, k + 1).wait()

        def store(tile, sub_new, cat_new):
            mid[0, k, span(tile), :] = sub_new
            mid[1, k, span(tile), :] = cat_new

        plane_step(
            lambda s, tile: old[s, k, span(tile), :],
            rows // ROWS,
            None,
            None,
            lambda s, tile: old[s, k - 1, span(tile), :] + old[s, k + 1, span(tile), :],
            store,
        )


def second_kernel(
    share, scale, mid, q_low, q_high, from_low, from_high, own_low, own_high,
    sub_out, cat_out, seen, near, far, rows_low, rows_high,
    heads, tails, new, sem_out,
):
    depth, rows, columns = sub_out.shape
    outputs = (sub_out, cat_out)
    tiles = rows // ROWS
    scale_sub, scale_cat = scale[0] * share, scale[1] * share

    def put(s, k):
        return pltpu.make_async_copy(new.at[s, k], outputs[s].at[k], sem_out.at[s, k])

    which = lax.broadcasted_iota(jnp.int32, (depth, columns), 0)
    for got, at, own, at_own, out in (
        (from_low, 1, own_low, 0, rows_low),
        (from_high, 0, own_high, 1, rows_high),
    ):
        sums, olds = [], []
        for s in range(2):
            here = got[s, at]
            ahead = jnp.where(which == 0, 0.0, pltpu.roll(here, 1, axis=0))
            behind = jnp.where(which == depth - 1, 0.0, pltpu.roll(here, depth - 1, axis=0))
            sums.append(lanes(here) + (got[s, 1 - at] + own[s, at_own]) + (ahead + behind))
            olds.append(here)
        sub, cat = react(olds[0], olds[1], sums[0], sums[1])
        out[0] = sub
        out[1] = cat

    index = lax.broadcasted_iota(jnp.int32, (ROWS, columns), 0)

    def with_low(s, k, tile):
        row = jnp.broadcast_to(from_low[s, 1, pl.ds(k, 1)], tile.shape)
        return tile + jnp.where(index == 0, RATES[s] * row, 0.0)

    def with_high(s, k, tile):
        row = jnp.broadcast_to(from_high[s, 0, pl.ds(k, 1)], tile.shape)
        return tile + jnp.where(index == ROWS - 1, RATES[s] * row, 0.0)

    @pl.loop(1, depth - 1)
    def _(k):
        for s in range(2):
            heads[s, k] = with_low(s, k, mid[s, k, span(0), :])
            tails[s, k] = with_high(s, k, mid[s, k, span(tiles - 1), :])

    def load(s, k, tile):
        if tile == 0:
            return heads[s, k]
        if tile == tiles - 1:
            return tails[s, k]
        return mid[s, k, span(tile), :]

    for s in range(2):
        for tile in range(tiles):
            first, last = q_low[s, span(tile), :], q_high[s, span(tile), :]
            if tile == 0:
                first, last = with_low(s, 0, first), with_low(s, depth - 1, last)
            if tile == tiles - 1:
                first, last = with_high(s, 0, first), with_high(s, depth - 1, last)
            near[s, 0, span(tile), :] = first
            far[s, 2, span(tile), :] = last
            for j in range(2):
                near[s, 1 + j, span(tile), :] = load(s, 1 + j, tile)
                far[s, j, span(tile), :] = load(s, depth - 3 + j, tile)

    seen[0] = jnp.zeros((rows, columns), jnp.float32)
    seen[1] = jnp.zeros((rows, columns), jnp.float32)
    seen[2] = jnp.ones((rows, columns), jnp.float32)

    @pl.loop(2, depth - 2)
    def _(k):
        def store(tile, sub, cat):
            at = span(tile)
            new[0, k, at, :] = sub
            new[1, k, at, :] = cat
            one, two, clear = composite(sub, cat, scale_sub, scale_cat, seen[2, at, :])
            seen[0, at, :] += one
            seen[1, at, :] += two
            seen[2, at, :] = clear

        plane_step(
            lambda s, tile: load(s, k, tile),
            tiles,
            [rows_low[s, pl.ds(k, 1)] for s in range(2)],
            [rows_high[s, pl.ds(k, 1)] for s in range(2)],
            lambda s, tile: load(s, k - 1, tile) + load(s, k + 1, tile),
            store,
        )
        for s in range(2):
            put(s, k).start()

    @pl.loop(2, depth - 2)
    def _(k):
        for s in range(2):
            put(s, k).wait()


def corner_kernel(p_low, p_high, first, last):
    rows = p_low.shape[1]
    for side, p in enumerate((p_low, p_high)):
        for s in range(2):
            first[side, s : s + 1] = p[s, :1]
            last[side, s : s + 1] = p[s, rows - 1 :]


def rim_kernel(
    share, scale, p_low, p_high, front, back, near, far, rows_low, rows_high, inner,
    ring, known, seen, mid,
):
    depth = rows_low.shape[1]
    rows = p_low.shape[1]
    tiles = rows // ROWS
    scale_sub, scale_cat = scale[0] * share, scale[1] * share
    for side, p, own, inside in ((0, p_low, front, near), (1, p_high, back, far)):
        zero, one, two = (0, 1, 2) if side == 0 else (2, 1, 0)
        outer, beside = (0, 1) if side == 0 else (depth - 1, depth - 2)
        for s in range(2):
            mid[side, s] = inside[s, zero] + RATES[s] * p[s]

        def store_known(tile, sub, cat, side=side, own=own):
            at = span(tile)
            known[side, 0, at, :] = sub + (RATES[0] * RATES[0]) * own[0, at, :]
            known[side, 1, at, :] = cat + (RATES[1] * RATES[1]) * own[1, at, :]

        plane_step(
            lambda s, tile, side=side: mid[side, s, span(tile), :],
            tiles,
            [rows_low[s, outer : outer + 1] for s in range(2)],
            [rows_high[s, outer : outer + 1] for s in range(2)],
            lambda s, tile, inside=inside, one=one: inside[s, one, span(tile), :],
            store_known,
        )

        def store_ring(tile, sub, cat, side=side):
            ring[0, side, span(tile), :] = sub
            ring[1, side, span(tile), :] = cat

        plane_step(
            lambda s, tile, inside=inside, one=one: inside[s, one, span(tile), :],
            tiles,
            [rows_low[s, beside : beside + 1] for s in range(2)],
            [rows_high[s, beside : beside + 1] for s in range(2)],
            lambda s, tile, inside=inside, two=two, side=side: inside[s, two, span(tile), :]
            + mid[side, s, span(tile), :],
            store_ring,
        )

    for tile in range(tiles):
        at = span(tile)
        one, two, clear = composite(ring[0, 0, at, :], ring[1, 0, at, :], scale_sub, scale_cat, 1.0)
        sub = one + clear * inner[0, at, :]
        cat = two + clear * inner[1, at, :]
        clear = clear * inner[2, at, :]
        one, two, clear = composite(ring[0, 1, at, :], ring[1, 1, at, :], scale_sub, scale_cat, clear)
        seen[0, at, :] = sub + one
        seen[1, at, :] = cat + two
        seen[2, at, :] = clear


def last_kernel(share, scale, me, known, q_low, q_high, seen, corner_low, corner_high, *outs_and_scratch):
    *pieces, outer, whole = outs_and_scratch
    rows, columns = seen.shape[1:]
    count = len(pieces)
    wide = columns // count
    tiles = rows // ROWS
    scale_sub, scale_cat = scale[0] * share, scale[1] * share
    index = lax.broadcasted_iota(jnp.int32, (ROWS, columns), 0)
    for tile in range(tiles):
        at = span(tile)
        planes = []
        for side, q in enumerate((q_low, q_high)):
            for s in range(2):
                value = known[side, s, at, :] + RATES[s] * q[s, at, :]
                twice = 2.0 * RATES[s] * RATES[s]
                if tile == 0:
                    row = jnp.broadcast_to(corner_low[side, s : s + 1], value.shape)
                    value = value + jnp.where(index == 0, twice * row, 0.0)
                if tile == tiles - 1:
                    row = jnp.broadcast_to(corner_high[side, s : s + 1], value.shape)
                    value = value + jnp.where(index == ROWS - 1, twice * row, 0.0)
                outer[s, side, at, :] = value
                planes.append(value)
        one, two, clear = composite(planes[0], planes[1], scale_sub, scale_cat, 1.0)
        sub = one + clear * seen[0, at, :]
        cat = two + clear * seen[1, at, :]
        clear = clear * seen[2, at, :]
        one, two, clear = composite(planes[2], planes[3], scale_sub, scale_cat, clear)
        whole[0, at, :] = sub + one
        whole[1, at, :] = cat + two
        whole[2, at, :] = clear
    for shift, piece in enumerate(pieces):
        target = lax.rem(me[0] + shift, count)
        if wide % 128 == 0:
            piece[...] = whole[:, :, pl.ds(pl.multiple_of(target * wide, 128), wide)]
        else:
            for other in range(count):

                @pl.when(target == other)
                def _(piece=piece, other=other):
                    piece[...] = whole[:, :, other * wide : (other + 1) * wide]


def shade_kernel(emission, me, *pieces_and_rest):
    *pieces, image, slabs = pieces_and_rest
    count = len(pieces)
    for shift, piece in enumerate(pieces):
        slabs[lax.rem(me[0] + count - shift, count)] = piece[...]
    sub, cat, clear = slabs[0, 0], slabs[0, 1], slabs[0, 2]
    for slab in range(1, count):
        sub = sub + clear * slabs[slab, 0]
        cat = cat + clear * slabs[slab, 1]
        clear = clear * slabs[slab, 2]
    for channel in range(3):
        image[channel] = emission[channel, 0] * sub + emission[channel, 1] * cat
    image[3] = 1.0 - clear


def place_kernel(ring, outer, sub_in, cat_in, sub_out, cat_out, sems):
    del sub_in, cat_in
    depth = sub_out.shape[0]
    outputs = (sub_out, cat_out)
    copies = []
    for s in range(2):
        for side in range(2):
            for at, source in ((side * (depth - 1), outer), (1 + side * (depth - 3), ring)):
                copies.append(pltpu.make_async_copy(source.at[s, side], outputs[s].at[at], sems.at[len(copies)]))
    for copy in copies:
        copy.start()
    for copy in copies:
        copy.wait()


def call(kernel, flops, room, **kwargs):
    return pl.pallas_call(
        kernel,
        cost_estimate=pl.CostEstimate(flops=flops, bytes_accessed=1 << 16, transcendentals=0),
        compiler_params=pltpu.CompilerParams(vmem_limit_bytes=room << 20),
        **kwargs,
    )


def body(substrate, catalyst, extinction, emission):
    depth, rows, columns = substrate.shape
    count = lax.axis_size("gz")
    wide = columns // count
    me = lax.axis_index("gz").astype(jnp.int32)[None]
    share = OPTICAL / (depth * count)

    def ring(size, shift):
        return [(i, (i + shift) % size) for i in range(size)]

    def up(x, axis):
        return lax.ppermute(x, axis, ring(lax.axis_size(axis), 1))

    def down(x, axis):
        return lax.ppermute(x, axis, ring(lax.axis_size(axis), -1))

    front, back = call(
        planes_kernel,
        1 << 20,
        2,
        name="planes",
        out_shape=(f32(2, rows, columns), f32(2, rows, columns)),
        in_specs=[HBM, HBM],
        out_specs=(VMEM, VMEM),
        scratch_shapes=[pltpu.SemaphoreType.DMA((4,))],
    )(hbm(substrate), hbm(catalyst))
    p_low = up(back, "gz")
    p_high = down(front, "gz")
    p_low = up(back, "gz")
    p_high = down(front, "gz")

    own_low, own_high, q_low, q_high = call(
        prepare_kernel,
        1 << 22,
        8,
        name="prepare",
        out_shape=(
            f32(2, 2, depth, columns),
            f32(2, 2, depth, columns),
            f32(2, rows, columns),
            f32(2, rows, columns),
        ),
        in_specs=[HBM, HBM, VMEM, VMEM],
        out_specs=(VMEM, VMEM, VMEM, VMEM),
        scratch_shapes=[
            pltpu.VMEM((2, depth, ROWS, columns), jnp.float32),
            pltpu.VMEM((2, depth, ROWS, columns), jnp.float32),
            pltpu.VMEM((2, rows, columns), jnp.float32),
            pltpu.VMEM((2, rows, columns), jnp.float32),
            pltpu.SemaphoreType.DMA((8,)),
        ],
    )(hbm(substrate), hbm(catalyst), front, back)
    from_low = up(own_high, "gx")
    from_high = down(own_low, "gx")
    q_from_low = up(q_high, "gz")
    q_from_high = down(q_low, "gz")

    mid = call(
        first_kernel,
        1 << 24,
        12,
        name="first",
        out_shape=f32(2, depth, rows, columns),
        in_specs=[SMEM, SMEM, HBM, HBM],
        out_specs=VMEM,
        scratch_shapes=[
            pltpu.VMEM((2, depth, rows, columns), jnp.float32),
            pltpu.SemaphoreType.DMA((2, depth)),
        ],
    )(emission, me, hbm(substrate), hbm(catalyst))

    sub_part, cat_part, inner, near, far, rows_low, rows_high = call(
        functools.partial(second_kernel, share),
        1 << 25,
        20,
        name="second",
        out_shape=(
            f32(depth, rows, columns),
            f32(depth, rows, columns),
            f32(3, rows, columns),
            f32(2, 3, rows, columns),
            f32(2, 3, rows, columns),
            f32(2, depth, columns),
            f32(2, depth, columns),
        ),
        in_specs=[SMEM] + [VMEM] * 7,
        out_specs=(HBM, HBM, VMEM, VMEM, VMEM, VMEM, VMEM),
        scratch_shapes=[
            pltpu.VMEM((2, depth, ROWS, columns), jnp.float32),
            pltpu.VMEM((2, depth, ROWS, columns), jnp.float32),
            pltpu.VMEM((2, depth, rows, columns), jnp.float32),
            pltpu.SemaphoreType.DMA((2, depth)),
        ],
    )(extinction, mid, q_low, q_high, from_low, from_high, own_low, own_high)

    p_low, p_high, inner = lax.optimization_barrier((p_low, p_high, inner))
    first_rows, last_rows = call(
        corner_kernel,
        1 << 18,
        2,
        name="corner",
        out_shape=(f32(2, 2, columns), f32(2, 2, columns)),
        in_specs=[VMEM, VMEM],
        out_specs=(VMEM, VMEM),
    )(p_low, p_high)
    corner_low = up(last_rows, "gx")
    corner_high = down(first_rows, "gx")

    ring_planes, known, seen = call(
        functools.partial(rim_kernel, share),
        1 << 23,
        12,
        name="rim",
        out_shape=(f32(2, 2, rows, columns), f32(2, 2, rows, columns), f32(3, rows, columns)),
        in_specs=[SMEM] + [VMEM] * 9,
        out_specs=(VMEM, VMEM, VMEM),
        scratch_shapes=[pltpu.VMEM((2, 2, rows, columns), jnp.float32)],
    )(extinction, p_low, p_high, front, back, near, far, rows_low, rows_high, inner)

    *pieces, outer = call(
        functools.partial(last_kernel, share),
        1 << 22,
        8,
        name="last",
        out_shape=(*[f32(3, rows, wide)] * count, f32(2, 2, rows, columns)),
        in_specs=[SMEM, SMEM] + [VMEM] * 6,
        out_specs=tuple([VMEM] * (count + 1)),
        scratch_shapes=[pltpu.VMEM((3, rows, columns), jnp.float32)],
    )(extinction, me, known, q_from_low, q_from_high, seen, corner_low, corner_high)

    received = [pieces[0]]
    for shift in range(1, count):
        received.append(lax.ppermute(pieces[shift], "gz", ring(count, shift)))

    sub_final, cat_final = call(
        place_kernel,
        1 << 22,
        4,
        name="place",
        out_shape=(f32(depth, rows, columns), f32(depth, rows, columns)),
        in_specs=[VMEM, VMEM, HBM, HBM],
        out_specs=(HBM, HBM),
        input_output_aliases={2: 0, 3: 1},
        scratch_shapes=[pltpu.SemaphoreType.DMA((8,))],
    )(ring_planes, outer, sub_part, cat_part)

    image = call(
        shade_kernel,
        1 << 20,
        8,
        name="shade",
        out_shape=f32(4, rows, wide),
        in_specs=[SMEM, SMEM] + [VMEM] * count,
        out_specs=VMEM,
        scratch_shapes=[pltpu.VMEM((count, 3, rows, wide), jnp.float32)],
    )(emission, me, *received)
    return sub_final, cat_final, image


def solution(mesh):
    placed = (P("gz", "gx", None), P("gz", "gx", None), P(), P())

    return jax.shard_map(
        body,
        mesh=mesh,
        in_specs=placed,
        out_specs=(P("gz", "gx", None), P("gz", "gx", None), P(None, "gx", "gz")),
        check_vma=False,
    )
```

time: 42.9 us -> 43 us (level)
  waiting for transfers between devices: 8.49 us -> 5.26 us
  Pallas kernels: 16.1 us -> 18.1 us
  starting transfers between devices: 17.4 us -> 18.6 us
    ppermute x4, starting transfers between devices: 8.59 us -> 12.1 us  [down(): return lax.ppermute(x, axis, ring(lax.axis_size(axis), -1))]
    ppermute x4, starting transfers between devices: 5.76 us -> 3.56 us  [up(): return lax.ppermute(x, axis, ring(lax.axis_size(axis), 1))]
    ppermute x4, waiting for transfers between devices: 3.3 us -> 1.3 us  [down(): return lax.ppermute(x, axis, ring(lax.axis_size(axis), -1))]
    pallas_call x3, Pallas kernels: 10.5 us -> 12.4 us  [the longest x1 5.44 us: body(): call(functools.partial(second_kernel, share), 1 << 25, 20, name='second',...]
    ppermute x4, waiting for transfers between devices: 1.48 us -> 0.25 us  [up(): return lax.ppermute(x, axis, ring(lax.axis_size(axis), 1))]
  transfers between devices with their start and end apart: 11 -> 11, of which waited for: 8 -> 5; matrix products, arithmetic and copies ran while one was open for 0% -> 0% of each run, Pallas kernels for 29% -> 30%
where the time goes in v1:
time: 43 us; the launch traced here: 42.8 us
  starting transfers between devices  18.6 us (43%)
  Pallas kernels  18.1 us (42%)
  waiting for transfers between devices  5.26 us (12%)
  between operations  0.75 us (2%)
    ppermute x4, starting transfers between devices, down(): return lax.ppermute(x, axis, ring(lax.axis_size(axis), -1))  12.1 us
    pallas_call x1, Pallas kernels, body(): call(functools.partial(second_kernel, share), 1 << 25, 20, name='second',...  5.44 us
    pallas_call x1, Pallas kernels, body(): call(first_kernel, 1 << 24, 12, name='first', out_shape=f32(2, depth, row...  5.03 us
    ppermute x3, waiting for transfers between devices, body(): received.append(lax.ppermute(pieces[shift], 'gz', ring(count, shift)))  3.71 us
    ppermute x4, starting transfers between devices, up(): return lax.ppermute(x, axis, ring(lax.axis_size(axis), 1))  3.56 us
    ppermute x3, starting transfers between devices, body(): received.append(lax.ppermute(pieces[shift], 'gz', ring(count, shift)))  3.01 us
    pallas_call x1, Pallas kernels, body(): call(prepare_kernel, 1 << 22, 8, name='prepare', out_shape=(f32(2, 2, dep...  1.95 us
    pallas_call x1, Pallas kernels, body(): call(functools.partial(rim_kernel, share), 1 << 23, 12, name='rim', out_s...  1.42 us
  transfers between devices with their start and end apart: 11, of which 5 were waited for; matrix products, arithmetic and copies ran while one was open for 0% of the time, Pallas kernels for 30%

profile of v1, /device:TPU:0, one launch (start us, length us, event | category | flops | bytes accessed | tf_op | source)
XLA Modules:
  0.0 42.8 jit_solution(2202506995454948206)
XLA Ops:
  0.6 1.1 %planes.1 = (f32[2,32,1024]{2,1,0:T(8,128)S(1)}, f32[2,32,1024]{2,1,0:T(8,128)S(1)}) custom-call(f32[16,32,1024]{2,1,0:T(8,128)} %sub.5, f32[16,32,1024]{2,1,0:T(8,128)} %cat.5), custom_call_target="tpu_custom_call" | custom-call | flops 1048576 | bytes 65536 | tf_op jit(solution)/shard_map/planes/pallas_call | solution.py:409
  1.8 0.0 copy-start.1
  1.8 2.0 %prepare.1 = (f32[2,2,16,1024]{3,2,1,0:T(8,128)S(1)}, f32[2,2,16,1024]{3,2,1,0:T(8,128)S(1)}, f32[2,32,1024]{2,1,0:T(8,128)S(1)}, f32[2,32,1024]{2,1,0:T(8,128)S(1)}) custom-call(f32[16,32,1024]{2,1,0:T(8,128)} %sub.5, f32[16,32,1024]{2,1,0:T(8,128)} %cat.5, f32[2,32,1024]{2,1,0:T(8,128)S(1)} %get-tuple-element.32.front, ...), custom_call_target="tpu_custom_call" | custom-call | flops 4194304 | bytes 65536 | tf_op jit(solution)/shard_map/prepare/pallas_call | solution.py:424
  3.7 0.5 %collective-permute-start.2 = (f32[2,2,16,1024]{3,2,1,0:T(8,128)S(1)}, f32[2,2,16,1024]{3,2,1,0:T(8,128)S(1)}, u32[]{:S(2)}, u32[]{:S(2)}) collective-permute-start(f32[2,2,16,1024]{3,2,1,0:T(8,128)S(1)} %get-tuple-element.35.own_high), channel_id=1, source_target_pairs={{0,1},{1,2},{2,3},{3,4},{4,5},{5,6},{6,7},{7,0},{8,9},{9,10},{10,1... | collective-permute-start | bytes 786440 | tf_op jit(solution)/shard_map/ppermute | solution.py:404
  4.3 4.1 %collective-permute-start.3 = (f32[2,2,16,1024]{3,2,1,0:T(8,128)S(1)}, f32[2,2,16,1024]{3,2,1,0:T(8,128)S(1)}, u32[]{:S(2)}, u32[]{:S(2)}) collective-permute-start(f32[2,2,16,1024]{3,2,1,0:T(8,128)S(1)} %get-tuple-element.36.own_low), channel_id=1, source_target_pairs={{0,7},{1,0},{2,1},{3,2},{4,3},{5,4},{6,5},{7,6},{8,15},{9,8},{10,9... | collective-permute-start | bytes 786440 | tf_op jit(solution)/shard_map/ppermute | solution.py:407
  8.4 1.9 %collective-permute-start = (f32[2,32,1024]{2,1,0:T(8,128)S(1)}, f32[2,32,1024]{2,1,0:T(8,128)S(1)}, u32[]{:S(2)}, u32[]{:S(2)}) collective-permute-start(f32[2,32,1024]{2,1,0:T(8,128)S(1)} %get-tuple-element.31.back), channel_id=1, source_target_pairs={{0,8},{8,16},{16,24},{24,0},{1,9},{9,17},{17,25},{25,1},{2,10},{10... | collective-permute-start | bytes 786440 | tf_op jit(solution)/shard_map/ppermute | solution.py:404
  10.3 1.0 %collective-permute-start.1 = (f32[2,32,1024]{2,1,0:T(8,128)S(1)}, f32[2,32,1024]{2,1,0:T(8,128)S(1)}, u32[]{:S(2)}, u32[]{:S(2)}) collective-permute-start(f32[2,32,1024]{2,1,0:T(8,128)S(1)} %get-tuple-element.32.front), channel_id=1, source_target_pairs={{0,24},{8,0},{16,8},{24,16},{1,25},{9,1},{17,9},{25,17},{2,26},{10... | collective-permute-start | bytes 786440 | tf_op jit(solution)/shard_map/ppermute | solution.py:407
  11.3 1.0 %collective-permute-start.4 = (f32[2,32,1024]{2,1,0:T(8,128)S(1)}, f32[2,32,1024]{2,1,0:T(8,128)S(1)}, u32[]{:S(2)}, u32[]{:S(2)}) collective-permute-start(f32[2,32,1024]{2,1,0:T(8,128)S(1)} %get-tuple-element.34.q_high), channel_id=1, source_target_pairs={{0,8},{8,16},{16,24},{24,0},{1,9},{9,17},{17,25},{25,1},{2,10},{10... | collective-permute-start | bytes 786440 | tf_op jit(solution)/shard_map/ppermute | solution.py:404
  12.3 0.2 collective-permute-done.2.from_low
  12.6 3.4 %collective-permute-start.5 = (f32[2,32,1024]{2,1,0:T(8,128)S(1)}, f32[2,32,1024]{2,1,0:T(8,128)S(1)}, u32[]{:S(2)}, u32[]{:S(2)}) collective-permute-start(f32[2,32,1024]{2,1,0:T(8,128)S(1)} %get-tuple-element.33.q_low), channel_id=1, source_target_pairs={{0,24},{8,0},{16,8},{24,16},{1,25},{9,1},{17,9},{25,17},{2,26},{10... | collective-permute-start | bytes 786440 | tf_op jit(solution)/shard_map/ppermute | solution.py:407
  16.0 0.0 copy-done.1
  16.0 0.1 copy.9.emission
  16.1 0.0 copy-start
  16.1 5.0 %first.1.mid = f32[2,16,32,1024]{3,2,1,0:T(8,128)S(1)} custom-call(f32[3,2]{1,0:T(4,128)S(1)} %copy.9.emission, s32[1]{0:T(128)} %bitcast.me, f32[16,32,1024]{2,1,0:T(8,128)} %sub.5, f32[16,32,1024]{2,1,0:T(8,128)} %cat.5), custom_call_target="tpu_custom_call" | custom-call | flops 16777216 | bytes 65536 | tf_op jit(solution)/shard_map/first/pallas_call | solution.py:450
  21.2 0.0 collective-permute-done.3.from_high
  21.2 0.0 copy-done
  21.2 5.4 %second.1 = (f32[16,32,1024]{2,1,0:T(8,128)}, f32[16,32,1024]{2,1,0:T(8,128)}, f32[3,32,1024]{2,1,0:T(8,128)S(1)}, f32[2,3,32,1024]{3,2,1,0:T(8,128)S(1)}, f32[2...) custom-call(f32[2]{0:T(128)S(1)} %copy-done, f32[2,16,32,1024]{3,2,1,0:T(8,128)S(1)} %first.1.mid, ...), custom_call_target="tpu_custom_call" | custom-call | flops 33554432 | bytes 65536 | tf_op jit(solution)/shard_map/second/pallas_call | solution.py:464
  26.6 0.0 collective-permute-done.p_low
  26.6 0.0 collective-permute-done.1.p_high
  26.7 0.1 collective-permute-start.6
  26.7 3.5 %collective-permute-start.7 = (f32[2,2,1024]{2,1,0:T(2,128)S(1)}, f32[2,2,1024]{2,1,0:T(2,128)S(1)}, u32[]{:S(2)}, u32[]{:S(2)}) collective-permute-start(f32[2,2,1024]{2,1,0:T(2,128)S(1)} %get-tuple-element.49), channel_id=1, source_target_pairs={{0,7},{1,0},{2,1},{3,2},{4,3},{5,4},{6,5},{7,6},{8,15},{9,8},{10,9... | collective-permute-start | bytes 49160 | tf_op jit(solution)/shard_map/ppermute | solution.py:407
  30.3 1.4 %rim.1 = (f32[2,2,32,1024]{3,2,1,0:T(8,128)S(1)}, f32[2,2,32,1024]{3,2,1,0:T(8,128)S(1)}, f32[3,32,1024]{2,1,0:T(8,128)S(1)}) custom-call(f32[2]{0:T(128)S(1)} %copy-done, f32[2,32,1024]{2,1,0:T(8,128)S(1)} %collective-permute-done.p_low, f32[2,32,1024]{2,1,0:T(8,128)S(1)} %collective-permute-done.1.p_high, f32[2,32,1024]{2,1,0:T(8,128)S(1)} %get-tuple-element.32.front, ...), custom_call_target="tpu_custom_call" | custom-call | flops 8388608 | bytes 65536 | tf_op jit(solution)/shard_map/rim/pallas_call | solution.py:501
  31.7 0.0 collective-permute-done.4.q_low
  31.7 1.3 %collective-permute-done.5.q_high = f32[2,32,1024]{2,1,0:T(8,128)S(1)} collective-permute-done((f32[2,32,1024]{2,1,0:T(8,128)S(1)}, f32[2,32,1024]{2,1,0:T(8,128)S(1)}, u32[]{:S(2)}, u32[]{:S(2)}) %collective-permute-start.5) | collective-permute-done | bytes 262176 | tf_op jit(solution)/shard_map/ppermute | solution.py:407
  33.0 0.0 collective-permute-done.6.corner_low
  33.0 0.0 collective-permute-done.7.corner_high
  33.0 0.8 %last.1 = (f32[3,32,256]{2,1,0:T(8,128)S(1)}, f32[3,32,256]{2,1,0:T(8,128)S(1)}, f32[3,32,256]{2,1,0:T(8,128)S(1)}, f32[3,32,256]{2,1,0:T(8,128)S(1)}, f32[2,2,32,1024]{3,2,1,0:T(8,128)S(1)}) custom-call(f32[2]{0:T(128)S(1)} %copy-done, s32[1]{0:T(128)} %bitcast.me, f32[2,2,32,1024]{3,2,1,0:T(8,128)S(1)} %get-tuple-element.46.known, ...), custom_call_target="tpu_custom_call" | custom-call | flops 4194304 | bytes 65536 | tf_op jit(solution)/shard_map/last/pallas_call | solution.py:512
  33.8 1.5 %collective-permute-start.10 = (f32[3,32,256]{2,1,0:T(8,128)S(1)}, f32[3,32,256]{2,1,0:T(8,128)S(1)}, u32[]{:S(2)}, u32[]{:S(2)}) collective-permute-start(f32[3,32,256]{2,1,0:T(8,128)S(1)} %get-tuple-element.58), channel_id=1, source_target_pairs={{0,24},{8,0},{16,8},{24,16},{1,25},{9,1},{17,9},{25,17},{2,26},{10... | collective-permute-start | bytes 294920 | tf_op jit(solution)/shard_map/ppermute | solution.py:525
  35.3 0.6 %collective-permute-start.8 = (f32[3,32,256]{2,1,0:T(8,128)S(1)}, f32[3,32,256]{2,1,0:T(8,128)S(1)}, u32[]{:S(2)}, u32[]{:S(2)}) collective-permute-start(f32[3,32,256]{2,1,0:T(8,128)S(1)} %get-tuple-element.56), channel_id=1, source_target_pairs={{0,8},{8,16},{16,24},{24,0},{1,9},{9,17},{17,25},{25,1},{2,10},{10... | collective-permute-start | bytes 294920 | tf_op jit(solution)/shard_map/ppermute | solution.py:525
  35.9 0.9 %collective-permute-start.9 = (f32[3,32,256]{2,1,0:T(8,128)S(1)}, f32[3,32,256]{2,1,0:T(8,128)S(1)}, u32[]{:S(2)}, u32[]{:S(2)}) collective-permute-start(f32[3,32,256]{2,1,0:T(8,128)S(1)} %get-tuple-element.57), channel_id=1, source_target_pairs={{0,16},{8,24},{16,0},{24,8},{1,17},{9,25},{17,1},{25,9},{2,18},{10... | collective-permute-start | bytes 294920 | tf_op jit(solution)/shard_map/ppermute | solution.py:525
  36.8 1.0 %place.1 = (f32[16,32,1024]{2,1,0:T(8,128)}, f32[16,32,1024]{2,1,0:T(8,128)}) custom-call(f32[2,2,32,1024]{3,2,1,0:T(8,128)S(1)} %get-tuple-element.45.ring, f32[2,2,32,1024]{3,2,1,0:T(8,128)S(1)} %get-tuple-element.50.outer, f32[16,32,1024]{2,1,0:T(8,128)} %get-tuple-element.51.sub_in, ...), custom_call_target="tpu_custom_call", output_to_operand_aliasing={{0}: (2, {}), {1}: (3, {})} | custom-call | flops 4194304 | bytes 65536 | tf_op jit(solution)/shard_map/place/pallas_call | solution.py:527
  37.8 0.6 %collective-permute-done.10.pieces_and_rest_3_ = f32[3,32,256]{2,1,0:T(8,128)S(1)} collective-permute-done((f32[3,32,256]{2,1,0:T(8,128)S(1)}, f32[3,32,256]{2,1,0:T(8,128)S(1)}, u32[]{:S(2)}, u32[]{:S(2)}) %collective-permute-start.10) | collective-permute-done | bytes 98336 | tf_op jit(solution)/shard_map/ppermute | solution.py:525
  38.5 2.4 %collective-permute-done.8.pieces_and_rest_1_ = f32[3,32,256]{2,1,0:T(8,128)S(1)} collective-permute-done((f32[3,32,256]{2,1,0:T(8,128)S(1)}, f32[3,32,256]{2,1,0:T(8,128)S(1)}, u32[]{:S(2)}, u32[]{:S(2)}) %collective-permute-start.8) | collective-permute-done | bytes 98336 | tf_op jit(solution)/shard_map/ppermute | solution.py:525
  40.9 0.6 %collective-permute-done.9.pieces_and_rest_2_ = f32[3,32,256]{2,1,0:T(8,128)S(1)} collective-permute-done((f32[3,32,256]{2,1,0:T(8,128)S(1)}, f32[3,32,256]{2,1,0:T(8,128)S(1)}, u32[]{:S(2)}, u32[]{:S(2)}) %collective-permute-start.9) | collective-permute-done | bytes 98336 | tf_op jit(solution)/shard_map/ppermute | solution.py:525
  41.5 1.3 %shade.1 = f32[4,32,256]{2,1,0:T(8,128)} custom-call(f32[3,2]{1,0:T(4,128)S(1)} %copy.9.emission, s32[1]{0:T(128)} %bitcast.me, f32[3,32,256]{2,1,0:T(8,128)S(1)} %get-tuple-element.55.pieces_and_rest_0_, f32[3,32,256]{2,1,0:T(8,128)S(1)} %collective-permute-done.8.pieces_and_rest_1_, f32[3,32,256]{2,1,0:T(8,128)S(1)} %collective-permute-done.9.pieces_and_rest_2_, ...), custom_call_target="tpu_custom_call" | custom-call | flops 1048576 | bytes 65536 | tf_op jit(solution)/shard_map/shade/pallas_call | solution.py:539
  (1 shorter events, 0.0 us)
Async XLA Ops:
  1.8 14.3 %copy-start.1 = (f32[3,2]{0,1:T(2,128)S(1)}, f32[3,2]{0,1:T(2,128)}, u32[]{:S(2)}) copy-start(f32[3,2]{0,1:T(2,128)} %param.7) | copy-start | bytes 76
  3.7 8.8 %collective-permute-start.2 = (f32[2,2,16,1024]{3,2,1,0:T(8,128)S(1)}, f32[2,2,16,1024]{3,2,1,0:T(8,128)S(1)}, u32[]{:S(2)}, u32[]{:S(2)}) collective-permute-start(f32[2,2,16,1024]{3,2,1,0:T(8,128)S(1)} %get-tuple-element.35.own_high), channel_id=1, source_target_pairs={{0,1},{1,2},{2,3},{3,4},{4,5},{5,6},{6,7},{7,0},{8,9},{9,10},{10,1... | collective-permute-start | bytes 786440 | tf_op jit(solution)/shard_map/ppermute | solution.py:404
  4.3 16.9 %collective-permute-start.3 = (f32[2,2,16,1024]{3,2,1,0:T(8,128)S(1)}, f32[2,2,16,1024]{3,2,1,0:T(8,128)S(1)}, u32[]{:S(2)}, u32[]{:S(2)}) collective-permute-start(f32[2,2,16,1024]{3,2,1,0:T(8,128)S(1)} %get-tuple-element.36.own_low), channel_id=1, source_target_pairs={{0,7},{1,0},{2,1},{3,2},{4,3},{5,4},{6,5},{7,6},{8,15},{9,8},{10,9... | collective-permute-start | bytes 786440 | tf_op jit(solution)/shard_map/ppermute | solution.py:407
  8.4 18.2 %collective-permute-start = (f32[2,32,1024]{2,1,0:T(8,128)S(1)}, f32[2,32,1024]{2,1,0:T(8,128)S(1)}, u32[]{:S(2)}, u32[]{:S(2)}) collective-permute-start(f32[2,32,1024]{2,1,0:T(8,128)S(1)} %get-tuple-element.31.back), channel_id=1, source_target_pairs={{0,8},{8,16},{16,24},{24,0},{1,9},{9,17},{17,25},{25,1},{2,10},{10... | collective-permute-start | bytes 786440 | tf_op jit(solution)/shard_map/ppermute | solution.py:404
  10.3 16.3 %collective-permute-start.1 = (f32[2,32,1024]{2,1,0:T(8,128)S(1)}, f32[2,32,1024]{2,1,0:T(8,128)S(1)}, u32[]{:S(2)}, u32[]{:S(2)}) collective-permute-start(f32[2,32,1024]{2,1,0:T(8,128)S(1)} %get-tuple-element.32.front), channel_id=1, source_target_pairs={{0,24},{8,0},{16,8},{24,16},{1,25},{9,1},{17,9},{25,17},{2,26},{10... | collective-permute-start | bytes 786440 | tf_op jit(solution)/shard_map/ppermute | solution.py:407
  11.3 20.4 %collective-permute-start.4 = (f32[2,32,1024]{2,1,0:T(8,128)S(1)}, f32[2,32,1024]{2,1,0:T(8,128)S(1)}, u32[]{:S(2)}, u32[]{:S(2)}) collective-permute-start(f32[2,32,1024]{2,1,0:T(8,128)S(1)} %get-tuple-element.34.q_high), channel_id=1, source_target_pairs={{0,8},{8,16},{16,24},{24,0},{1,9},{9,17},{17,25},{25,1},{2,10},{10... | collective-permute-start | bytes 786440 | tf_op jit(solution)/shard_map/ppermute | solution.py:404
  12.6 20.4 %collective-permute-start.5 = (f32[2,32,1024]{2,1,0:T(8,128)S(1)}, f32[2,32,1024]{2,1,0:T(8,128)S(1)}, u32[]{:S(2)}, u32[]{:S(2)}) collective-permute-start(f32[2,32,1024]{2,1,0:T(8,128)S(1)} %get-tuple-element.33.q_low), channel_id=1, source_target_pairs={{0,24},{8,0},{16,8},{24,16},{1,25},{9,1},{17,9},{25,17},{2,26},{10... | collective-permute-start | bytes 786440 | tf_op jit(solution)/shard_map/ppermute | solution.py:407
  16.1 5.0 %copy-start = (f32[2]{0:T(128)S(1)}, f32[2]{0:T(128)}, u32[]{:S(2)}) copy-start(f32[2]{0:T(128)} %scale.5) | copy-start | bytes 28
  26.7 6.3 %collective-permute-start.6 = (f32[2,2,1024]{2,1,0:T(2,128)S(1)}, f32[2,2,1024]{2,1,0:T(2,128)S(1)}, u32[]{:S(2)}, u32[]{:S(2)}) collective-permute-start(f32[2,2,1024]{2,1,0:T(2,128)S(1)} %get-tuple-element.48), channel_id=1, source_target_pairs={{0,1},{1,2},{2,3},{3,4},{4,5},{5,6},{6,7},{7,0},{8,9},{9,10},{10,1... | collective-permute-start | bytes 49160 | tf_op jit(solution)/shard_map/ppermute | solution.py:404
  26.7 6.3 %collective-permute-start.7 = (f32[2,2,1024]{2,1,0:T(2,128)S(1)}, f32[2,2,1024]{2,1,0:T(2,128)S(1)}, u32[]{:S(2)}, u32[]{:S(2)}) collective-permute-start(f32[2,2,1024]{2,1,0:T(2,128)S(1)} %get-tuple-element.49), channel_id=1, source_target_pairs={{0,7},{1,0},{2,1},{3,2},{4,3},{5,4},{6,5},{7,6},{8,15},{9,8},{10,9... | collective-permute-start | bytes 49160 | tf_op jit(solution)/shard_map/ppermute | solution.py:407
  33.8 4.7 %collective-permute-start.10 = (f32[3,32,256]{2,1,0:T(8,128)S(1)}, f32[3,32,256]{2,1,0:T(8,128)S(1)}, u32[]{:S(2)}, u32[]{:S(2)}) collective-permute-start(f32[3,32,256]{2,1,0:T(8,128)S(1)} %get-tuple-element.58), channel_id=1, source_target_pairs={{0,24},{8,0},{16,8},{24,16},{1,25},{9,1},{17,9},{25,17},{2,26},{10... | collective-permute-start | bytes 294920 | tf_op jit(solution)/shard_map/ppermute | solution.py:525
  35.3 5.6 %collective-permute-start.8 = (f32[3,32,256]{2,1,0:T(8,128)S(1)}, f32[3,32,256]{2,1,0:T(8,128)S(1)}, u32[]{:S(2)}, u32[]{:S(2)}) collective-permute-start(f32[3,32,256]{2,1,0:T(8,128)S(1)} %get-tuple-element.56), channel_id=1, source_target_pairs={{0,8},{8,16},{16,24},{24,0},{1,9},{9,17},{17,25},{25,1},{2,10},{10... | collective-permute-start | bytes 294920 | tf_op jit(solution)/shard_map/ppermute | solution.py:525
  35.9 5.7 %collective-permute-start.9 = (f32[3,32,256]{2,1,0:T(8,128)S(1)}, f32[3,32,256]{2,1,0:T(8,128)S(1)}, u32[]{:S(2)}, u32[]{:S(2)}) collective-permute-start(f32[3,32,256]{2,1,0:T(8,128)S(1)} %get-tuple-element.57), channel_id=1, source_target_pairs={{0,16},{8,24},{16,0},{24,8},{1,17},{9,25},{17,1},{25,9},{2,18},{10... | collective-permute-start | bytes 294920 | tf_op jit(solution)/shard_map/ppermute | solution.py:525

commit v2 on v1

v2 whole, which is shorter than its diff:
```python
import functools

import jax
import jax.numpy as jnp
from jax import lax
from jax.experimental import pallas as pl
from jax.experimental.pallas import tpu as pltpu
from jax.sharding import PartitionSpec as P


RATES = (0.16, 0.08)
FEED = 0.037
KILL = 0.06
OPTICAL = 4.0
ROWS, LANES = 8, 128

HBM = pl.BlockSpec(memory_space=pltpu.HBM)
VMEM = pl.BlockSpec(memory_space=pltpu.VMEM)
SMEM = pl.BlockSpec(memory_space=pltpu.SMEM)


def f32(*shape):
    return jax.ShapeDtypeStruct(shape, jnp.float32)


def hbm(x):
    return pltpu.with_memory_space_constraint(x, pltpu.HBM)


def lanes(x):
    return pltpu.roll(x, 1, axis=x.ndim - 1) + pltpu.roll(x, x.shape[-1] - 1, axis=x.ndim - 1)


def react(sub, cat, around_sub, around_cat):
    growth = sub * cat * cat
    sub_new = (1.0 - 6.0 * RATES[0] - FEED) * sub + RATES[0] * around_sub - growth + FEED
    cat_new = (1.0 - 6.0 * RATES[1] - FEED - KILL) * cat + RATES[1] * around_cat + growth
    return sub_new, cat_new


def plane_step(load, tiles, low_rows, high_rows, across, store, only=None):
    for tile in range(tiles) if only is None else only:
        sums, olds = [], []
        for s in range(2):
            old = load(s, tile)
            index = lax.broadcasted_iota(jnp.int32, old.shape, 0)
            above = load(s, tile - 1)[ROWS - 1 :] if tile else low_rows and low_rows[s]
            below = load(s, tile + 1)[:1] if tile < tiles - 1 else high_rows and high_rows[s]
            above = 0.0 if above is None else jnp.broadcast_to(above, old.shape)
            below = 0.0 if below is None else jnp.broadcast_to(below, old.shape)
            up = jnp.where(index == 0, above, pltpu.roll(old, 1, axis=0))
            down = jnp.where(index == ROWS - 1, below, pltpu.roll(old, ROWS - 1, axis=0))
            sums.append(lanes(old) + (up + down) + across(s, tile))
            olds.append(old)
        store(tile, *react(olds[0], olds[1], sums[0], sums[1]))


def span(tile):
    return pl.ds(tile * ROWS, ROWS)


def across_columns(tile, columns):
    return tile[:, :columns] if columns <= LANES else jnp.concatenate([tile] * (columns // LANES), axis=1)


def outer_step(outer, inner, rows, only, store):
    plane_step(
        lambda s, tile: outer[s, span(tile), :],
        rows // ROWS,
        None,
        None,
        lambda s, tile: inner[s, span(tile), :],
        store,
        only,
    )


def planes_kernel(sub, cat, up, down, second, penult, sems):
    depth, rows, _ = sub.shape
    copies = []
    for s, field in enumerate((sub, cat)):
        for plane, out in (
            (depth - 1, up.at[s, pl.ds(0, rows)]),
            (depth - 2, penult.at[s]),
            (0, down.at[s, pl.ds(0, rows)]),
            (1, second.at[s]),
        ):
            copies.append(pltpu.make_async_copy(field.at[plane], out, sems.at[len(copies)]))
    for copy in copies:
        copy.start()
    for copy in copies:
        copy.wait()
    for outer, inner in ((up, penult), (down, second)):

        def store(tile, sub_new, cat_new, outer=outer):
            at = pl.ds(rows + (tile - 1) * ROWS, ROWS)
            outer[0, at, :] = sub_new
            outer[1, at, :] = cat_new

        outer_step(outer, inner, rows, range(1, rows // ROWS - 1), store)


def prepare_kernel(
    share, scale, emission, sub, cat, up, down, second, penult,
    old, low, high, q_up, q_down, values, sems,
):
    depth, rows, _ = sub.shape
    copies = []
    for plane in range(depth):
        for s, field in enumerate((sub, cat)):
            copies.append(pltpu.make_async_copy(field.at[plane], old.at[s, plane], sems.at[s, plane]))
    for copy in copies:
        copy.start()
    shape = values.shape[1:]
    for s in range(2):
        values[s] = jnp.full(shape, scale[s] * share, jnp.float32)
        for channel in range(3):
            values[2 + channel * 2 + s] = jnp.full(shape, emission[channel, s], jnp.float32)
    for outer, inner, out in ((up, penult, q_up), (down, second, q_down)):

        def store(tile, sub_new, cat_new, out=out):
            at = span(0 if tile == 0 else 1)
            out[0, at, :] = sub_new
            out[1, at, :] = cat_new

        outer_step(outer, inner, rows, (0, rows // ROWS - 1), store)
    for copy in copies:
        copy.wait()
    for s in range(2):
        for row in range(2):
            for plane in range(depth):
                low[s, row, plane : plane + 1] = old[s, plane, row : row + 1]
                high[s, row, plane : plane + 1] = old[s, plane, rows - 2 + row : rows - 1 + row]


def composite(sub, cat, scale_sub, scale_cat, clear):
    keep = jnp.exp(-(scale_sub * sub + scale_cat * cat))
    weight = clear * (1.0 - keep)
    return weight * sub, weight * cat, clear * keep


def first_kernel(old, mid):
    depth, rows, _ = old.shape[1:]

    @pl.loop(1, depth - 1)
    def _(k):
        def store(tile, sub, cat):
            mid[0, k, span(tile), :] = sub
            mid[1, k, span(tile), :] = cat

        plane_step(
            lambda s, tile: old[s, k, span(tile), :],
            rows // ROWS,
            None,
            None,
            lambda s, tile: old[s, k - 1, span(tile), :] + old[s, k + 1, span(tile), :],
            store,
        )


def second_kernel(
    values, mid, up, down, q_up, q_down, from_low, from_high, own_low, own_high,
    sub_out, cat_out, seen, near, far, rows_low, rows_high,
    heads, tails, new, sem_out,
):
    depth, rows, columns = sub_out.shape
    outputs = (sub_out, cat_out)
    tiles = rows // ROWS
    scale_sub, scale_cat = across_columns(values[0], columns), across_columns(values[1], columns)

    def put(s, k):
        return pltpu.make_async_copy(new.at[s, k], outputs[s].at[k], sem_out.at[s, k])

    which = lax.broadcasted_iota(jnp.int32, (depth, columns), 0)
    for got, at, own, at_own, out in (
        (from_low, 1, own_low, 0, rows_low),
        (from_high, 0, own_high, 1, rows_high),
    ):
        sums, olds = [], []
        for s in range(2):
            here = got[s, at]
            ahead = jnp.where(which == 0, 0.0, pltpu.roll(here, 1, axis=0))
            behind = jnp.where(which == depth - 1, 0.0, pltpu.roll(here, depth - 1, axis=0))
            sums.append(lanes(here) + (got[s, 1 - at] + own[s, at_own]) + (ahead + behind))
            olds.append(here)
        sub, cat = react(olds[0], olds[1], sums[0], sums[1])
        out[0] = sub
        out[1] = cat

    index = lax.broadcasted_iota(jnp.int32, (ROWS, columns), 0)

    def with_low(s, k, tile):
        row = jnp.broadcast_to(from_low[s, 1, pl.ds(k, 1)], tile.shape)
        return tile + jnp.where(index == 0, RATES[s] * row, 0.0)

    def with_high(s, k, tile):
        row = jnp.broadcast_to(from_high[s, 0, pl.ds(k, 1)], tile.shape)
        return tile + jnp.where(index == ROWS - 1, RATES[s] * row, 0.0)

    @pl.loop(1, depth - 1)
    def _(k):
        for s in range(2):
            heads[s, k] = with_low(s, k, mid[s, k, span(0), :])
            tails[s, k] = with_high(s, k, mid[s, k, span(tiles - 1), :])

    def load(s, k, tile):
        if tile == 0:
            return heads[s, k]
        if tile == tiles - 1:
            return tails[s, k]
        return mid[s, k, span(tile), :]

    for s in range(2):
        for tile in range(tiles):
            if 0 < tile < tiles - 1:
                at = pl.ds(rows + (tile - 1) * ROWS, ROWS)
                first, last = down[s, at, :], up[s, at, :]
            else:
                first, last = q_down[s, span(1 if tile else 0), :], q_up[s, span(1 if tile else 0), :]
            if tile == 0:
                first, last = with_low(s, 0, first), with_low(s, depth - 1, last)
            if tile == tiles - 1:
                first, last = with_high(s, 0, first), with_high(s, depth - 1, last)
            near[s, 0, span(tile), :] = first
            far[s, 2, span(tile), :] = last
            for j in range(2):
                near[s, 1 + j, span(tile), :] = load(s, 1 + j, tile)
                far[s, j, span(tile), :] = load(s, depth - 3 + j, tile)

    seen[0] = jnp.zeros((rows, columns), jnp.float32)
    seen[1] = jnp.zeros((rows, columns), jnp.float32)
    seen[2] = jnp.ones((rows, columns), jnp.float32)

    @pl.loop(2, depth - 2)
    def _(k):
        def store(tile, sub, cat):
            at = span(tile)
            new[0, k, at, :] = sub
            new[1, k, at, :] = cat
            one, two, clear = composite(sub, cat, scale_sub, scale_cat, seen[2, at, :])
            seen[0, at, :] += one
            seen[1, at, :] += two
            seen[2, at, :] = clear

        plane_step(
            lambda s, tile: load(s, k, tile),
            tiles,
            [rows_low[s, pl.ds(k, 1)] for s in range(2)],
            [rows_high[s, pl.ds(k, 1)] for s in range(2)],
            lambda s, tile: load(s, k - 1, tile) + load(s, k + 1, tile),
            store,
        )
        for s in range(2):
            put(s, k).start()

    @pl.loop(2, depth - 2)
    def _(k):
        for s in range(2):
            put(s, k).wait()


def corner_kernel(rows, p_low, p_high, first, last):
    for side, p in enumerate((p_low, p_high)):
        for s in range(2):
            first[side, s : s + 1] = p[s, :1]
            last[side, s : s + 1] = p[s, rows - 1 : rows]


def rim_kernel(
    values, p_low, p_high, down, up, near, far, rows_low, rows_high, inner,
    ring, known, seen, mid,
):
    depth = rows_low.shape[1]
    rows, columns = inner.shape[1:]
    tiles = rows // ROWS
    scale_sub, scale_cat = across_columns(values[0], columns), across_columns(values[1], columns)
    for side, p, own, inside in ((0, p_low, down, near), (1, p_high, up, far)):
        zero, one, two = (0, 1, 2) if side == 0 else (2, 1, 0)
        outer, beside = (0, 1) if side == 0 else (depth - 1, depth - 2)
        for s in range(2):
            mid[side, s] = inside[s, zero] + RATES[s] * p[s, :rows]

        def store_known(tile, sub, cat, side=side, own=own):
            at = span(tile)
            known[side, 0, at, :] = sub + (RATES[0] * RATES[0]) * own[0, at, :]
            known[side, 1, at, :] = cat + (RATES[1] * RATES[1]) * own[1, at, :]

        plane_step(
            lambda s, tile, side=side: mid[side, s, span(tile), :],
            tiles,
            [rows_low[s, outer : outer + 1] for s in range(2)],
            [rows_high[s, outer : outer + 1] for s in range(2)],
            lambda s, tile, inside=inside, one=one: inside[s, one, span(tile), :],
            store_known,
        )

        def store_ring(tile, sub, cat, side=side):
            ring[0, side, span(tile), :] = sub
            ring[1, side, span(tile), :] = cat

        plane_step(
            lambda s, tile, inside=inside, one=one: inside[s, one, span(tile), :],
            tiles,
            [rows_low[s, beside : beside + 1] for s in range(2)],
            [rows_high[s, beside : beside + 1] for s in range(2)],
            lambda s, tile, inside=inside, two=two, side=side: inside[s, two, span(tile), :]
            + mid[side, s, span(tile), :],
            store_ring,
        )

    for tile in range(tiles):
        at = span(tile)
        one, two, clear = composite(ring[0, 0, at, :], ring[1, 0, at, :], scale_sub, scale_cat, 1.0)
        sub = one + clear * inner[0, at, :]
        cat = two + clear * inner[1, at, :]
        clear = clear * inner[2, at, :]
        one, two, clear = composite(ring[0, 1, at, :], ring[1, 1, at, :], scale_sub, scale_cat, clear)
        seen[0, at, :] = sub + one
        seen[1, at, :] = cat + two
        seen[2, at, :] = clear


def last_kernel(corners, values, known, q_low, q_high, seen, *rest):
    if corners:
        corner_low, corner_high, *rest = rest
    *pieces, outer, whole = rest
    rows, columns = seen.shape[1:]
    count = len(pieces)
    wide = columns // count
    tiles = rows // ROWS
    scale_sub, scale_cat = across_columns(values[0], columns), across_columns(values[1], columns)
    index = lax.broadcasted_iota(jnp.int32, (ROWS, columns), 0)
    for place, tile in enumerate((0, tiles - 1) if corners else range(1, tiles - 1)):
        at, to = span(tile), span(place)
        source = to if corners else pl.ds(rows + place * ROWS, ROWS)
        planes = []
        for side, q in enumerate((q_low, q_high)):
            for s in range(2):
                value = known[side, s, at, :] + RATES[s] * q[s, source, :]
                if corners:
                    corner, edge = (corner_low, 0) if tile == 0 else (corner_high, ROWS - 1)
                    row = jnp.broadcast_to(corner[side, s : s + 1], value.shape)
                    value = value + jnp.where(index == edge, (2.0 * RATES[s] * RATES[s]) * row, 0.0)
                outer[s, side, to, :] = value
                planes.append(value)
        one, two, clear = composite(planes[0], planes[1], scale_sub, scale_cat, 1.0)
        sub = one + clear * seen[0, at, :]
        cat = two + clear * seen[1, at, :]
        clear = clear * seen[2, at, :]
        one, two, clear = composite(planes[2], planes[3], scale_sub, scale_cat, clear)
        whole[0, to, :] = sub + one
        whole[1, to, :] = cat + two
        whole[2, to, :] = clear
    me = lax.axis_index("gz")
    for shift, piece in enumerate(pieces):
        target = lax.rem(me + shift, count)
        if wide % LANES == 0:
            piece[...] = whole[:, :, pl.ds(pl.multiple_of(target * wide, LANES), wide)]
        else:
            for other in range(count):

                @pl.when(target == other)
                def _(piece=piece, other=other):
                    piece[...] = whole[:, :, other * wide : (other + 1) * wide]


def shade_kernel(values, *pieces_and_rest):
    *pieces, image, slabs = pieces_and_rest
    count = len(pieces) // 2
    rows, wide = image.shape[1:]
    me = lax.axis_index("gz")
    for shift in range(count):
        slab = lax.rem(me + count - shift, count)
        inner, outer = pieces[shift], pieces[count + shift]
        slabs[slab, :, pl.ds(ROWS, rows - 2 * ROWS), :] = inner[...]
        slabs[slab, :, pl.ds(0, ROWS), :] = outer[:, :ROWS]
        slabs[slab, :, pl.ds(rows - ROWS, ROWS), :] = outer[:, ROWS:]
    for tile in range(rows // ROWS):
        at = span(tile)
        sub, cat, clear = slabs[0, 0, at, :], slabs[0, 1, at, :], slabs[0, 2, at, :]
        for slab in range(1, count):
            sub = sub + clear * slabs[slab, 0, at, :]
            cat = cat + clear * slabs[slab, 1, at, :]
            clear = clear * slabs[slab, 2, at, :]
        for channel in range(3):
            of_sub = across_columns(values[2 + channel * 2], wide)
            of_cat = across_columns(values[3 + channel * 2], wide)
            image[channel, at, :] = of_sub * sub + of_cat * cat
        image[3, at, :] = 1.0 - clear


def place_kernel(ring, inner, outer, sub_in, cat_in, sub_out, cat_out, sems):
    del sub_in, cat_in
    depth, rows, _ = sub_out.shape
    copies = []
    for s, out in enumerate((sub_out, cat_out)):
        for side in range(2):
            plane = side * (depth - 1)
            for source, target in (
                (ring.at[s, side], out.at[1 + side * (depth - 3)]),
                (inner.at[s, side], out.at[plane, pl.ds(ROWS, rows - 2 * ROWS)]),
                (outer.at[s, side, pl.ds(0, ROWS)], out.at[plane, pl.ds(0, ROWS)]),
                (outer.at[s, side, pl.ds(ROWS, ROWS)], out.at[plane, pl.ds(rows - ROWS, ROWS)]),
            ):
                copies.append(pltpu.make_async_copy(source, target, sems.at[len(copies)]))
    for copy in copies:
        copy.start()
    for copy in copies:
        copy.wait()


def call(kernel, flops, room, **kwargs):
    return pl.pallas_call(
        kernel,
        cost_estimate=pl.CostEstimate(flops=flops, bytes_accessed=1 << 16, transcendentals=0),
        compiler_params=pltpu.CompilerParams(vmem_limit_bytes=room << 20),
        **kwargs,
    )


def body(substrate, catalyst, extinction, emission):
    depth, rows, columns = substrate.shape
    count = lax.axis_size("gz")
    wide = columns // count
    share = OPTICAL / (depth * count)
    middle = rows - 2 * ROWS
    outers = 2 * ROWS

    def ring(size, shift):
        return [(i, (i + shift) % size) for i in range(size)]

    def shifted(x, axis, shift):
        return lax.ppermute(x, axis, ring(lax.axis_size(axis), shift))

    up, down, second, penult = call(
        planes_kernel,
        1 << 20,
        2,
        name="planes",
        out_shape=(f32(2, rows + middle, columns),) * 2 + (f32(2, rows, columns),) * 2,
        in_specs=[HBM, HBM],
        out_specs=(VMEM,) * 4,
        scratch_shapes=[pltpu.SemaphoreType.DMA((8,))],
    )(hbm(substrate), hbm(catalyst))
    p_low = shifted(up, "gz", 1)
    p_high = shifted(down, "gz", -1)

    old, own_low, own_high, q_up, q_down, values = call(
        functools.partial(prepare_kernel, share),
        1 << 22,
        2,
        name="prepare",
        out_shape=(
            f32(2, depth, rows, columns),
            f32(2, 2, depth, columns),
            f32(2, 2, depth, columns),
            f32(2, outers, columns),
            f32(2, outers, columns),
            f32(8, ROWS, LANES),
        ),
        in_specs=[SMEM, SMEM, HBM, HBM, VMEM, VMEM, VMEM, VMEM],
        out_specs=(VMEM,) * 6,
        scratch_shapes=[pltpu.SemaphoreType.DMA((2, depth))],
    )(extinction, emission, hbm(substrate), hbm(catalyst), up, down, second, penult)
    from_low = shifted(own_high, "gx", 1)
    from_high = shifted(own_low, "gx", -1)
    q_low = shifted(q_up, "gz", 1)
    q_high = shifted(q_down, "gz", -1)

    mid = call(
        first_kernel,
        1 << 24,
        2,
        name="first",
        out_shape=f32(2, depth, rows, columns),
        in_specs=[VMEM],
        out_specs=VMEM,
    )(old)

    sub_part, cat_part, inner, near, far, rows_low, rows_high = call(
        second_kernel,
        1 << 25,
        10,
        name="second",
        out_shape=(
            f32(depth, rows, columns),
            f32(depth, rows, columns),
            f32(3, rows, columns),
            f32(2, 3, rows, columns),
            f32(2, 3, rows, columns),
            f32(2, depth, columns),
            f32(2, depth, columns),
        ),
        in_specs=[VMEM] * 10,
        out_specs=(HBM, HBM) + (VMEM,) * 5,
        scratch_shapes=[
            pltpu.VMEM((2, depth, ROWS, columns), jnp.float32),
            pltpu.VMEM((2, depth, ROWS, columns), jnp.float32),
            pltpu.VMEM((2, depth, rows, columns), jnp.float32),
            pltpu.SemaphoreType.DMA((2, depth)),
        ],
    )(values, mid, up, down, q_up, q_down, from_low, from_high, own_low, own_high)

    p_low, p_high, inner = lax.optimization_barrier((p_low, p_high, inner))
    ring_planes, known, seen = call(
        rim_kernel,
        1 << 23,
        4,
        name="rim",
        out_shape=(f32(2, 2, rows, columns), f32(2, 2, rows, columns), f32(3, rows, columns)),
        in_specs=[VMEM] * 10,
        out_specs=(VMEM,) * 3,
        scratch_shapes=[pltpu.VMEM((2, 2, rows, columns), jnp.float32)],
    )(values, p_low, p_high, down, up, near, far, rows_low, rows_high, inner)

    def finish(corners, high, *args):
        *pieces, outer = call(
            functools.partial(last_kernel, corners),
            1 << 22,
            4,
            name="last" if corners else "most",
            out_shape=(f32(3, high, wide),) * count + (f32(2, 2, high, columns),),
            in_specs=[VMEM] * len(args),
            out_specs=(VMEM,) * (count + 1),
            scratch_shapes=[pltpu.VMEM((3, high, columns), jnp.float32)],
        )(*args)
        return [pieces[0]] + [shifted(pieces[i], "gz", i) for i in range(1, count)], outer

    inner_pieces, inner_rows = finish(False, middle, values, known, p_low, p_high, seen)

    first_rows, last_rows = call(
        functools.partial(corner_kernel, rows),
        1 << 18,
        2,
        name="corner",
        out_shape=(f32(2, 2, columns), f32(2, 2, columns)),
        in_specs=[VMEM, VMEM],
        out_specs=(VMEM, VMEM),
    )(p_low, p_high)
    corner_low = shifted(last_rows, "gx", 1)
    corner_high = shifted(first_rows, "gx", -1)

    outer_pieces, outer_rows = finish(True, outers, values, known, q_low, q_high, seen, corner_low, corner_high)

    sub_final, cat_final = call(
        place_kernel,
        1 << 22,
        2,
        name="place",
        out_shape=(f32(depth, rows, columns), f32(depth, rows, columns)),
        in_specs=[VMEM, VMEM, VMEM, HBM, HBM],
        out_specs=(HBM, HBM),
        input_output_aliases={3: 0, 4: 1},
        scratch_shapes=[pltpu.SemaphoreType.DMA((16,))],
    )(ring_planes, inner_rows, outer_rows, sub_part, cat_part)

    image = call(
        shade_kernel,
        1 << 20,
        4,
        name="shade",
        out_shape=f32(4, rows, wide),
        in_specs=[VMEM] * (1 + 2 * count),
        out_specs=VMEM,
        scratch_shapes=[pltpu.VMEM((count, 3, rows, wide), jnp.float32)],
    )(values, *inner_pieces, *outer_pieces)
    return sub_final, cat_final, image


def solution(mesh):
    placed = (P("gz", "gx", None), P("gz", "gx", None), P(), P())

    return jax.shard_map(
        body,
        mesh=mesh,
        in_specs=placed,
        out_specs=(P("gz", "gx", None), P("gz", "gx", None), P(None, "gx", "gz")),
        check_vma=False,
    )
```

time: 43 us -> 42.6 us (level)
  starting transfers between devices: 18.6 us -> 21.3 us
  Pallas kernels: 18.1 us -> 15.6 us
  waiting for transfers between devices: 5.26 us -> 4.62 us
    ppermute x11 -> x14, starting transfers between devices: 18.6 us -> 21.3 us  [shifted(): return lax.ppermute(x, axis, ring(lax.axis_size(axis), shift))]
    pallas_call x9 -> x10, Pallas kernels: 18.1 us -> 15.6 us  [the longest x1 4.86 us: body(): call(second_kernel, 1 << 25, 10, name='second', out_shape=(f32(depth, row...]
    ppermute x11 -> x14, waiting for transfers between devices: 5.26 us -> 4.62 us  [shifted(): return lax.ppermute(x, axis, ring(lax.axis_size(axis), shift))]
  transfers between devices with their start and end apart: 11 -> 14, of which waited for: 5 -> 3; matrix products, arithmetic and copies ran while one was open for 0% -> 0% of each run, Pallas kernels for 30% -> 31%
where the time goes in v2:
time: 42.6 us; the launch traced here: 42.5 us
  starting transfers between devices  21.3 us (50%)
  Pallas kernels  15.6 us (37%)
  waiting for transfers between devices  4.62 us (11%)
  between operations  0.78 us (2%)
    ppermute x14, starting transfers between devices, shifted(): return lax.ppermute(x, axis, ring(lax.axis_size(axis), shift))  21.3 us
    pallas_call x1, Pallas kernels, body(): call(second_kernel, 1 << 25, 10, name='second', out_shape=(f32(depth, row...  4.86 us
    ppermute x14, waiting for transfers between devices, shifted(): return lax.ppermute(x, axis, ring(lax.axis_size(axis), shift))  4.62 us
    pallas_call x1, Pallas kernels, body(): call(functools.partial(prepare_kernel, share), 1 << 22, 2, name='prepare'...  3.24 us
    pallas_call x1, Pallas kernels, body(): call(first_kernel, 1 << 24, 2, name='first', out_shape=f32(2, depth, rows...  3.08 us
    pallas_call x1, Pallas kernels, body(): call(planes_kernel, 1 << 20, 2, name='planes', out_shape=(f32(2, rows + m...  1.57 us
    pallas_call x1, Pallas kernels, body(): call(place_kernel, 1 << 22, 2, name='place', out_shape=(f32(depth, rows,...  1.08 us
  transfers between devices with their start and end apart: 14, of which 3 were waited for; matrix products, arithmetic and copies ran while one was open for 0% of the time, Pallas kernels for 31%

profile of v2, /device:TPU:0, one launch (start us, length us, event | category | flops | bytes accessed | tf_op | source)
XLA Modules:
  0.0 42.5 jit_solution(18297502084702997842)
XLA Ops:
  0.6 0.0 copy-start.1
  0.6 0.0 copy-start
  0.7 1.6 %planes.1 = (f32[2,48,1024]{2,1,0:T(8,128)S(1)}, f32[2,48,1024]{2,1,0:T(8,128)S(1)}, f32[2,32,1024]{2,1,0:T(8,128)S(1)}, f32[2,32,1024]{2,1,0:T(8,128)S(1)}) custom-call(f32[16,32,1024]{2,1,0:T(8,128)} %sub.3, f32[16,32,1024]{2,1,0:T(8,128)} %cat.3), custom_call_target="tpu_custom_call" | custom-call | flops 1048576 | bytes 65536 | tf_op jit(solution)/shard_map/planes/pallas_call | solution.py:435
  2.2 3.0 %collective-permute-start = (f32[2,48,1024]{2,1,0:T(8,128)S(1)}, f32[2,48,1024]{2,1,0:T(8,128)S(1)}, u32[]{:S(2)}, u32[]{:S(2)}) collective-permute-start(f32[2,48,1024]{2,1,0:T(8,128)S(1)} %get-tuple-element.40.up), channel_id=1, source_target_pairs={{0,8},{8,16},{16,24},{24,0},{1,9},{9,17},{17,25},{25,1},{2,10},{10... | collective-permute-start | bytes 1179656 | tf_op jit(solution)/shard_map/ppermute | solution.py:433
  5.2 1.0 %collective-permute-start.1 = (f32[2,48,1024]{2,1,0:T(8,128)S(1)}, f32[2,48,1024]{2,1,0:T(8,128)S(1)}, u32[]{:S(2)}, u32[]{:S(2)}) collective-permute-start(f32[2,48,1024]{2,1,0:T(8,128)S(1)} %get-tuple-element.41.down), channel_id=1, source_target_pairs={{0,24},{8,0},{16,8},{24,16},{1,25},{9,1},{17,9},{25,17},{2,26},{10... | collective-permute-start | bytes 1179656 | tf_op jit(solution)/shard_map/ppermute | solution.py:433
  6.3 0.0 copy-done.1
  6.3 0.1 copy.9.emission
  6.4 0.0 copy-done
  6.4 3.2 %prepare.1 = (f32[2,16,32,1024]{3,2,1,0:T(8,128)S(1)}, f32[2,2,16,1024]{3,2,1,0:T(8,128)S(1)}, f32[2,2,16,1024]{3,2,1,0:T(8,128)S(1)}, f32[2,16,1024]{2,1,0:T(8,...) custom-call(f32[2]{0:T(128)S(1)} %copy-done, f32[3,2]{1,0:T(4,128)S(1)} %copy.9.emission, ...), custom_call_target="tpu_custom_call" | custom-call | flops 4194304 | bytes 65536 | tf_op jit(solution)/shard_map/prepare/pallas_call | solution.py:448
  9.6 0.1 collective-permute-start.2
  9.7 3.5 %collective-permute-start.3 = (f32[2,2,16,1024]{3,2,1,0:T(8,128)S(1)}, f32[2,2,16,1024]{3,2,1,0:T(8,128)S(1)}, u32[]{:S(2)}, u32[]{:S(2)}) collective-permute-start(f32[2,2,16,1024]{3,2,1,0:T(8,128)S(1)} %get-tuple-element.49.own_low), channel_id=1, source_target_pairs={{0,7},{1,0},{2,1},{3,2},{4,3},{5,4},{6,5},{7,6},{8,15},{9,8},{10,9... | collective-permute-start | bytes 786440 | tf_op jit(solution)/shard_map/ppermute | solution.py:433
  13.2 1.0 %collective-permute-start.4 = (f32[2,16,1024]{2,1,0:T(8,128)S(1)}, f32[2,16,1024]{2,1,0:T(8,128)S(1)}, u32[]{:S(2)}, u32[]{:S(2)}) collective-permute-start(f32[2,16,1024]{2,1,0:T(8,128)S(1)} %get-tuple-element.46.q_up), channel_id=1, source_target_pairs={{0,8},{8,16},{16,24},{24,0},{1,9},{9,17},{17,25},{25,1},{2,10},{10... | collective-permute-start | bytes 393224 | tf_op jit(solution)/shard_map/ppermute | solution.py:433
  14.2 3.3 %collective-permute-done.2.from_low = f32[2,2,16,1024]{3,2,1,0:T(8,128)S(1)} collective-permute-done((f32[2,2,16,1024]{3,2,1,0:T(8,128)S(1)}, f32[2,2,16,1024]{3,2,1,0:T(8,128)S(1)}, u32[]{:S(2)}, u32[]{:S(2)}) %collective-permute-start.2) | collective-permute-done | bytes 262176 | tf_op jit(solution)/shard_map/ppermute | solution.py:433
  17.5 2.4 %collective-permute-start.5 = (f32[2,16,1024]{2,1,0:T(8,128)S(1)}, f32[2,16,1024]{2,1,0:T(8,128)S(1)}, u32[]{:S(2)}, u32[]{:S(2)}) collective-permute-start(f32[2,16,1024]{2,1,0:T(8,128)S(1)} %get-tuple-element.47.q_down), channel_id=1, source_target_pairs={{0,24},{8,0},{16,8},{24,16},{1,25},{9,1},{17,9},{25,17},{2,26},{10... | collective-permute-start | bytes 393224 | tf_op jit(solution)/shard_map/ppermute | solution.py:433
  19.9 3.1 %first.1.mid = f32[2,16,32,1024]{3,2,1,0:T(8,128)S(1)} custom-call(f32[2,16,32,1024]{3,2,1,0:T(8,128)S(1)} %get-tuple-element.45.old), custom_call_target="tpu_custom_call" | custom-call | flops 16777216 | bytes 65536 | tf_op jit(solution)/shard_map/first/pallas_call | solution.py:470
  23.0 0.0 collective-permute-done.3.from_high
  23.0 4.9 %second.1 = (f32[16,32,1024]{2,1,0:T(8,128)}, f32[16,32,1024]{2,1,0:T(8,128)}, f32[3,32,1024]{2,1,0:T(8,128)S(1)}, f32[2,3,32,1024]{3,2,1,0:T(8,128)S(1)}, f32[2...) custom-call(f32[8,8,128]{2,1,0:T(8,128)S(1)} %get-tuple-element.44.values, ...), custom_call_target="tpu_custom_call" | custom-call | flops 33554432 | bytes 65536 | tf_op jit(solution)/shard_map/second/pallas_call | solution.py:480
  27.9 0.0 collective-permute-done.p_low.q_low
  27.9 0.0 collective-permute-done.1.p_high.q_high
  27.9 0.8 %rim.1 = (f32[2,2,32,1024]{3,2,1,0:T(8,128)S(1)}, f32[2,2,32,1024]{3,2,1,0:T(8,128)S(1)}, f32[3,32,1024]{2,1,0:T(8,128)S(1)}) custom-call(f32[8,8,128]{2,1,0:T(8,128)S(1)} %get-tuple-element.44.values, f32[2,48,1024]{2,1,0:T(8,128)S(1)} %collective-permute-done.p_low.q_low, f32[2,48,1024]{2,1,0:T(8,128)S(1)} %collective-permute-done.1.p_high.q_high, ...), custom_call_target="tpu_custom_call" | custom-call | flops 8388608 | bytes 65536 | tf_op jit(solution)/shard_map/rim/pallas_call | solution.py:505
  28.7 0.1 most.1
  28.9 1.5 %collective-permute-start.10 = (f32[3,16,256]{2,1,0:T(8,128)S(1)}, f32[3,16,256]{2,1,0:T(8,128)S(1)}, u32[]{:S(2)}, u32[]{:S(2)}) collective-permute-start(f32[3,16,256]{2,1,0:T(8,128)S(1)} %get-tuple-element.72), channel_id=1, source_target_pairs={{0,24},{8,0},{16,8},{24,16},{1,25},{9,1},{17,9},{25,17},{2,26},{10... | collective-permute-start | bytes 147464 | tf_op jit(solution)/shard_map/ppermute | solution.py:433
  30.4 0.1 collective-permute-start.6
  30.4 3.5 %collective-permute-start.7 = (f32[2,2,1024]{2,1,0:T(2,128)S(1)}, f32[2,2,1024]{2,1,0:T(2,128)S(1)}, u32[]{:S(2)}, u32[]{:S(2)}) collective-permute-start(f32[2,2,1024]{2,1,0:T(2,128)S(1)} %get-tuple-element.63), channel_id=1, source_target_pairs={{0,7},{1,0},{2,1},{3,2},{4,3},{5,4},{6,5},{7,6},{8,15},{9,8},{10,9... | collective-permute-start | bytes 49160 | tf_op jit(solution)/shard_map/ppermute | solution.py:433
  33.9 0.0 collective-permute-done.4.q_low
  33.9 0.6 %collective-permute-start.8 = (f32[3,16,256]{2,1,0:T(8,128)S(1)}, f32[3,16,256]{2,1,0:T(8,128)S(1)}, u32[]{:S(2)}, u32[]{:S(2)}) collective-permute-start(f32[3,16,256]{2,1,0:T(8,128)S(1)} %get-tuple-element.70), channel_id=1, source_target_pairs={{0,8},{8,16},{16,24},{24,0},{1,9},{9,17},{17,25},{25,1},{2,10},{10... | collective-permute-start | bytes 147464 | tf_op jit(solution)/shard_map/ppermute | solution.py:433
  34.5 0.0 collective-permute-done.5.q_high
  34.5 0.5 %collective-permute-start.9 = (f32[3,16,256]{2,1,0:T(8,128)S(1)}, f32[3,16,256]{2,1,0:T(8,128)S(1)}, u32[]{:S(2)}, u32[]{:S(2)}) collective-permute-start(f32[3,16,256]{2,1,0:T(8,128)S(1)} %get-tuple-element.71), channel_id=1, source_target_pairs={{0,16},{8,24},{16,0},{24,8},{1,17},{9,25},{17,1},{25,9},{2,18},{10... | collective-permute-start | bytes 147464 | tf_op jit(solution)/shard_map/ppermute | solution.py:433
  35.0 0.3 collective-permute-done.6.rest_0_
  35.4 0.0 collective-permute-done.7.rest_1_
  35.4 0.1 last.1
  35.5 2.1 %collective-permute-start.11 = (f32[3,16,256]{2,1,0:T(8,128)S(1)}, f32[3,16,256]{2,1,0:T(8,128)S(1)}, u32[]{:S(2)}, u32[]{:S(2)}) collective-permute-start(f32[3,16,256]{2,1,0:T(8,128)S(1)} %get-tuple-element.74), channel_id=1, source_target_pairs={{0,8},{8,16},{16,24},{24,0},{1,9},{9,17},{17,25},{25,1},{2,10},{10... | collective-permute-start | bytes 147464 | tf_op jit(solution)/shard_map/ppermute | solution.py:433
  37.6 0.0 collective-permute-start.12
  37.7 0.0 collective-permute-done.10.pieces_and_rest_3_
  37.7 2.0 %collective-permute-start.13 = (f32[3,16,256]{2,1,0:T(8,128)S(1)}, f32[3,16,256]{2,1,0:T(8,128)S(1)}, u32[]{:S(2)}, u32[]{:S(2)}) collective-permute-start(f32[3,16,256]{2,1,0:T(8,128)S(1)} %get-tuple-element.76), channel_id=1, source_target_pairs={{0,24},{8,0},{16,8},{24,16},{1,25},{9,1},{17,9},{25,17},{2,26},{10... | collective-permute-start | bytes 147464 | tf_op jit(solution)/shard_map/ppermute | solution.py:433
  39.7 1.1 %place.1 = (f32[16,32,1024]{2,1,0:T(8,128)}, f32[16,32,1024]{2,1,0:T(8,128)}) custom-call(f32[2,2,32,1024]{3,2,1,0:T(8,128)S(1)} %get-tuple-element.58.ring, f32[2,2,16,1024]{3,2,1,0:T(8,128)S(1)} %get-tuple-element.61.inner, f32[2,2,16,1024]{3,2,1,0:T(8,128)S(1)} %get-tuple-element.64.outer, ...), custom_call_target="tpu_custom_call", output_to_operand_aliasing={{0}: (3, {}), {1}: (4, {})} | custom-call | flops 4194304 | bytes 65536 | tf_op jit(solution)/shard_map/place/pallas_call | solution.py:545
  40.8 0.0 collective-permute-done.8.pieces_and_rest_1_
  40.8 0.0 collective-permute-done.9.pieces_and_rest_2_
  40.8 0.0 collective-permute-done.11.pieces_and_rest_5_
  40.8 0.9 %collective-permute-done.12.pieces_and_rest_6_ = f32[3,16,256]{2,1,0:T(8,128)S(1)} collective-permute-done((f32[3,16,256]{2,1,0:T(8,128)S(1)}, f32[3,16,256]{2,1,0:T(8,128)S(1)}, u32[]{:S(2)}, u32[]{:S(2)}) %collective-permute-start.12) | collective-permute-done | bytes 49184 | tf_op jit(solution)/shard_map/ppermute | solution.py:433
  41.7 0.0 collective-permute-done.13.pieces_and_rest_7_
  41.8 0.7 %shade.1 = f32[4,32,256]{2,1,0:T(8,128)} custom-call(f32[8,8,128]{2,1,0:T(8,128)S(1)} %get-tuple-element.44.values, f32[3,16,256]{2,1,0:T(8,128)S(1)} %get-tuple-element.69.pieces_and_rest_0_, f32[3,16,256]{2,1,0:T(8,128)S(1)} %collective-permute-done.8.pieces_and_rest_1_, f32[3,16,256]{2,1,0:T(8,128)S(1)} %collective-permute-done.9.pieces_and_rest_2_, ...), custom_call_target="tpu_custom_call" | custom-call | flops 1048576 | bytes 65536 | tf_op jit(solution)/shard_map/shade/pallas_call | solution.py:557
  (1 shorter events, 0.0 us)
Async XLA Ops:
  0.6 5.6 %copy-start.1 = (f32[3,2]{0,1:T(2,128)S(1)}, f32[3,2]{0,1:T(2,128)}, u32[]{:S(2)}) copy-start(f32[3,2]{0,1:T(2,128)} %param.7) | copy-start | bytes 76
  0.6 5.7 %copy-start = (f32[2]{0:T(128)S(1)}, f32[2]{0:T(128)}, u32[]{:S(2)}) copy-start(f32[2]{0:T(128)} %scale.1) | copy-start | bytes 28
  2.2 25.7 %collective-permute-start = (f32[2,48,1024]{2,1,0:T(8,128)S(1)}, f32[2,48,1024]{2,1,0:T(8,128)S(1)}, u32[]{:S(2)}, u32[]{:S(2)}) collective-permute-start(f32[2,48,1024]{2,1,0:T(8,128)S(1)} %get-tuple-element.40.up), channel_id=1, source_target_pairs={{0,8},{8,16},{16,24},{24,0},{1,9},{9,17},{17,25},{25,1},{2,10},{10... | collective-permute-start | bytes 1179656 | tf_op jit(solution)/shard_map/ppermute | solution.py:433
  5.2 22.7 %collective-permute-start.1 = (f32[2,48,1024]{2,1,0:T(8,128)S(1)}, f32[2,48,1024]{2,1,0:T(8,128)S(1)}, u32[]{:S(2)}, u32[]{:S(2)}) collective-permute-start(f32[2,48,1024]{2,1,0:T(8,128)S(1)} %get-tuple-element.41.down), channel_id=1, source_target_pairs={{0,24},{8,0},{16,8},{24,16},{1,25},{9,1},{17,9},{25,17},{2,26},{10... | collective-permute-start | bytes 1179656 | tf_op jit(solution)/shard_map/ppermute | solution.py:433
  9.6 7.9 %collective-permute-start.2 = (f32[2,2,16,1024]{3,2,1,0:T(8,128)S(1)}, f32[2,2,16,1024]{3,2,1,0:T(8,128)S(1)}, u32[]{:S(2)}, u32[]{:S(2)}) collective-permute-start(f32[2,2,16,1024]{3,2,1,0:T(8,128)S(1)} %get-tuple-element.48.own_high), channel_id=1, source_target_pairs={{0,1},{1,2},{2,3},{3,4},{4,5},{5,6},{6,7},{7,0},{8,9},{9,10},{10,1... | collective-permute-start | bytes 786440 | tf_op jit(solution)/shard_map/ppermute | solution.py:433
  9.7 13.3 %collective-permute-start.3 = (f32[2,2,16,1024]{3,2,1,0:T(8,128)S(1)}, f32[2,2,16,1024]{3,2,1,0:T(8,128)S(1)}, u32[]{:S(2)}, u32[]{:S(2)}) collective-permute-start(f32[2,2,16,1024]{3,2,1,0:T(8,128)S(1)} %get-tuple-element.49.own_low), channel_id=1, source_target_pairs={{0,7},{1,0},{2,1},{3,2},{4,3},{5,4},{6,5},{7,6},{8,15},{9,8},{10,9... | collective-permute-start | bytes 786440 | tf_op jit(solution)/shard_map/ppermute | solution.py:433
  13.2 20.7 %collective-permute-start.4 = (f32[2,16,1024]{2,1,0:T(8,128)S(1)}, f32[2,16,1024]{2,1,0:T(8,128)S(1)}, u32[]{:S(2)}, u32[]{:S(2)}) collective-permute-start(f32[2,16,1024]{2,1,0:T(8,128)S(1)} %get-tuple-element.46.q_up), channel_id=1, source_target_pairs={{0,8},{8,16},{16,24},{24,0},{1,9},{9,17},{17,25},{25,1},{2,10},{10... | collective-permute-start | bytes 393224 | tf_op jit(solution)/shard_map/ppermute | solution.py:433
  17.5 17.0 %collective-permute-start.5 = (f32[2,16,1024]{2,1,0:T(8,128)S(1)}, f32[2,16,1024]{2,1,0:T(8,128)S(1)}, u32[]{:S(2)}, u32[]{:S(2)}) collective-permute-start(f32[2,16,1024]{2,1,0:T(8,128)S(1)} %get-tuple-element.47.q_down), channel_id=1, source_target_pairs={{0,24},{8,0},{16,8},{24,16},{1,25},{9,1},{17,9},{25,17},{2,26},{10... | collective-permute-start | bytes 393224 | tf_op jit(solution)/shard_map/ppermute | solution.py:433
  28.9 8.8 %collective-permute-start.10 = (f32[3,16,256]{2,1,0:T(8,128)S(1)}, f32[3,16,256]{2,1,0:T(8,128)S(1)}, u32[]{:S(2)}, u32[]{:S(2)}) collective-permute-start(f32[3,16,256]{2,1,0:T(8,128)S(1)} %get-tuple-element.72), channel_id=1, source_target_pairs={{0,24},{8,0},{16,8},{24,16},{1,25},{9,1},{17,9},{25,17},{2,26},{10... | collective-permute-start | bytes 147464 | tf_op jit(solution)/shard_map/ppermute | solution.py:433
  30.4 5.0 %collective-permute-start.6 = (f32[2,2,1024]{2,1,0:T(2,128)S(1)}, f32[2,2,1024]{2,1,0:T(2,128)S(1)}, u32[]{:S(2)}, u32[]{:S(2)}) collective-permute-start(f32[2,2,1024]{2,1,0:T(2,128)S(1)} %get-tuple-element.62), channel_id=1, source_target_pairs={{0,1},{1,2},{2,3},{3,4},{4,5},{5,6},{6,7},{7,0},{8,9},{9,10},{10,1... | collective-permute-start | bytes 49160 | tf_op jit(solution)/shard_map/ppermute | solution.py:433
  30.4 5.0 %collective-permute-start.7 = (f32[2,2,1024]{2,1,0:T(2,128)S(1)}, f32[2,2,1024]{2,1,0:T(2,128)S(1)}, u32[]{:S(2)}, u32[]{:S(2)}) collective-permute-start(f32[2,2,1024]{2,1,0:T(2,128)S(1)} %get-tuple-element.63), channel_id=1, source_target_pairs={{0,7},{1,0},{2,1},{3,2},{4,3},{5,4},{6,5},{7,6},{8,15},{9,8},{10,9... | collective-permute-start | bytes 49160 | tf_op jit(solution)/shard_map/ppermute | solution.py:433
  33.9 6.8 %collective-permute-start.8 = (f32[3,16,256]{2,1,0:T(8,128)S(1)}, f32[3,16,256]{2,1,0:T(8,128)S(1)}, u32[]{:S(2)}, u32[]{:S(2)}) collective-permute-start(f32[3,16,256]{2,1,0:T(8,128)S(1)} %get-tuple-element.70), channel_id=1, source_target_pairs={{0,8},{8,16},{16,24},{24,0},{1,9},{9,17},{17,25},{25,1},{2,10},{10... | collective-permute-start | bytes 147464 | tf_op jit(solution)/shard_map/ppermute | solution.py:433
  34.5 6.3 %collective-permute-start.9 = (f32[3,16,256]{2,1,0:T(8,128)S(1)}, f32[3,16,256]{2,1,0:T(8,128)S(1)}, u32[]{:S(2)}, u32[]{:S(2)}) collective-permute-start(f32[3,16,256]{2,1,0:T(8,128)S(1)} %get-tuple-element.71), channel_id=1, source_target_pairs={{0,16},{8,24},{16,0},{24,8},{1,17},{9,25},{17,1},{25,9},{2,18},{10... | collective-permute-start | bytes 147464 | tf_op jit(solution)/shard_map/ppermute | solution.py:433
  35.5 5.3 %collective-permute-start.11 = (f32[3,16,256]{2,1,0:T(8,128)S(1)}, f32[3,16,256]{2,1,0:T(8,128)S(1)}, u32[]{:S(2)}, u32[]{:S(2)}) collective-permute-start(f32[3,16,256]{2,1,0:T(8,128)S(1)} %get-tuple-element.74), channel_id=1, source_target_pairs={{0,8},{8,16},{16,24},{24,0},{1,9},{9,17},{17,25},{25,1},{2,10},{10... | collective-permute-start | bytes 147464 | tf_op jit(solution)/shard_map/ppermute | solution.py:433
  37.6 4.1 %collective-permute-start.12 = (f32[3,16,256]{2,1,0:T(8,128)S(1)}, f32[3,16,256]{2,1,0:T(8,128)S(1)}, u32[]{:S(2)}, u32[]{:S(2)}) collective-permute-start(f32[3,16,256]{2,1,0:T(8,128)S(1)} %get-tuple-element.75), channel_id=1, source_target_pairs={{0,16},{8,24},{16,0},{24,8},{1,17},{9,25},{17,1},{25,9},{2,18},{10... | collective-permute-start | bytes 147464 | tf_op jit(solution)/shard_map/ppermute | solution.py:433
  37.7 4.1 %collective-permute-start.13 = (f32[3,16,256]{2,1,0:T(8,128)S(1)}, f32[3,16,256]{2,1,0:T(8,128)S(1)}, u32[]{:S(2)}, u32[]{:S(2)}) collective-permute-start(f32[3,16,256]{2,1,0:T(8,128)S(1)} %get-tuple-element.76), channel_id=1, source_target_pairs={{0,24},{8,0},{16,8},{24,16},{1,25},{9,1},{17,9},{25,17},{2,26},{10... | collective-permute-start | bytes 147464 | tf_op jit(solution)/shard_map/ppermute | solution.py:433

commit v3 on v2

--- a/solution.py
+++ b/solution.py
@@ -100,10 +100,7 @@
         outer_step(outer, inner, rows, range(1, rows // ROWS - 1), store)
 
 
-def prepare_kernel(
-    share, scale, emission, sub, cat, up, down, second, penult,
-    old, low, high, q_up, q_down, values, sems,
-):
+def prepare_kernel(sub, cat, up, down, second, penult, old, low, high, q_up, q_down, sems):
     depth, rows, _ = sub.shape
     copies = []
     for plane in range(depth):
@@ -111,32 +108,34 @@
             copies.append(pltpu.make_async_copy(field.at[plane], old.at[s, plane], sems.at[s, plane]))
     for copy in copies:
         copy.start()
+    for outer, inner, out in ((up, penult, q_up), (down, second, q_down)):
+
+        def store(tile, sub_new, cat_new, out=out):
+            at = span(0 if tile == 0 else 1)
+            out[0, at, :] = sub_new
+            out[1, at, :] = cat_new
+
+        outer_step(outer, inner, rows, (0, rows // ROWS - 1), store)
+    for plane in range(depth):
+        for s in range(2):
+            copies[2 * plane + s].wait()
+            for row in range(2):
+                low[s, row, plane : plane + 1] = old[s, plane, row : row + 1]
+                high[s, row, plane : plane + 1] = old[s, plane, rows - 2 + row : rows - 1 + row]
+
+
+def composite(sub, cat, scale_sub, scale_cat, clear):
+    keep = jnp.exp(-(scale_sub * sub + scale_cat * cat))
+    weight = clear * (1.0 - keep)
+    return weight * sub, weight * cat, clear * keep
+
+
+def scalars_kernel(share, scale, emission, values):
     shape = values.shape[1:]
     for s in range(2):
         values[s] = jnp.full(shape, scale[s] * share, jnp.float32)
         for channel in range(3):
-            values[2 + channel * 2 + s] = jnp.full(shape, emission[channel, s], jnp.float32)
-    for outer, inner, out in ((up, penult, q_up), (down, second, q_down)):
-
-        def store(tile, sub_new, cat_new, out=out):
-            at = span(0 if tile == 0 else 1)
-            out[0, at, :] = sub_new
-            out[1, at, :] = cat_new
-
-        outer_step(outer, inner, rows, (0, rows // ROWS - 1), store)
-    for copy in copies:
-        copy.wait()
-    for s in range(2):
-        for row in range(2):
-            for plane in range(depth):
-                low[s, row, plane : plane + 1] = old[s, plane, row : row + 1]
-                high[s, row, plane : plane + 1] = old[s, plane, rows - 2 + row : rows - 1 + row]
-
-
-def composite(sub, cat, scale_sub, scale_cat, clear):
-    keep = jnp.exp(-(scale_sub * sub + scale_cat * cat))
-    weight = clear * (1.0 - keep)
-    return weight * sub, weight * cat, clear * keep
+            values[2 + channel * 2 + s] = jnp.full(shape, emission[s, channel], jnp.float32)
 
 
 def first_kernel(old, mid):
@@ -259,11 +258,15 @@
             put(s, k).wait()
 
 
-def corner_kernel(rows, p_low, p_high, first, last):
-    for side, p in enumerate((p_low, p_high)):
-        for s in range(2):
-            first[side, s : s + 1] = p[s, :1]
-            last[side, s : s + 1] = p[s, rows - 1 : rows]
+def rows_kernel(q_up, q_down, from_low, from_high, up, down):
+    depth = from_low.shape[2]
+    for plane, q, out in ((depth - 1, q_up, up), (0, q_down, down)):
+        for place, edge, source in ((0, 0, from_low.at[:, 1]), (1, ROWS - 1, from_high.at[:, 0])):
+            for s in range(2):
+                tile = q[s, span(place), :]
+                index = lax.broadcasted_iota(jnp.int32, tile.shape, 0)
+                row = jnp.broadcast_to(source[s, plane : plane + 1], tile.shape)
+                out[s, span(place), :] = tile + jnp.where(index == edge, (2.0 * RATES[s]) * row, 0.0)
 
 
 def rim_kernel(
@@ -320,27 +323,20 @@
         seen[2, at, :] = clear
 
 
-def last_kernel(corners, values, known, q_low, q_high, seen, *rest):
-    if corners:
-        corner_low, corner_high, *rest = rest
+def last_kernel(outermost, values, known, q_low, q_high, seen, *rest):
     *pieces, outer, whole = rest
     rows, columns = seen.shape[1:]
     count = len(pieces)
     wide = columns // count
     tiles = rows // ROWS
     scale_sub, scale_cat = across_columns(values[0], columns), across_columns(values[1], columns)
-    index = lax.broadcasted_iota(jnp.int32, (ROWS, columns), 0)
-    for place, tile in enumerate((0, tiles - 1) if corners else range(1, tiles - 1)):
+    for place, tile in enumerate((0, tiles - 1) if outermost else range(1, tiles - 1)):
         at, to = span(tile), span(place)
-        source = to if corners else pl.ds(rows + place * ROWS, ROWS)
+        source = to if outermost else pl.ds(rows + place * ROWS, ROWS)
         planes = []
         for side, q in enumerate((q_low, q_high)):
             for s in range(2):
                 value = known[side, s, at, :] + RATES[s] * q[s, source, :]
-                if corners:
-                    corner, edge = (corner_low, 0) if tile == 0 else (corner_high, ROWS - 1)
-                    row = jnp.broadcast_to(corner[side, s : s + 1], value.shape)
-                    value = value + jnp.where(index == edge, (2.0 * RATES[s] * RATES[s]) * row, 0.0)
                 outer[s, side, to, :] = value
                 planes.append(value)
         one, two, clear = composite(planes[0], planes[1], scale_sub, scale_cat, 1.0)
@@ -445,8 +441,8 @@
     p_low = shifted(up, "gz", 1)
     p_high = shifted(down, "gz", -1)
 
-    old, own_low, own_high, q_up, q_down, values = call(
-        functools.partial(prepare_kernel, share),
+    old, own_low, own_high, q_up, q_down = call(
+        prepare_kernel,
         1 << 22,
         2,
         name="prepare",
@@ -456,16 +452,13 @@
             f32(2, 2, depth, columns),
             f32(2, outers, columns),
             f32(2, outers, columns),
-            f32(8, ROWS, LANES),
         ),
-        in_specs=[SMEM, SMEM, HBM, HBM, VMEM, VMEM, VMEM, VMEM],
-        out_specs=(VMEM,) * 6,
+        in_specs=[HBM, HBM, VMEM, VMEM, VMEM, VMEM],
+        out_specs=(VMEM,) * 5,
         scratch_shapes=[pltpu.SemaphoreType.DMA((2, depth))],
-    )(extinction, emission, hbm(substrate), hbm(catalyst), up, down, second, penult)
+    )(hbm(substrate), hbm(catalyst), up, down, second, penult)
     from_low = shifted(own_high, "gx", 1)
     from_high = shifted(own_low, "gx", -1)
-    q_low = shifted(q_up, "gz", 1)
-    q_high = shifted(q_down, "gz", -1)
 
     mid = call(
         first_kernel,
@@ -476,6 +469,27 @@
         in_specs=[VMEM],
         out_specs=VMEM,
     )(old)
+    values = call(
+        functools.partial(scalars_kernel, share),
+        1 << 18,
+        2,
+        name="scalars",
+        out_shape=f32(8, ROWS, LANES),
+        in_specs=[SMEM, SMEM],
+        out_specs=VMEM,
+    )(extinction, emission.T)
+
+    m_up, m_down = call(
+        rows_kernel,
+        1 << 18,
+        2,
+        name="rows",
+        out_shape=(f32(2, outers, columns),) * 2,
+        in_specs=[VMEM] * 4,
+        out_specs=(VMEM,) * 2,
+    )(q_up, q_down, from_low, from_high)
+    q_low = shifted(m_up, "gz", 1)
+    q_high = shifted(m_down, "gz", -1)
 
     sub_part, cat_part, inner, near, far, rows_low, rows_high = call(
         second_kernel,
@@ -513,34 +527,25 @@
         scratch_shapes=[pltpu.VMEM((2, 2, rows, columns), jnp.float32)],
     )(values, p_low, p_high, down, up, near, far, rows_low, rows_high, inner)
 
-    def finish(corners, high, *args):
+    def finish(outermost, high, *args):
         *pieces, outer = call(
-            functools.partial(last_kernel, corners),
+            functools.partial(last_kernel, outermost),
             1 << 22,
             4,
-            name="last" if corners else "most",
+            name="last" if outermost else "most",
             out_shape=(f32(3, high, wide),) * count + (f32(2, 2, high, columns),),
             in_specs=[VMEM] * len(args),
             out_specs=(VMEM,) * (count + 1),
             scratch_shapes=[pltpu.VMEM((3, high, columns), jnp.float32)],
         )(*args)
-        return [pieces[0]] + [shifted(pieces[i], "gz", i) for i in range(1, count)], outer
+        received = [pieces[0]]
+        for shift in range(1, count):
+            received.append(shifted(pieces[shift], "gz", shift))
+        return received, outer
 
     inner_pieces, inner_rows = finish(False, middle, values, known, p_low, p_high, seen)
 
-    first_rows, last_rows = call(
-        functools.partial(corner_kernel, rows),
-        1 << 18,
-        2,
-        name="corner",
-        out_shape=(f32(2, 2, columns), f32(2, 2, columns)),
-        in_specs=[VMEM, VMEM],
-        out_specs=(VMEM, VMEM),
-    )(p_low, p_high)
-    corner_low = shifted(last_rows, "gx", 1)
-    corner_high = shifted(first_rows, "gx", -1)
-
-    outer_pieces, outer_rows = finish(True, outers, values, known, q_low, q_high, seen, corner_low, corner_high)
+    outer_pieces, outer_rows = finish(True, outers, values, known, q_low, q_high, seen)
 
     sub_final, cat_final = call(
         place_kernel,

time: 42.6 us -> 41.3 us (0.969)
  starting transfers between devices: 21.3 us -> 17.7 us
  waiting for transfers between devices: 4.62 us -> 7.34 us
    ppermute x14 -> x12, starting transfers between devices: 21.3 us -> 17.7 us  [shifted(): return lax.ppermute(x, axis, ring(lax.axis_size(axis), shift))]
    ppermute x14 -> x12, waiting for transfers between devices: 4.62 us -> 7.34 us  [shifted(): return lax.ppermute(x, axis, ring(lax.axis_size(axis), shift))]
    pallas_call x4 -> x5, Pallas kernels: 3.48 us -> 3.37 us  [the longest x1 2.56 us: body(): call(prepare_kernel, 1 << 22, 2, name='prepare', out_shape=(f32(2, depth,...]
  transfers between devices with their start and end apart: 14 -> 12, of which waited for: 3 -> 6; matrix products, arithmetic and copies ran while one was open for 0% -> 0% of each run, Pallas kernels for 31% -> 32%
where the time goes in v3:
time: 41.3 us; the launch traced here: 41.2 us
  starting transfers between devices  17.7 us (43%)
  Pallas kernels  15.4 us (37%)
  waiting for transfers between devices  7.34 us (18%)
  between operations  0.75 us (2%)
    ppermute x12, starting transfers between devices, shifted(): return lax.ppermute(x, axis, ring(lax.axis_size(axis), shift))  17.7 us
    ppermute x12, waiting for transfers between devices, shifted(): return lax.ppermute(x, axis, ring(lax.axis_size(axis), shift))  7.34 us
    pallas_call x1, Pallas kernels, body(): call(second_kernel, 1 << 25, 10, name='second', out_shape=(f32(depth, row...  4.86 us
    pallas_call x1, Pallas kernels, body(): call(first_kernel, 1 << 24, 2, name='first', out_shape=f32(2, depth, rows...  2.95 us
    pallas_call x1, Pallas kernels, body(): call(prepare_kernel, 1 << 22, 2, name='prepare', out_shape=(f32(2, depth,...  2.56 us
    pallas_call x1, Pallas kernels, body(): call(planes_kernel, 1 << 20, 2, name='planes', out_shape=(f32(2, rows + m...  1.56 us
    pallas_call x1, Pallas kernels, body(): call(place_kernel, 1 << 22, 2, name='place', out_shape=(f32(depth, rows,...  1.08 us
    pallas_call x1, Pallas kernels, body(): call(rim_kernel, 1 << 23, 4, name='rim', out_shape=(f32(2, 2, rows, colum...  0.83 us
  transfers between devices with their start and end apart: 12, of which 6 were waited for; matrix products, arithmetic and copies ran while one was open for 0% of the time, Pallas kernels for 32%

profile of v3, /device:TPU:0, one launch (start us, length us, event | category | flops | bytes accessed | tf_op | source)
XLA Modules:
  0.0 41.2 jit_solution(6596370026750261934)
XLA Ops:
  0.6 1.6 %planes.1 = (f32[2,48,1024]{2,1,0:T(8,128)S(1)}, f32[2,48,1024]{2,1,0:T(8,128)S(1)}, f32[2,32,1024]{2,1,0:T(8,128)S(1)}, f32[2,32,1024]{2,1,0:T(8,128)S(1)}) custom-call(f32[16,32,1024]{2,1,0:T(8,128)} %sub.3, f32[16,32,1024]{2,1,0:T(8,128)} %cat.3), custom_call_target="tpu_custom_call" | custom-call | flops 1048576 | bytes 65536 | tf_op jit(solution)/shard_map/planes/pallas_call | solution.py:431
  2.2 3.0 %collective-permute-start = (f32[2,48,1024]{2,1,0:T(8,128)S(1)}, f32[2,48,1024]{2,1,0:T(8,128)S(1)}, u32[]{:S(2)}, u32[]{:S(2)}) collective-permute-start(f32[2,48,1024]{2,1,0:T(8,128)S(1)} %get-tuple-element.39.up), channel_id=1, source_target_pairs={{0,8},{8,16},{16,24},{24,0},{1,9},{9,17},{17,25},{25,1},{2,10},{10... | collective-permute-start | bytes 1179656 | tf_op jit(solution)/shard_map/ppermute | solution.py:429
  5.2 1.0 %collective-permute-start.1 = (f32[2,48,1024]{2,1,0:T(8,128)S(1)}, f32[2,48,1024]{2,1,0:T(8,128)S(1)}, u32[]{:S(2)}, u32[]{:S(2)}) collective-permute-start(f32[2,48,1024]{2,1,0:T(8,128)S(1)} %get-tuple-element.40.down), channel_id=1, source_target_pairs={{0,24},{8,0},{16,8},{24,16},{1,25},{9,1},{17,9},{25,17},{2,26},{10... | collective-permute-start | bytes 1179656 | tf_op jit(solution)/shard_map/ppermute | solution.py:429
  6.2 0.0 copy-start
  6.2 0.0 copy-start.1
  6.2 2.6 %prepare.1 = (f32[2,16,32,1024]{3,2,1,0:T(8,128)S(1)}, f32[2,2,16,1024]{3,2,1,0:T(8,128)S(1)}, f32[2,2,16,1024]{3,2,1,0:T(8,128)S(1)}, f32[2,16,1024]{2,1,0:T(8,128)S(1)}, f32[2,16,1024]{2,1,0:T(8,128)S(1)}) custom-call(f32[16,32,1024]{2,1,0:T(8,128)} %sub.3, f32[16,32,1024]{2,1,0:T(8,128)} %cat.3, f32[2,48,1024]{2,1,0:T(8,128)S(1)} %get-tuple-element.39.up, ...), custom_call_target="tpu_custom_call" | custom-call | flops 4194304 | bytes 65536 | tf_op jit(solution)/shard_map/prepare/pallas_call | solution.py:444
  8.8 0.1 collective-permute-start.2
  8.9 3.5 %collective-permute-start.3 = (f32[2,2,16,1024]{3,2,1,0:T(8,128)S(1)}, f32[2,2,16,1024]{3,2,1,0:T(8,128)S(1)}, u32[]{:S(2)}, u32[]{:S(2)}) collective-permute-start(f32[2,2,16,1024]{3,2,1,0:T(8,128)S(1)} %get-tuple-element.47.own_low), channel_id=1, source_target_pairs={{0,7},{1,0},{2,1},{3,2},{4,3},{5,4},{6,5},{7,6},{8,15},{9,8},{10,9... | collective-permute-start | bytes 786440 | tf_op jit(solution)/shard_map/ppermute | solution.py:429
  12.4 4.3 %collective-permute-done.2.from_low = f32[2,2,16,1024]{3,2,1,0:T(8,128)S(1)} collective-permute-done((f32[2,2,16,1024]{3,2,1,0:T(8,128)S(1)}, f32[2,2,16,1024]{3,2,1,0:T(8,128)S(1)}, u32[]{:S(2)}, u32[]{:S(2)}) %collective-permute-start.2) | collective-permute-done | bytes 262176 | tf_op jit(solution)/shard_map/ppermute | solution.py:429
  16.8 0.3 collective-permute-done.3.from_high
  17.1 1.2 %collective-permute-start.4 = (f32[2,16,1024]{2,1,0:T(8,128)S(1)}, f32[2,16,1024]{2,1,0:T(8,128)S(1)}, u32[]{:S(2)}, u32[]{:S(2)}) collective-permute-start(f32[2,16,1024]{2,1,0:T(8,128)S(1)} %get-tuple-element.60), channel_id=1, source_target_pairs={{0,8},{8,16},{16,24},{24,0},{1,9},{9,17},{17,25},{25,1},{2,10},{10... | collective-permute-start | bytes 393224 | tf_op jit(solution)/shard_map/ppermute | solution.py:429
  18.3 1.8 %collective-permute-start.5 = (f32[2,16,1024]{2,1,0:T(8,128)S(1)}, f32[2,16,1024]{2,1,0:T(8,128)S(1)}, u32[]{:S(2)}, u32[]{:S(2)}) collective-permute-start(f32[2,16,1024]{2,1,0:T(8,128)S(1)} %get-tuple-element.61), channel_id=1, source_target_pairs={{0,24},{8,0},{16,8},{24,16},{1,25},{9,1},{17,9},{25,17},{2,26},{10... | collective-permute-start | bytes 393224 | tf_op jit(solution)/shard_map/ppermute | solution.py:429
  20.1 0.0 copy-done
  20.1 0.0 copy-done.1
  20.1 0.6 %scalars.1.values = f32[8,8,128]{2,1,0:T(8,128)S(1)} custom-call(f32[2]{0:T(128)S(1)} %copy-done.1, f32[2,3]{1,0:T(2,128)S(1)} %bitcast.1), custom_call_target="tpu_custom_call" | custom-call | flops 262144 | bytes 65536 | tf_op jit(solution)/shard_map/scalars/pallas_call | solution.py:472
  20.6 3.0 %first.1.mid = f32[2,16,32,1024]{3,2,1,0:T(8,128)S(1)} custom-call(f32[2,16,32,1024]{3,2,1,0:T(8,128)S(1)} %get-tuple-element.43.old), custom_call_target="tpu_custom_call" | custom-call | flops 16777216 | bytes 65536 | tf_op jit(solution)/shard_map/first/pallas_call | solution.py:463
  23.6 4.9 %second.1 = (f32[16,32,1024]{2,1,0:T(8,128)}, f32[16,32,1024]{2,1,0:T(8,128)}, f32[3,32,1024]{2,1,0:T(8,128)S(1)}, f32[2,3,32,1024]{3,2,1,0:T(8,128)S(1)}, f32[2...) custom-call(f32[8,8,128]{2,1,0:T(8,128)S(1)} %scalars.1.values, ...), custom_call_target="tpu_custom_call" | custom-call | flops 33554432 | bytes 65536 | tf_op jit(solution)/shard_map/second/pallas_call | solution.py:494
  28.5 0.0 collective-permute-done.p_low.q_low
  28.5 0.0 collective-permute-done.1.p_high.q_high
  28.5 0.8 %rim.1 = (f32[2,2,32,1024]{3,2,1,0:T(8,128)S(1)}, f32[2,2,32,1024]{3,2,1,0:T(8,128)S(1)}, f32[3,32,1024]{2,1,0:T(8,128)S(1)}) custom-call(f32[8,8,128]{2,1,0:T(8,128)S(1)} %scalars.1.values, f32[2,48,1024]{2,1,0:T(8,128)S(1)} %collective-permute-done.p_low.q_low, f32[2,48,1024]{2,1,0:T(8,128)S(1)} %collective-permute-done.1.p_high.q_high, ...), custom_call_target="tpu_custom_call" | custom-call | flops 8388608 | bytes 65536 | tf_op jit(solution)/shard_map/rim/pallas_call | solution.py:519
  29.3 0.0 collective-permute-done.4.q_low
  29.3 0.3 collective-permute-done.5.q_high
  29.6 0.1 last.1
  29.7 1.9 %collective-permute-start.10 = (f32[3,16,256]{2,1,0:T(8,128)S(1)}, f32[3,16,256]{2,1,0:T(8,128)S(1)}, u32[]{:S(2)}, u32[]{:S(2)}) collective-permute-start(f32[3,16,256]{2,1,0:T(8,128)S(1)} %get-tuple-element.73), channel_id=1, source_target_pairs={{0,16},{8,24},{16,0},{24,8},{1,17},{9,25},{17,1},{25,9},{2,18},{10... | collective-permute-start | bytes 147464 | tf_op jit(solution)/shard_map/ppermute | solution.py:429
  31.6 1.1 %collective-permute-start.11 = (f32[3,16,256]{2,1,0:T(8,128)S(1)}, f32[3,16,256]{2,1,0:T(8,128)S(1)}, u32[]{:S(2)}, u32[]{:S(2)}) collective-permute-start(f32[3,16,256]{2,1,0:T(8,128)S(1)} %get-tuple-element.74), channel_id=1, source_target_pairs={{0,24},{8,0},{16,8},{24,16},{1,25},{9,1},{17,9},{25,17},{2,26},{10... | collective-permute-start | bytes 147464 | tf_op jit(solution)/shard_map/ppermute | solution.py:429
  32.7 0.9 %collective-permute-start.9 = (f32[3,16,256]{2,1,0:T(8,128)S(1)}, f32[3,16,256]{2,1,0:T(8,128)S(1)}, u32[]{:S(2)}, u32[]{:S(2)}) collective-permute-start(f32[3,16,256]{2,1,0:T(8,128)S(1)} %get-tuple-element.72), channel_id=1, source_target_pairs={{0,8},{8,16},{16,24},{24,0},{1,9},{9,17},{17,25},{25,1},{2,10},{10... | collective-permute-start | bytes 147464 | tf_op jit(solution)/shard_map/ppermute | solution.py:429
  33.6 0.1 most.1
  33.7 1.1 %collective-permute-start.6 = (f32[3,16,256]{2,1,0:T(8,128)S(1)}, f32[3,16,256]{2,1,0:T(8,128)S(1)}, u32[]{:S(2)}, u32[]{:S(2)}) collective-permute-start(f32[3,16,256]{2,1,0:T(8,128)S(1)} %get-tuple-element.68), channel_id=1, source_target_pairs={{0,8},{8,16},{16,24},{24,0},{1,9},{9,17},{17,25},{25,1},{2,10},{10... | collective-permute-start | bytes 147464 | tf_op jit(solution)/shard_map/ppermute | solution.py:429
  34.8 1.5 %collective-permute-start.7 = (f32[3,16,256]{2,1,0:T(8,128)S(1)}, f32[3,16,256]{2,1,0:T(8,128)S(1)}, u32[]{:S(2)}, u32[]{:S(2)}) collective-permute-start(f32[3,16,256]{2,1,0:T(8,128)S(1)} %get-tuple-element.69), channel_id=1, source_target_pairs={{0,16},{8,24},{16,0},{24,8},{1,17},{9,25},{17,1},{25,9},{2,18},{10... | collective-permute-start | bytes 147464 | tf_op jit(solution)/shard_map/ppermute | solution.py:429
  36.4 0.0 collective-permute-done.10.pieces_and_rest_6_
  36.4 0.5 %collective-permute-start.8 = (f32[3,16,256]{2,1,0:T(8,128)S(1)}, f32[3,16,256]{2,1,0:T(8,128)S(1)}, u32[]{:S(2)}, u32[]{:S(2)}) collective-permute-start(f32[3,16,256]{2,1,0:T(8,128)S(1)} %get-tuple-element.70), channel_id=1, source_target_pairs={{0,24},{8,0},{16,8},{24,16},{1,25},{9,1},{17,9},{25,17},{2,26},{10... | collective-permute-start | bytes 147464 | tf_op jit(solution)/shard_map/ppermute | solution.py:429
  36.9 1.1 %place.1 = (f32[16,32,1024]{2,1,0:T(8,128)}, f32[16,32,1024]{2,1,0:T(8,128)}) custom-call(f32[2,2,32,1024]{3,2,1,0:T(8,128)S(1)} %get-tuple-element.56.ring, f32[2,2,16,1024]{3,2,1,0:T(8,128)S(1)} %get-tuple-element.59.inner, f32[2,2,16,1024]{3,2,1,0:T(8,128)S(1)} %get-tuple-element.62.outer, ...), custom_call_target="tpu_custom_call", output_to_operand_aliasing={{0}: (3, {}), {1}: (4, {})} | custom-call | flops 4194304 | bytes 65536 | tf_op jit(solution)/shard_map/place/pallas_call | solution.py:550
  38.0 0.0 collective-permute-done.11.pieces_and_rest_7_
  38.0 0.0 collective-permute-done.9.pieces_and_rest_5_
  38.0 1.3 %collective-permute-done.6.pieces_and_rest_1_ = f32[3,16,256]{2,1,0:T(8,128)S(1)} collective-permute-done((f32[3,16,256]{2,1,0:T(8,128)S(1)}, f32[3,16,256]{2,1,0:T(8,128)S(1)}, u32[]{:S(2)}, u32[]{:S(2)}) %collective-permute-start.6) | collective-permute-done | bytes 49184 | tf_op jit(solution)/shard_map/ppermute | solution.py:429
  39.3 0.5 %collective-permute-done.7.pieces_and_rest_2_ = f32[3,16,256]{2,1,0:T(8,128)S(1)} collective-permute-done((f32[3,16,256]{2,1,0:T(8,128)S(1)}, f32[3,16,256]{2,1,0:T(8,128)S(1)}, u32[]{:S(2)}, u32[]{:S(2)}) %collective-permute-start.7) | collective-permute-done | bytes 49184 | tf_op jit(solution)/shard_map/ppermute | solution.py:429
  39.8 0.6 %collective-permute-done.8.pieces_and_rest_3_ = f32[3,16,256]{2,1,0:T(8,128)S(1)} collective-permute-done((f32[3,16,256]{2,1,0:T(8,128)S(1)}, f32[3,16,256]{2,1,0:T(8,128)S(1)}, u32[]{:S(2)}, u32[]{:S(2)}) %collective-permute-start.8) | collective-permute-done | bytes 49184 | tf_op jit(solution)/shard_map/ppermute | solution.py:429
  40.5 0.7 %shade.1 = f32[4,32,256]{2,1,0:T(8,128)} custom-call(f32[8,8,128]{2,1,0:T(8,128)S(1)} %scalars.1.values, f32[3,16,256]{2,1,0:T(8,128)S(1)} %get-tuple-element.67.pieces_and_rest_0_, f32[3,16,256]{2,1,0:T(8,128)S(1)} %collective-permute-done.6.pieces_and_rest_1_, f32[3,16,256]{2,1,0:T(8,128)S(1)} %collective-permute-done.7.pieces_and_rest_2_, ...), custom_call_target="tpu_custom_call" | custom-call | flops 1048576 | bytes 65536 | tf_op jit(solution)/shard_map/shade/pallas_call | solution.py:562
  (1 shorter events, 0.0 us)
Async XLA Ops:
  2.2 26.3 %collective-permute-start = (f32[2,48,1024]{2,1,0:T(8,128)S(1)}, f32[2,48,1024]{2,1,0:T(8,128)S(1)}, u32[]{:S(2)}, u32[]{:S(2)}) collective-permute-start(f32[2,48,1024]{2,1,0:T(8,128)S(1)} %get-tuple-element.39.up), channel_id=1, source_target_pairs={{0,8},{8,16},{16,24},{24,0},{1,9},{9,17},{17,25},{25,1},{2,10},{10... | collective-permute-start | bytes 1179656 | tf_op jit(solution)/shard_map/ppermute | solution.py:429
  5.2 23.2 %collective-permute-start.1 = (f32[2,48,1024]{2,1,0:T(8,128)S(1)}, f32[2,48,1024]{2,1,0:T(8,128)S(1)}, u32[]{:S(2)}, u32[]{:S(2)}) collective-permute-start(f32[2,48,1024]{2,1,0:T(8,128)S(1)} %get-tuple-element.40.down), channel_id=1, source_target_pairs={{0,24},{8,0},{16,8},{24,16},{1,25},{9,1},{17,9},{25,17},{2,26},{10... | collective-permute-start | bytes 1179656 | tf_op jit(solution)/shard_map/ppermute | solution.py:429
  6.2 13.8 %copy-start = (f32[3,2]{0,1:T(2,128)S(1)}, f32[3,2]{0,1:T(2,128)}, u32[]{:S(2)}) copy-start(f32[3,2]{0,1:T(2,128)} %param.7) | copy-start | bytes 76
  6.2 13.8 %copy-start.1 = (f32[2]{0:T(128)S(1)}, f32[2]{0:T(128)}, u32[]{:S(2)}) copy-start(f32[2]{0:T(128)} %scale.1) | copy-start | bytes 28
  8.8 7.9 %collective-permute-start.2 = (f32[2,2,16,1024]{3,2,1,0:T(8,128)S(1)}, f32[2,2,16,1024]{3,2,1,0:T(8,128)S(1)}, u32[]{:S(2)}, u32[]{:S(2)}) collective-permute-start(f32[2,2,16,1024]{3,2,1,0:T(8,128)S(1)} %get-tuple-element.46.own_high), channel_id=1, source_target_pairs={{0,1},{1,2},{2,3},{3,4},{4,5},{5,6},{6,7},{7,0},{8,9},{9,10},{10,1... | collective-permute-start | bytes 786440 | tf_op jit(solution)/shard_map/ppermute | solution.py:429
  8.9 8.1 %collective-permute-start.3 = (f32[2,2,16,1024]{3,2,1,0:T(8,128)S(1)}, f32[2,2,16,1024]{3,2,1,0:T(8,128)S(1)}, u32[]{:S(2)}, u32[]{:S(2)}) collective-permute-start(f32[2,2,16,1024]{3,2,1,0:T(8,128)S(1)} %get-tuple-element.47.own_low), channel_id=1, source_target_pairs={{0,7},{1,0},{2,1},{3,2},{4,3},{5,4},{6,5},{7,6},{8,15},{9,8},{10,9... | collective-permute-start | bytes 786440 | tf_op jit(solution)/shard_map/ppermute | solution.py:429
  17.1 12.2 %collective-permute-start.4 = (f32[2,16,1024]{2,1,0:T(8,128)S(1)}, f32[2,16,1024]{2,1,0:T(8,128)S(1)}, u32[]{:S(2)}, u32[]{:S(2)}) collective-permute-start(f32[2,16,1024]{2,1,0:T(8,128)S(1)} %get-tuple-element.60), channel_id=1, source_target_pairs={{0,8},{8,16},{16,24},{24,0},{1,9},{9,17},{17,25},{25,1},{2,10},{10... | collective-permute-start | bytes 393224 | tf_op jit(solution)/shard_map/ppermute | solution.py:429
  18.3 11.3 %collective-permute-start.5 = (f32[2,16,1024]{2,1,0:T(8,128)S(1)}, f32[2,16,1024]{2,1,0:T(8,128)S(1)}, u32[]{:S(2)}, u32[]{:S(2)}) collective-permute-start(f32[2,16,1024]{2,1,0:T(8,128)S(1)} %get-tuple-element.61), channel_id=1, source_target_pairs={{0,24},{8,0},{16,8},{24,16},{1,25},{9,1},{17,9},{25,17},{2,26},{10... | collective-permute-start | bytes 393224 | tf_op jit(solution)/shard_map/ppermute | solution.py:429
  29.7 6.7 %collective-permute-start.10 = (f32[3,16,256]{2,1,0:T(8,128)S(1)}, f32[3,16,256]{2,1,0:T(8,128)S(1)}, u32[]{:S(2)}, u32[]{:S(2)}) collective-permute-start(f32[3,16,256]{2,1,0:T(8,128)S(1)} %get-tuple-element.73), channel_id=1, source_target_pairs={{0,16},{8,24},{16,0},{24,8},{1,17},{9,25},{17,1},{25,9},{2,18},{10... | collective-permute-start | bytes 147464 | tf_op jit(solution)/shard_map/ppermute | solution.py:429
  31.6 6.4 %collective-permute-start.11 = (f32[3,16,256]{2,1,0:T(8,128)S(1)}, f32[3,16,256]{2,1,0:T(8,128)S(1)}, u32[]{:S(2)}, u32[]{:S(2)}) collective-permute-start(f32[3,16,256]{2,1,0:T(8,128)S(1)} %get-tuple-element.74), channel_id=1, source_target_pairs={{0,24},{8,0},{16,8},{24,16},{1,25},{9,1},{17,9},{25,17},{2,26},{10... | collective-permute-start | bytes 147464 | tf_op jit(solution)/shard_map/ppermute | solution.py:429
  32.7 5.3 %collective-permute-start.9 = (f32[3,16,256]{2,1,0:T(8,128)S(1)}, f32[3,16,256]{2,1,0:T(8,128)S(1)}, u32[]{:S(2)}, u32[]{:S(2)}) collective-permute-start(f32[3,16,256]{2,1,0:T(8,128)S(1)} %get-tuple-element.72), channel_id=1, source_target_pairs={{0,8},{8,16},{16,24},{24,0},{1,9},{9,17},{17,25},{25,1},{2,10},{10... | collective-permute-start | bytes 147464 | tf_op jit(solution)/shard_map/ppermute | solution.py:429
  33.7 5.6 %collective-permute-start.6 = (f32[3,16,256]{2,1,0:T(8,128)S(1)}, f32[3,16,256]{2,1,0:T(8,128)S(1)}, u32[]{:S(2)}, u32[]{:S(2)}) collective-permute-start(f32[3,16,256]{2,1,0:T(8,128)S(1)} %get-tuple-element.68), channel_id=1, source_target_pairs={{0,8},{8,16},{16,24},{24,0},{1,9},{9,17},{17,25},{25,1},{2,10},{10... | collective-permute-start | bytes 147464 | tf_op jit(solution)/shard_map/ppermute | solution.py:429
  34.8 5.0 %collective-permute-start.7 = (f32[3,16,256]{2,1,0:T(8,128)S(1)}, f32[3,16,256]{2,1,0:T(8,128)S(1)}, u32[]{:S(2)}, u32[]{:S(2)}) collective-permute-start(f32[3,16,256]{2,1,0:T(8,128)S(1)} %get-tuple-element.69), channel_id=1, source_target_pairs={{0,16},{8,24},{16,0},{24,8},{1,17},{9,25},{17,1},{25,9},{2,18},{10... | collective-permute-start | bytes 147464 | tf_op jit(solution)/shard_map/ppermute | solution.py:429
  36.4 4.1 %collective-permute-start.8 = (f32[3,16,256]{2,1,0:T(8,128)S(1)}, f32[3,16,256]{2,1,0:T(8,128)S(1)}, u32[]{:S(2)}, u32[]{:S(2)}) collective-permute-start(f32[3,16,256]{2,1,0:T(8,128)S(1)} %get-tuple-element.70), channel_id=1, source_target_pairs={{0,24},{8,0},{16,8},{24,16},{1,25},{9,1},{17,9},{25,17},{2,26},{10... | collective-permute-start | bytes 147464 | tf_op jit(solution)/shard_map/ppermute | solution.py:429

commit v4 on v3

--- a/solution.py
+++ b/solution.py
@@ -100,14 +100,13 @@
         outer_step(outer, inner, rows, range(1, rows // ROWS - 1), store)
 
 
-def prepare_kernel(sub, cat, up, down, second, penult, old, low, high, q_up, q_down, sems):
+def prepare_kernel(sub, cat, up, down, second, penult, low, high, q_up, q_down):
     depth, rows, _ = sub.shape
-    copies = []
-    for plane in range(depth):
-        for s, field in enumerate((sub, cat)):
-            copies.append(pltpu.make_async_copy(field.at[plane], old.at[s, plane], sems.at[s, plane]))
-    for copy in copies:
-        copy.start()
+    for s, field in enumerate((sub, cat)):
+        for plane in range(depth):
+            for row in range(2):
+                low[s, row, plane : plane + 1] = field[plane, row : row + 1]
+                high[s, row, plane : plane + 1] = field[plane, rows - 2 + row : rows - 1 + row]
     for outer, inner, out in ((up, penult, q_up), (down, second, q_down)):
 
         def store(tile, sub_new, cat_new, out=out):
@@ -116,12 +115,6 @@
             out[1, at, :] = cat_new
 
         outer_step(outer, inner, rows, (0, rows // ROWS - 1), store)
-    for plane in range(depth):
-        for s in range(2):
-            copies[2 * plane + s].wait()
-            for row in range(2):
-                low[s, row, plane : plane + 1] = old[s, plane, row : row + 1]
-                high[s, row, plane : plane + 1] = old[s, plane, rows - 2 + row : rows - 1 + row]
 
 
 def composite(sub, cat, scale_sub, scale_cat, clear):
@@ -138,37 +131,96 @@
             values[2 + channel * 2 + s] = jnp.full(shape, emission[s, channel], jnp.float32)
 
 
-def first_kernel(old, mid):
-    depth, rows, _ = old.shape[1:]
+def first_kernel(sub, cat, mid):
+    depth, rows, _ = sub.shape
+    old = (sub, cat)
 
     @pl.loop(1, depth - 1)
     def _(k):
-        def store(tile, sub, cat):
-            mid[0, k, span(tile), :] = sub
-            mid[1, k, span(tile), :] = cat
+        def store(tile, sub_new, cat_new):
+            mid[0, k, span(tile), :] = sub_new
+            mid[1, k, span(tile), :] = cat_new
 
         plane_step(
-            lambda s, tile: old[s, k, span(tile), :],
+            lambda s, tile: old[s][k, span(tile), :],
             rows // ROWS,
             None,
             None,
-            lambda s, tile: old[s, k - 1, span(tile), :] + old[s, k + 1, span(tile), :],
+            lambda s, tile: old[s][k - 1, span(tile), :] + old[s][k + 1, span(tile), :],
             store,
         )
 
 
+def image_step(k, load, tiles, only, low_rows, high_rows, scales, seen, keep):
+    def store(tile, sub, cat):
+        at = span(tile)
+        keep(tile, sub, cat)
+        one, two, clear = composite(sub, cat, *scales, seen[2, at, :])
+        seen[0, at, :] += one
+        seen[1, at, :] += two
+        seen[2, at, :] = clear
+
+    plane_step(
+        lambda s, tile: load(s, k, tile),
+        tiles,
+        low_rows,
+        high_rows,
+        lambda s, tile: load(s, k - 1, tile) + load(s, k + 1, tile),
+        store,
+        only,
+    )
+
+
+def clear_image(seen):
+    seen[0] = jnp.zeros(seen.shape[1:], jnp.float32)
+    seen[1] = jnp.zeros(seen.shape[1:], jnp.float32)
+    seen[2] = jnp.ones(seen.shape[1:], jnp.float32)
+
+
+def center_kernel(values, mid, sub_out, cat_out, seen, new, sem_out):
+    depth, rows, columns = sub_out.shape
+    outputs = (sub_out, cat_out)
+    tiles = rows // ROWS
+    scales = across_columns(values[0], columns), across_columns(values[1], columns)
+    inside = pl.ds(ROWS, rows - 2 * ROWS)
+
+    def put(s, k):
+        return pltpu.make_async_copy(new.at[s, k], outputs[s].at[k, inside], sem_out.at[s, k])
+
+    clear_image(seen)
+
+    @pl.loop(2, depth - 2)
+    def _(k):
+        def keep(tile, sub, cat):
+            new[0, k, span(tile - 1), :] = sub
+            new[1, k, span(tile - 1), :] = cat
+
+        image_step(
+            k, lambda s, k, tile: mid[s, k, span(tile), :], tiles, range(1, tiles - 1), None, None, scales, seen, keep
+        )
+        for s in range(2):
+            put(s, k).start()
+
+    @pl.loop(2, depth - 2)
+    def _(k):
+        for s in range(2):
+            put(s, k).wait()
+
+
 def second_kernel(
-    values, mid, up, down, q_up, q_down, from_low, from_high, own_low, own_high,
+    values, mid, up, down, q_up, q_down, from_low, from_high, own_low, own_high, center, sub_in, cat_in,
     sub_out, cat_out, seen, near, far, rows_low, rows_high,
     heads, tails, new, sem_out,
 ):
+    del sub_in, cat_in
     depth, rows, columns = sub_out.shape
     outputs = (sub_out, cat_out)
     tiles = rows // ROWS
-    scale_sub, scale_cat = across_columns(values[0], columns), across_columns(values[1], columns)
-
-    def put(s, k):
-        return pltpu.make_async_copy(new.at[s, k], outputs[s].at[k], sem_out.at[s, k])
+    scales = across_columns(values[0], columns), across_columns(values[1], columns)
+
+    def put(s, k, end):
+        at = pl.ds(end * (rows - ROWS), ROWS)
+        return pltpu.make_async_copy(new.at[s, end, k], outputs[s].at[k, at], sem_out.at[s, end, k])
 
     which = lax.broadcasted_iota(jnp.int32, (depth, columns), 0)
     for got, at, own, at_own, out in (
@@ -226,36 +278,37 @@
                 near[s, 1 + j, span(tile), :] = load(s, 1 + j, tile)
                 far[s, j, span(tile), :] = load(s, depth - 3 + j, tile)
 
-    seen[0] = jnp.zeros((rows, columns), jnp.float32)
-    seen[1] = jnp.zeros((rows, columns), jnp.float32)
-    seen[2] = jnp.ones((rows, columns), jnp.float32)
+    clear_image(seen)
+    for tile in range(1, tiles - 1):
+        for part in range(3):
+            seen[part, span(tile), :] = center[part, span(tile), :]
 
     @pl.loop(2, depth - 2)
     def _(k):
-        def store(tile, sub, cat):
-            at = span(tile)
-            new[0, k, at, :] = sub
-            new[1, k, at, :] = cat
-            one, two, clear = composite(sub, cat, scale_sub, scale_cat, seen[2, at, :])
-            seen[0, at, :] += one
-            seen[1, at, :] += two
-            seen[2, at, :] = clear
-
-        plane_step(
-            lambda s, tile: load(s, k, tile),
+        def keep(tile, sub, cat):
+            new[0, 1 if tile else 0, k] = sub
+            new[1, 1 if tile else 0, k] = cat
+
+        image_step(
+            k,
+            load,
             tiles,
+            (0, tiles - 1),
             [rows_low[s, pl.ds(k, 1)] for s in range(2)],
             [rows_high[s, pl.ds(k, 1)] for s in range(2)],
-            lambda s, tile: load(s, k - 1, tile) + load(s, k + 1, tile),
-            store,
+            scales,
+            seen,
+            keep,
         )
         for s in range(2):
-            put(s, k).start()
+            for end in range(2):
+                put(s, k, end).start()
 
     @pl.loop(2, depth - 2)
     def _(k):
         for s in range(2):
-            put(s, k).wait()
+            for end in range(2):
+                put(s, k, end).wait()
 
 
 def rows_kernel(q_up, q_down, from_low, from_high, up, down):
@@ -441,22 +494,20 @@
     p_low = shifted(up, "gz", 1)
     p_high = shifted(down, "gz", -1)
 
-    old, own_low, own_high, q_up, q_down = call(
+    own_low, own_high, q_up, q_down = call(
         prepare_kernel,
         1 << 22,
         2,
         name="prepare",
         out_shape=(
-            f32(2, depth, rows, columns),
             f32(2, 2, depth, columns),
             f32(2, 2, depth, columns),
             f32(2, outers, columns),
             f32(2, outers, columns),
         ),
-        in_specs=[HBM, HBM, VMEM, VMEM, VMEM, VMEM],
-        out_specs=(VMEM,) * 5,
-        scratch_shapes=[pltpu.SemaphoreType.DMA((2, depth))],
-    )(hbm(substrate), hbm(catalyst), up, down, second, penult)
+        in_specs=[VMEM] * 6,
+        out_specs=(VMEM,) * 4,
+    )(substrate, catalyst, up, down, second, penult)
     from_low = shifted(own_high, "gx", 1)
     from_high = shifted(own_low, "gx", -1)
 
@@ -466,9 +517,9 @@
         2,
         name="first",
         out_shape=f32(2, depth, rows, columns),
-        in_specs=[VMEM],
+        in_specs=[VMEM, VMEM],
         out_specs=VMEM,
-    )(old)
+    )(substrate, catalyst)
     values = call(
         functools.partial(scalars_kernel, share),
         1 << 18,
@@ -478,6 +529,20 @@
         in_specs=[SMEM, SMEM],
         out_specs=VMEM,
     )(extinction, emission.T)
+
+    sub_part, cat_part, center = call(
+        center_kernel,
+        1 << 24,
+        4,
+        name="center",
+        out_shape=(f32(depth, rows, columns), f32(depth, rows, columns), f32(3, rows, columns)),
+        in_specs=[VMEM, VMEM],
+        out_specs=(HBM, HBM, VMEM),
+        scratch_shapes=[
+            pltpu.VMEM((2, depth, middle, columns), jnp.float32),
+            pltpu.SemaphoreType.DMA((2, depth)),
+        ],
+    )(values, mid)
 
     m_up, m_down = call(
         rows_kernel,
@@ -505,15 +570,16 @@
             f32(2, depth, columns),
             f32(2, depth, columns),
         ),
-        in_specs=[VMEM] * 10,
+        in_specs=[VMEM] * 11 + [HBM, HBM],
         out_specs=(HBM, HBM) + (VMEM,) * 5,
+        input_output_aliases={11: 0, 12: 1},
         scratch_shapes=[
             pltpu.VMEM((2, depth, ROWS, columns), jnp.float32),
             pltpu.VMEM((2, depth, ROWS, columns), jnp.float32),
-            pltpu.VMEM((2, depth, rows, columns), jnp.float32),
-            pltpu.SemaphoreType.DMA((2, depth)),
+            pltpu.VMEM((2, 2, depth, ROWS, columns), jnp.float32),
+            pltpu.SemaphoreType.DMA((2, 2, depth)),
         ],
-    )(values, mid, up, down, q_up, q_down, from_low, from_high, own_low, own_high)
+    )(values, mid, up, down, q_up, q_down, from_low, from_high, own_low, own_high, center, sub_part, cat_part)
 
     p_low, p_high, inner = lax.optimization_barrier((p_low, p_high, inner))
     ring_planes, known, seen = call(

time: 41.3 us -> 41.5 us (level)
    pallas_call x1, Pallas kernels: 4.86 us -> 4.02 us  [body(): call(second_kernel, 1 << 25, 10, name='second', out_shape=(f32(depth, row...]
    pallas_call x1 -> x2, Pallas kernels: 2.56 us -> 3.3 us  [the longest x1 2.98 us: body(): call(center_kernel, 1 << 24, 4, name='center', out_shape=(f32(depth, rows...]
  transfers between devices with their start and end apart: 12 -> 12, of which waited for: 6 -> 6; matrix products, arithmetic and copies ran while one was open for 0% -> 0% of each run, Pallas kernels for 32% -> 31%
where the time goes in v4:
time: 41.5 us; the launch traced here: 41.3 us
  starting transfers between devices  17.7 us (43%)
  Pallas kernels  15.4 us (37%)
  waiting for transfers between devices  7.41 us (18%)
  between operations  0.78 us (2%)
    ppermute x12, starting transfers between devices, shifted(): return lax.ppermute(x, axis, ring(lax.axis_size(axis), shift))  17.7 us
    ppermute x12, waiting for transfers between devices, shifted(): return lax.ppermute(x, axis, ring(lax.axis_size(axis), shift))  7.41 us
    pallas_call x1, Pallas kernels, body(): call(second_kernel, 1 << 25, 10, name='second', out_shape=(f32(depth, row...  4.02 us
    pallas_call x1, Pallas kernels, body(): call(center_kernel, 1 << 24, 4, name='center', out_shape=(f32(depth, rows...  2.98 us
    pallas_call x1, Pallas kernels, body(): call(first_kernel, 1 << 24, 2, name='first', out_shape=f32(2, depth, rows...  2.95 us
    pallas_call x1, Pallas kernels, body(): call(planes_kernel, 1 << 20, 2, name='planes', out_shape=(f32(2, rows + m...  1.7 us
    pallas_call x1, Pallas kernels, body(): call(place_kernel, 1 << 22, 2, name='place', out_shape=(f32(depth, rows,...  1.08 us
  transfers between devices with their start and end apart: 12, of which 6 were waited for; matrix products, arithmetic and copies ran while one was open for 0% of the time, Pallas kernels for 31%

profile of v4, /device:TPU:0, one launch (start us, length us, event | category | flops | bytes accessed | tf_op | source)
XLA Modules:
  0.0 41.3 jit_solution(12559398794664987842)
XLA Ops:
  0.6 0.0 copy-start
  0.6 0.0 copy-start.1
  0.6 1.7 %planes.1 = (f32[2,48,1024]{2,1,0:T(8,128)S(1)}, f32[2,48,1024]{2,1,0:T(8,128)S(1)}, f32[2,32,1024]{2,1,0:T(8,128)S(1)}, f32[2,32,1024]{2,1,0:T(8,128)S(1)}) custom-call(f32[16,32,1024]{2,1,0:T(8,128)} %sub.5, f32[16,32,1024]{2,1,0:T(8,128)} %cat.5), custom_call_target="tpu_custom_call" | custom-call | flops 1048576 | bytes 65536 | tf_op jit(solution)/shard_map/planes/pallas_call | solution.py:484
  2.4 3.0 %collective-permute-start = (f32[2,48,1024]{2,1,0:T(8,128)S(1)}, f32[2,48,1024]{2,1,0:T(8,128)S(1)}, u32[]{:S(2)}, u32[]{:S(2)}) collective-permute-start(f32[2,48,1024]{2,1,0:T(8,128)S(1)} %get-tuple-element.41.up), channel_id=1, source_target_pairs={{0,8},{8,16},{16,24},{24,0},{1,9},{9,17},{17,25},{25,1},{2,10},{10... | collective-permute-start | bytes 1179656 | tf_op jit(solution)/shard_map/ppermute | solution.py:482
  5.4 1.0 %collective-permute-start.1 = (f32[2,48,1024]{2,1,0:T(8,128)S(1)}, f32[2,48,1024]{2,1,0:T(8,128)S(1)}, u32[]{:S(2)}, u32[]{:S(2)}) collective-permute-start(f32[2,48,1024]{2,1,0:T(8,128)S(1)} %get-tuple-element.42.down), channel_id=1, source_target_pairs={{0,24},{8,0},{16,8},{24,16},{1,25},{9,1},{17,9},{25,17},{2,26},{10... | collective-permute-start | bytes 1179656 | tf_op jit(solution)/shard_map/ppermute | solution.py:482
  6.4 0.0 copy-done
  6.4 0.0 copy-done.1
  6.4 0.0 copy-start.2
  6.4 0.0 copy-start.3
  6.4 0.3 prepare.1
  6.7 0.1 collective-permute-start.2
  6.8 3.5 %collective-permute-start.3 = (f32[2,2,16,1024]{3,2,1,0:T(8,128)S(1)}, f32[2,2,16,1024]{3,2,1,0:T(8,128)S(1)}, u32[]{:S(2)}, u32[]{:S(2)}) collective-permute-start(f32[2,2,16,1024]{3,2,1,0:T(8,128)S(1)} %get-tuple-element.48.own_low), channel_id=1, source_target_pairs={{0,7},{1,0},{2,1},{3,2},{4,3},{5,4},{6,5},{7,6},{8,15},{9,8},{10,9... | collective-permute-start | bytes 786440 | tf_op jit(solution)/shard_map/ppermute | solution.py:482
  10.3 4.3 %collective-permute-done.2.from_low = f32[2,2,16,1024]{3,2,1,0:T(8,128)S(1)} collective-permute-done((f32[2,2,16,1024]{3,2,1,0:T(8,128)S(1)}, f32[2,2,16,1024]{3,2,1,0:T(8,128)S(1)}, u32[]{:S(2)}, u32[]{:S(2)}) %collective-permute-start.2) | collective-permute-done | bytes 262176 | tf_op jit(solution)/shard_map/ppermute | solution.py:482
  14.7 0.3 collective-permute-done.3.from_high
  15.0 1.2 %collective-permute-start.4 = (f32[2,16,1024]{2,1,0:T(8,128)S(1)}, f32[2,16,1024]{2,1,0:T(8,128)S(1)}, u32[]{:S(2)}, u32[]{:S(2)}) collective-permute-start(f32[2,16,1024]{2,1,0:T(8,128)S(1)} %get-tuple-element.64), channel_id=1, source_target_pairs={{0,8},{8,16},{16,24},{24,0},{1,9},{9,17},{17,25},{25,1},{2,10},{10... | collective-permute-start | bytes 393224 | tf_op jit(solution)/shard_map/ppermute | solution.py:482
  16.2 1.8 %collective-permute-start.5 = (f32[2,16,1024]{2,1,0:T(8,128)S(1)}, f32[2,16,1024]{2,1,0:T(8,128)S(1)}, u32[]{:S(2)}, u32[]{:S(2)}) collective-permute-start(f32[2,16,1024]{2,1,0:T(8,128)S(1)} %get-tuple-element.65), channel_id=1, source_target_pairs={{0,24},{8,0},{16,8},{24,16},{1,25},{9,1},{17,9},{25,17},{2,26},{10... | collective-permute-start | bytes 393224 | tf_op jit(solution)/shard_map/ppermute | solution.py:482
  18.0 0.0 copy-done.2
  18.0 0.0 copy-done.3
  18.0 0.6 %scalars.1.values = f32[8,8,128]{2,1,0:T(8,128)S(1)} custom-call(f32[2]{0:T(128)S(1)} %copy-done.3, f32[2,3]{1,0:T(2,128)S(1)} %bitcast.1), custom_call_target="tpu_custom_call" | custom-call | flops 262144 | bytes 65536 | tf_op jit(solution)/shard_map/scalars/pallas_call | solution.py:523
  18.6 3.0 %first.1.mid = f32[2,16,32,1024]{3,2,1,0:T(8,128)S(1)} custom-call(f32[16,32,1024]{2,1,0:T(8,128)S(1)} %copy-done, f32[16,32,1024]{2,1,0:T(8,128)S(1)} %copy-done.1), custom_call_target="tpu_custom_call" | custom-call | flops 16777216 | bytes 65536 | tf_op jit(solution)/shard_map/first/pallas_call | solution.py:514
  21.5 3.0 %center.1 = (f32[16,32,1024]{2,1,0:T(8,128)}, f32[16,32,1024]{2,1,0:T(8,128)}, f32[3,32,1024]{2,1,0:T(8,128)S(1)}) custom-call(f32[8,8,128]{2,1,0:T(8,128)S(1)} %scalars.1.values, f32[2,16,32,1024]{3,2,1,0:T(8,128)S(1)} %first.1.mid), custom_call_target="tpu_custom_call" | custom-call | flops 16777216 | bytes 65536 | tf_op jit(solution)/shard_map/center/pallas_call | solution.py:533
  24.5 4.0 %second.1 = (f32[16,32,1024]{2,1,0:T(8,128)}, f32[16,32,1024]{2,1,0:T(8,128)}, f32[3,32,1024]{2,1,0:T(8,128)S(1)}, f32[2,3,32,1024]{3,2,1,0:T(8,128)S(1)}, f32[2...) custom-call(f32[8,8,128]{2,1,0:T(8,128)S(1)} %scalars.1.values, ...), custom_call_target="tpu_custom_call", output_to_operand_aliasing={{0}: (11, {}), {1}: (12, {})} | custom-call | flops 33554432 | bytes 65536 | tf_op jit(solution)/shard_map/second/pallas_call | solution.py:559
  28.5 0.0 collective-permute-done.p_low.q_low
  28.6 0.0 collective-permute-done.1.p_high.q_high
  28.6 0.8 %rim.1 = (f32[2,2,32,1024]{3,2,1,0:T(8,128)S(1)}, f32[2,2,32,1024]{3,2,1,0:T(8,128)S(1)}, f32[3,32,1024]{2,1,0:T(8,128)S(1)}) custom-call(f32[8,8,128]{2,1,0:T(8,128)S(1)} %scalars.1.values, f32[2,48,1024]{2,1,0:T(8,128)S(1)} %collective-permute-done.p_low.q_low, f32[2,48,1024]{2,1,0:T(8,128)S(1)} %collective-permute-done.1.p_high.q_high, ...), custom_call_target="tpu_custom_call" | custom-call | flops 8388608 | bytes 65536 | tf_op jit(solution)/shard_map/rim/pallas_call | solution.py:585
  29.4 0.0 collective-permute-done.4.q_low
  29.4 0.3 collective-permute-done.5.q_high
  29.7 0.1 last.1
  29.9 1.8 %collective-permute-start.10 = (f32[3,16,256]{2,1,0:T(8,128)S(1)}, f32[3,16,256]{2,1,0:T(8,128)S(1)}, u32[]{:S(2)}, u32[]{:S(2)}) collective-permute-start(f32[3,16,256]{2,1,0:T(8,128)S(1)} %get-tuple-element.77), channel_id=1, source_target_pairs={{0,16},{8,24},{16,0},{24,8},{1,17},{9,25},{17,1},{25,9},{2,18},{10... | collective-permute-start | bytes 147464 | tf_op jit(solution)/shard_map/ppermute | solution.py:482
  31.7 1.2 %collective-permute-start.11 = (f32[3,16,256]{2,1,0:T(8,128)S(1)}, f32[3,16,256]{2,1,0:T(8,128)S(1)}, u32[]{:S(2)}, u32[]{:S(2)}) collective-permute-start(f32[3,16,256]{2,1,0:T(8,128)S(1)} %get-tuple-element.78), channel_id=1, source_target_pairs={{0,24},{8,0},{16,8},{24,16},{1,25},{9,1},{17,9},{25,17},{2,26},{10... | collective-permute-start | bytes 147464 | tf_op jit(solution)/shard_map/ppermute | solution.py:482
  32.9 0.8 %collective-permute-start.9 = (f32[3,16,256]{2,1,0:T(8,128)S(1)}, f32[3,16,256]{2,1,0:T(8,128)S(1)}, u32[]{:S(2)}, u32[]{:S(2)}) collective-permute-start(f32[3,16,256]{2,1,0:T(8,128)S(1)} %get-tuple-element.76), channel_id=1, source_target_pairs={{0,8},{8,16},{16,24},{24,0},{1,9},{9,17},{17,25},{25,1},{2,10},{10... | collective-permute-start | bytes 147464 | tf_op jit(solution)/shard_map/ppermute | solution.py:482
  33.7 0.1 most.1
  33.8 1.2 %collective-permute-start.6 = (f32[3,16,256]{2,1,0:T(8,128)S(1)}, f32[3,16,256]{2,1,0:T(8,128)S(1)}, u32[]{:S(2)}, u32[]{:S(2)}) collective-permute-start(f32[3,16,256]{2,1,0:T(8,128)S(1)} %get-tuple-element.72), channel_id=1, source_target_pairs={{0,8},{8,16},{16,24},{24,0},{1,9},{9,17},{17,25},{25,1},{2,10},{10... | collective-permute-start | bytes 147464 | tf_op jit(solution)/shard_map/ppermute | solution.py:482
  35.0 1.5 %collective-permute-start.7 = (f32[3,16,256]{2,1,0:T(8,128)S(1)}, f32[3,16,256]{2,1,0:T(8,128)S(1)}, u32[]{:S(2)}, u32[]{:S(2)}) collective-permute-start(f32[3,16,256]{2,1,0:T(8,128)S(1)} %get-tuple-element.73), channel_id=1, source_target_pairs={{0,16},{8,24},{16,0},{24,8},{1,17},{9,25},{17,1},{25,9},{2,18},{10... | collective-permute-start | bytes 147464 | tf_op jit(solution)/shard_map/ppermute | solution.py:482
  36.5 0.0 collective-permute-done.10.pieces_and_rest_6_
  36.5 0.5 %collective-permute-start.8 = (f32[3,16,256]{2,1,0:T(8,128)S(1)}, f32[3,16,256]{2,1,0:T(8,128)S(1)}, u32[]{:S(2)}, u32[]{:S(2)}) collective-permute-start(f32[3,16,256]{2,1,0:T(8,128)S(1)} %get-tuple-element.74), channel_id=1, source_target_pairs={{0,24},{8,0},{16,8},{24,16},{1,25},{9,1},{17,9},{25,17},{2,26},{10... | collective-permute-start | bytes 147464 | tf_op jit(solution)/shard_map/ppermute | solution.py:482
  37.1 1.1 %place.1 = (f32[16,32,1024]{2,1,0:T(8,128)}, f32[16,32,1024]{2,1,0:T(8,128)}) custom-call(f32[2,2,32,1024]{3,2,1,0:T(8,128)S(1)} %get-tuple-element.60.ring, f32[2,2,16,1024]{3,2,1,0:T(8,128)S(1)} %get-tuple-element.63.inner, f32[2,2,16,1024]{3,2,1,0:T(8,128)S(1)} %get-tuple-element.66.outer, ...), custom_call_target="tpu_custom_call", output_to_operand_aliasing={{0}: (3, {}), {1}: (4, {})} | custom-call | flops 4194304 | bytes 65536 | tf_op jit(solution)/shard_map/place/pallas_call | solution.py:616
  38.1 0.0 collective-permute-done.11.pieces_and_rest_7_
  38.2 0.0 collective-permute-done.9.pieces_and_rest_5_
  38.2 1.2 %collective-permute-done.6.pieces_and_rest_1_ = f32[3,16,256]{2,1,0:T(8,128)S(1)} collective-permute-done((f32[3,16,256]{2,1,0:T(8,128)S(1)}, f32[3,16,256]{2,1,0:T(8,128)S(1)}, u32[]{:S(2)}, u32[]{:S(2)}) %collective-permute-start.6) | collective-permute-done | bytes 49184 | tf_op jit(solution)/shard_map/ppermute | solution.py:482
  39.4 0.6 %collective-permute-done.7.pieces_and_rest_2_ = f32[3,16,256]{2,1,0:T(8,128)S(1)} collective-permute-done((f32[3,16,256]{2,1,0:T(8,128)S(1)}, f32[3,16,256]{2,1,0:T(8,128)S(1)}, u32[]{:S(2)}, u32[]{:S(2)}) %collective-permute-start.7) | collective-permute-done | bytes 49184 | tf_op jit(solution)/shard_map/ppermute | solution.py:482
  40.0 0.6 %collective-permute-done.8.pieces_and_rest_3_ = f32[3,16,256]{2,1,0:T(8,128)S(1)} collective-permute-done((f32[3,16,256]{2,1,0:T(8,128)S(1)}, f32[3,16,256]{2,1,0:T(8,128)S(1)}, u32[]{:S(2)}, u32[]{:S(2)}) %collective-permute-start.8) | collective-permute-done | bytes 49184 | tf_op jit(solution)/shard_map/ppermute | solution.py:482
  40.6 0.7 %shade.1 = f32[4,32,256]{2,1,0:T(8,128)} custom-call(f32[8,8,128]{2,1,0:T(8,128)S(1)} %scalars.1.values, f32[3,16,256]{2,1,0:T(8,128)S(1)} %get-tuple-element.71.pieces_and_rest_0_, f32[3,16,256]{2,1,0:T(8,128)S(1)} %collective-permute-done.6.pieces_and_rest_1_, f32[3,16,256]{2,1,0:T(8,128)S(1)} %collective-permute-done.7.pieces_and_rest_2_, ...), custom_call_target="tpu_custom_call" | custom-call | flops 1048576 | bytes 65536 | tf_op jit(solution)/shard_map/shade/pallas_call | solution.py:628
  (1 shorter events, 0.0 us)
Async XLA Ops:
  0.6 5.8 %copy-start = (f32[16,32,1024]{2,1,0:T(8,128)S(1)}, f32[16,32,1024]{2,1,0:T(8,128)}, u32[]{:S(2)}) copy-start(f32[16,32,1024]{2,1,0:T(8,128)} %sub.5) | copy-start | bytes 6291460
  0.6 5.8 %copy-start.1 = (f32[16,32,1024]{2,1,0:T(8,128)S(1)}, f32[16,32,1024]{2,1,0:T(8,128)}, u32[]{:S(2)}) copy-start(f32[16,32,1024]{2,1,0:T(8,128)} %cat.5) | copy-start | bytes 6291460
  2.4 26.2 %collective-permute-start = (f32[2,48,1024]{2,1,0:T(8,128)S(1)}, f32[2,48,1024]{2,1,0:T(8,128)S(1)}, u32[]{:S(2)}, u32[]{:S(2)}) collective-permute-start(f32[2,48,1024]{2,1,0:T(8,128)S(1)} %get-tuple-element.41.up), channel_id=1, source_target_pairs={{0,8},{8,16},{16,24},{24,0},{1,9},{9,17},{17,25},{25,1},{2,10},{10... | collective-permute-start | bytes 1179656 | tf_op jit(solution)/shard_map/ppermute | solution.py:482
  5.4 23.2 %collective-permute-start.1 = (f32[2,48,1024]{2,1,0:T(8,128)S(1)}, f32[2,48,1024]{2,1,0:T(8,128)S(1)}, u32[]{:S(2)}, u32[]{:S(2)}) collective-permute-start(f32[2,48,1024]{2,1,0:T(8,128)S(1)} %get-tuple-element.42.down), channel_id=1, source_target_pairs={{0,24},{8,0},{16,8},{24,16},{1,25},{9,1},{17,9},{25,17},{2,26},{10... | collective-permute-start | bytes 1179656 | tf_op jit(solution)/shard_map/ppermute | solution.py:482
  6.4 11.6 %copy-start.2 = (f32[3,2]{0,1:T(2,128)S(1)}, f32[3,2]{0,1:T(2,128)}, u32[]{:S(2)}) copy-start(f32[3,2]{0,1:T(2,128)} %param.7) | copy-start | bytes 76
  6.4 11.6 %copy-start.3 = (f32[2]{0:T(128)S(1)}, f32[2]{0:T(128)}, u32[]{:S(2)}) copy-start(f32[2]{0:T(128)} %scale.1) | copy-start | bytes 28
  6.7 7.9 %collective-permute-start.2 = (f32[2,2,16,1024]{3,2,1,0:T(8,128)S(1)}, f32[2,2,16,1024]{3,2,1,0:T(8,128)S(1)}, u32[]{:S(2)}, u32[]{:S(2)}) collective-permute-start(f32[2,2,16,1024]{3,2,1,0:T(8,128)S(1)} %get-tuple-element.47.own_high), channel_id=1, source_target_pairs={{0,1},{1,2},{2,3},{3,4},{4,5},{5,6},{6,7},{7,0},{8,9},{9,10},{10,1... | collective-permute-start | bytes 786440 | tf_op jit(solution)/shard_map/ppermute | solution.py:482
  6.8 8.1 %collective-permute-start.3 = (f32[2,2,16,1024]{3,2,1,0:T(8,128)S(1)}, f32[2,2,16,1024]{3,2,1,0:T(8,128)S(1)}, u32[]{:S(2)}, u32[]{:S(2)}) collective-permute-start(f32[2,2,16,1024]{3,2,1,0:T(8,128)S(1)} %get-tuple-element.48.own_low), channel_id=1, source_target_pairs={{0,7},{1,0},{2,1},{3,2},{4,3},{5,4},{6,5},{7,6},{8,15},{9,8},{10,9... | collective-permute-start | bytes 786440 | tf_op jit(solution)/shard_map/ppermute | solution.py:482
  15.0 14.4 %collective-permute-start.4 = (f32[2,16,1024]{2,1,0:T(8,128)S(1)}, f32[2,16,1024]{2,1,0:T(8,128)S(1)}, u32[]{:S(2)}, u32[]{:S(2)}) collective-permute-start(f32[2,16,1024]{2,1,0:T(8,128)S(1)} %get-tuple-element.64), channel_id=1, source_target_pairs={{0,8},{8,16},{16,24},{24,0},{1,9},{9,17},{17,25},{25,1},{2,10},{10... | collective-permute-start | bytes 393224 | tf_op jit(solution)/shard_map/ppermute | solution.py:482
  16.2 13.5 %collective-permute-start.5 = (f32[2,16,1024]{2,1,0:T(8,128)S(1)}, f32[2,16,1024]{2,1,0:T(8,128)S(1)}, u32[]{:S(2)}, u32[]{:S(2)}) collective-permute-start(f32[2,16,1024]{2,1,0:T(8,128)S(1)} %get-tuple-element.65), channel_id=1, source_target_pairs={{0,24},{8,0},{16,8},{24,16},{1,25},{9,1},{17,9},{25,17},{2,26},{10... | collective-permute-start | bytes 393224 | tf_op jit(solution)/shard_map/ppermute | solution.py:482
  29.9 6.7 %collective-permute-start.10 = (f32[3,16,256]{2,1,0:T(8,128)S(1)}, f32[3,16,256]{2,1,0:T(8,128)S(1)}, u32[]{:S(2)}, u32[]{:S(2)}) collective-permute-start(f32[3,16,256]{2,1,0:T(8,128)S(1)} %get-tuple-element.77), channel_id=1, source_target_pairs={{0,16},{8,24},{16,0},{24,8},{1,17},{9,25},{17,1},{25,9},{2,18},{10... | collective-permute-start | bytes 147464 | tf_op jit(solution)/shard_map/ppermute | solution.py:482
  31.7 6.5 %collective-permute-start.11 = (f32[3,16,256]{2,1,0:T(8,128)S(1)}, f32[3,16,256]{2,1,0:T(8,128)S(1)}, u32[]{:S(2)}, u32[]{:S(2)}) collective-permute-start(f32[3,16,256]{2,1,0:T(8,128)S(1)} %get-tuple-element.78), channel_id=1, source_target_pairs={{0,24},{8,0},{16,8},{24,16},{1,25},{9,1},{17,9},{25,17},{2,26},{10... | collective-permute-start | bytes 147464 | tf_op jit(solution)/shard_map/ppermute | solution.py:482
  32.9 5.3 %collective-permute-start.9 = (f32[3,16,256]{2,1,0:T(8,128)S(1)}, f32[3,16,256]{2,1,0:T(8,128)S(1)}, u32[]{:S(2)}, u32[]{:S(2)}) collective-permute-start(f32[3,16,256]{2,1,0:T(8,128)S(1)} %get-tuple-element.76), channel_id=1, source_target_pairs={{0,8},{8,16},{16,24},{24,0},{1,9},{9,17},{17,25},{25,1},{2,10},{10... | collective-permute-start | bytes 147464 | tf_op jit(solution)/shard_map/ppermute | solution.py:482
  33.8 5.6 %collective-permute-start.6 = (f32[3,16,256]{2,1,0:T(8,128)S(1)}, f32[3,16,256]{2,1,0:T(8,128)S(1)}, u32[]{:S(2)}, u32[]{:S(2)}) collective-permute-start(f32[3,16,256]{2,1,0:T(8,128)S(1)} %get-tuple-element.72), channel_id=1, source_target_pairs={{0,8},{8,16},{16,24},{24,0},{1,9},{9,17},{17,25},{25,1},{2,10},{10... | collective-permute-start | bytes 147464 | tf_op jit(solution)/shard_map/ppermute | solution.py:482
  35.0 5.0 %collective-permute-start.7 = (f32[3,16,256]{2,1,0:T(8,128)S(1)}, f32[3,16,256]{2,1,0:T(8,128)S(1)}, u32[]{:S(2)}, u32[]{:S(2)}) collective-permute-start(f32[3,16,256]{2,1,0:T(8,128)S(1)} %get-tuple-element.73), channel_id=1, source_target_pairs={{0,16},{8,24},{16,0},{24,8},{1,17},{9,25},{17,1},{25,9},{2,18},{10... | collective-permute-start | bytes 147464 | tf_op jit(solution)/shard_map/ppermute | solution.py:482
  36.5 4.1 %collective-permute-start.8 = (f32[3,16,256]{2,1,0:T(8,128)S(1)}, f32[3,16,256]{2,1,0:T(8,128)S(1)}, u32[]{:S(2)}, u32[]{:S(2)}) collective-permute-start(f32[3,16,256]{2,1,0:T(8,128)S(1)} %get-tuple-element.74), channel_id=1, source_target_pairs={{0,24},{8,0},{16,8},{24,16},{1,25},{9,1},{17,9},{25,17},{2,26},{10... | collective-permute-start | bytes 147464 | tf_op jit(solution)/shard_map/ppermute | solution.py:482

commit v5 on v4

--- a/solution.py
+++ b/solution.py
@@ -63,58 +63,40 @@
     return tile[:, :columns] if columns <= LANES else jnp.concatenate([tile] * (columns // LANES), axis=1)
 
 
-def outer_step(outer, inner, rows, only, store):
-    plane_step(
-        lambda s, tile: outer[s, span(tile), :],
-        rows // ROWS,
-        None,
-        None,
-        lambda s, tile: inner[s, span(tile), :],
-        store,
-        only,
-    )
-
-
-def planes_kernel(sub, cat, up, down, second, penult, sems):
-    depth, rows, _ = sub.shape
+def planes_kernel(sub, cat, up, down, sems):
+    depth = sub.shape[0]
     copies = []
-    for s, field in enumerate((sub, cat)):
-        for plane, out in (
-            (depth - 1, up.at[s, pl.ds(0, rows)]),
-            (depth - 2, penult.at[s]),
-            (0, down.at[s, pl.ds(0, rows)]),
-            (1, second.at[s]),
-        ):
-            copies.append(pltpu.make_async_copy(field.at[plane], out, sems.at[len(copies)]))
+    for out, plane in ((up, depth - 1), (down, 0)):
+        for s, field in enumerate((sub, cat)):
+            copies.append(pltpu.make_async_copy(field.at[plane], out.at[s], sems.at[len(copies)]))
     for copy in copies:
         copy.start()
     for copy in copies:
         copy.wait()
-    for outer, inner in ((up, penult), (down, second)):
-
-        def store(tile, sub_new, cat_new, outer=outer):
-            at = pl.ds(rows + (tile - 1) * ROWS, ROWS)
-            outer[0, at, :] = sub_new
-            outer[1, at, :] = cat_new
-
-        outer_step(outer, inner, rows, range(1, rows // ROWS - 1), store)
-
-
-def prepare_kernel(sub, cat, up, down, second, penult, low, high, q_up, q_down):
+
+
+def prepare_kernel(sub, cat, low, high, q_up, q_down):
     depth, rows, _ = sub.shape
-    for s, field in enumerate((sub, cat)):
+    fields = (sub, cat)
+    for s, field in enumerate(fields):
         for plane in range(depth):
             for row in range(2):
                 low[s, row, plane : plane + 1] = field[plane, row : row + 1]
                 high[s, row, plane : plane + 1] = field[plane, rows - 2 + row : rows - 1 + row]
-    for outer, inner, out in ((up, penult, q_up), (down, second, q_down)):
+    for outer, inner, out in ((depth - 1, depth - 2, q_up), (0, 1, q_down)):
 
         def store(tile, sub_new, cat_new, out=out):
-            at = span(0 if tile == 0 else 1)
-            out[0, at, :] = sub_new
-            out[1, at, :] = cat_new
-
-        outer_step(outer, inner, rows, (0, rows // ROWS - 1), store)
+            out[0, span(tile), :] = sub_new
+            out[1, span(tile), :] = cat_new
+
+        plane_step(
+            lambda s, tile, outer=outer: fields[s][outer, span(tile), :],
+            rows // ROWS,
+            None,
+            None,
+            lambda s, tile, inner=inner: fields[s][inner, span(tile), :],
+            store,
+        )
 
 
 def composite(sub, cat, scale_sub, scale_cat, clear):
@@ -208,7 +190,7 @@
 
 
 def second_kernel(
-    values, mid, up, down, q_up, q_down, from_low, from_high, own_low, own_high, center, sub_in, cat_in,
+    values, mid, q_up, q_down, from_low, from_high, own_low, own_high, center, sub_in, cat_in,
     sub_out, cat_out, seen, near, far, rows_low, rows_high,
     heads, tails, new, sem_out,
 ):
@@ -263,11 +245,7 @@
 
     for s in range(2):
         for tile in range(tiles):
-            if 0 < tile < tiles - 1:
-                at = pl.ds(rows + (tile - 1) * ROWS, ROWS)
-                first, last = down[s, at, :], up[s, at, :]
-            else:
-                first, last = q_down[s, span(1 if tile else 0), :], q_up[s, span(1 if tile else 0), :]
+            first, last = q_down[s, span(tile), :], q_up[s, span(tile), :]
             if tile == 0:
                 first, last = with_low(s, 0, first), with_low(s, depth - 1, last)
             if tile == tiles - 1:
@@ -313,13 +291,20 @@
 
 def rows_kernel(q_up, q_down, from_low, from_high, up, down):
     depth = from_low.shape[2]
+    tiles = q_up.shape[1] // ROWS
     for plane, q, out in ((depth - 1, q_up, up), (0, q_down, down)):
-        for place, edge, source in ((0, 0, from_low.at[:, 1]), (1, ROWS - 1, from_high.at[:, 0])):
-            for s in range(2):
-                tile = q[s, span(place), :]
-                index = lax.broadcasted_iota(jnp.int32, tile.shape, 0)
-                row = jnp.broadcast_to(source[s, plane : plane + 1], tile.shape)
-                out[s, span(place), :] = tile + jnp.where(index == edge, (2.0 * RATES[s]) * row, 0.0)
+        for s in range(2):
+            for tile in range(tiles):
+                value = q[s, span(tile), :]
+                index = lax.broadcasted_iota(jnp.int32, value.shape, 0)
+                for at, edge, row in (
+                    (0, 0, from_low[s, 1, plane : plane + 1]),
+                    (tiles - 1, ROWS - 1, from_high[s, 0, plane : plane + 1]),
+                ):
+                    if tile == at:
+                        beside = jnp.broadcast_to((2.0 * RATES[s]) * row, value.shape)
+                        value = value + jnp.where(index == edge, beside, 0.0)
+                out[s, span(tile), :] = value
 
 
 def rim_kernel(
@@ -334,7 +319,7 @@
         zero, one, two = (0, 1, 2) if side == 0 else (2, 1, 0)
         outer, beside = (0, 1) if side == 0 else (depth - 1, depth - 2)
         for s in range(2):
-            mid[side, s] = inside[s, zero] + RATES[s] * p[s, :rows]
+            mid[side, s] = inside[s, zero] + RATES[s] * p[s]
 
         def store_known(tile, sub, cat, side=side, own=own):
             at = span(tile)
@@ -376,33 +361,39 @@
         seen[2, at, :] = clear
 
 
-def last_kernel(outermost, values, known, q_low, q_high, seen, *rest):
+def partner(index, shift, count):
+    return index ^ shift if count & (count - 1) == 0 else (index + shift) % count
+
+
+def origin(index, shift, count):
+    return index ^ shift if count & (count - 1) == 0 else (index + count - shift) % count
+
+
+def last_kernel(values, known, q_low, q_high, seen, *rest):
     *pieces, outer, whole = rest
     rows, columns = seen.shape[1:]
     count = len(pieces)
     wide = columns // count
-    tiles = rows // ROWS
-    scale_sub, scale_cat = across_columns(values[0], columns), across_columns(values[1], columns)
-    for place, tile in enumerate((0, tiles - 1) if outermost else range(1, tiles - 1)):
-        at, to = span(tile), span(place)
-        source = to if outermost else pl.ds(rows + place * ROWS, ROWS)
+    scales = across_columns(values[0], columns), across_columns(values[1], columns)
+    for tile in range(rows // ROWS):
+        at = span(tile)
         planes = []
         for side, q in enumerate((q_low, q_high)):
             for s in range(2):
-                value = known[side, s, at, :] + RATES[s] * q[s, source, :]
-                outer[s, side, to, :] = value
+                value = known[side, s, at, :] + RATES[s] * q[s, at, :]
+                outer[s, side, at, :] = value
                 planes.append(value)
-        one, two, clear = composite(planes[0], planes[1], scale_sub, scale_cat, 1.0)
+        one, two, clear = composite(planes[0], planes[1], *scales, 1.0)
         sub = one + clear * seen[0, at, :]
         cat = two + clear * seen[1, at, :]
         clear = clear * seen[2, at, :]
-        one, two, clear = composite(planes[2], planes[3], scale_sub, scale_cat, clear)
-        whole[0, to, :] = sub + one
-        whole[1, to, :] = cat + two
-        whole[2, to, :] = clear
+        one, two, clear = composite(planes[2], planes[3], *scales, clear)
+        whole[0, at, :] = sub + one
+        whole[1, at, :] = cat + two
+        whole[2, at, :] = clear
     me = lax.axis_index("gz")
     for shift, piece in enumerate(pieces):
-        target = lax.rem(me + shift, count)
+        target = partner(me, shift, count)
         if wide % LANES == 0:
             piece[...] = whole[:, :, pl.ds(pl.multiple_of(target * wide, LANES), wide)]
         else:
@@ -415,15 +406,11 @@
 
 def shade_kernel(values, *pieces_and_rest):
     *pieces, image, slabs = pieces_and_rest
-    count = len(pieces) // 2
+    count = len(pieces)
     rows, wide = image.shape[1:]
     me = lax.axis_index("gz")
-    for shift in range(count):
-        slab = lax.rem(me + count - shift, count)
-        inner, outer = pieces[shift], pieces[count + shift]
-        slabs[slab, :, pl.ds(ROWS, rows - 2 * ROWS), :] = inner[...]
-        slabs[slab, :, pl.ds(0, ROWS), :] = outer[:, :ROWS]
-        slabs[slab, :, pl.ds(rows - ROWS, ROWS), :] = outer[:, ROWS:]
+    for shift, piece in enumerate(pieces):
+        slabs[origin(me, shift, count)] = piece[...]
     for tile in range(rows // ROWS):
         at = span(tile)
         sub, cat, clear = slabs[0, 0, at, :], slabs[0, 1, at, :], slabs[0, 2, at, :]
@@ -438,20 +425,14 @@
         image[3, at, :] = 1.0 - clear
 
 
-def place_kernel(ring, inner, outer, sub_in, cat_in, sub_out, cat_out, sems):
+def place_kernel(ring, outer, sub_in, cat_in, sub_out, cat_out, sems):
     del sub_in, cat_in
-    depth, rows, _ = sub_out.shape
+    depth = sub_out.shape[0]
     copies = []
     for s, out in enumerate((sub_out, cat_out)):
         for side in range(2):
-            plane = side * (depth - 1)
-            for source, target in (
-                (ring.at[s, side], out.at[1 + side * (depth - 3)]),
-                (inner.at[s, side], out.at[plane, pl.ds(ROWS, rows - 2 * ROWS)]),
-                (outer.at[s, side, pl.ds(0, ROWS)], out.at[plane, pl.ds(0, ROWS)]),
-                (outer.at[s, side, pl.ds(ROWS, ROWS)], out.at[plane, pl.ds(rows - ROWS, ROWS)]),
-            ):
-                copies.append(pltpu.make_async_copy(source, target, sems.at[len(copies)]))
+            for at, source in ((side * (depth - 1), outer), (1 + side * (depth - 3), ring)):
+                copies.append(pltpu.make_async_copy(source.at[s, side], out.at[at], sems.at[len(copies)]))
     for copy in copies:
         copy.start()
     for copy in copies:
@@ -473,7 +454,6 @@
     wide = columns // count
     share = OPTICAL / (depth * count)
     middle = rows - 2 * ROWS
-    outers = 2 * ROWS
 
     def ring(size, shift):
         return [(i, (i + shift) % size) for i in range(size)]
@@ -481,15 +461,15 @@
     def shifted(x, axis, shift):
         return lax.ppermute(x, axis, ring(lax.axis_size(axis), shift))
 
-    up, down, second, penult = call(
+    up, down = call(
         planes_kernel,
         1 << 20,
         2,
         name="planes",
-        out_shape=(f32(2, rows + middle, columns),) * 2 + (f32(2, rows, columns),) * 2,
+        out_shape=(f32(2, rows, columns),) * 2,
         in_specs=[HBM, HBM],
-        out_specs=(VMEM,) * 4,
-        scratch_shapes=[pltpu.SemaphoreType.DMA((8,))],
+        out_specs=(VMEM,) * 2,
+        scratch_shapes=[pltpu.SemaphoreType.DMA((4,))],
     )(hbm(substrate), hbm(catalyst))
     p_low = shifted(up, "gz", 1)
     p_high = shifted(down, "gz", -1)
@@ -499,15 +479,10 @@
         1 << 22,
         2,
         name="prepare",
-        out_shape=(
-            f32(2, 2, depth, columns),
-            f32(2, 2, depth, columns),
-            f32(2, outers, columns),
-            f32(2, outers, columns),
-        ),
-        in_specs=[VMEM] * 6,
+        out_shape=(f32(2, 2, depth, columns),) * 2 + (f32(2, rows, columns),) * 2,
+        in_specs=[VMEM] * 2,
         out_specs=(VMEM,) * 4,
-    )(substrate, catalyst, up, down, second, penult)
+    )(substrate, catalyst)
     from_low = shifted(own_high, "gx", 1)
     from_high = shifted(own_low, "gx", -1)
 
@@ -549,7 +524,7 @@
         1 << 18,
         2,
         name="rows",
-        out_shape=(f32(2, outers, columns),) * 2,
+        out_shape=(f32(2, rows, columns),) * 2,
         in_specs=[VMEM] * 4,
         out_specs=(VMEM,) * 2,
     )(q_up, q_down, from_low, from_high)
@@ -570,16 +545,16 @@
             f32(2, depth, columns),
             f32(2, depth, columns),
         ),
-        in_specs=[VMEM] * 11 + [HBM, HBM],
+        in_specs=[VMEM] * 9 + [HBM, HBM],
         out_specs=(HBM, HBM) + (VMEM,) * 5,
-        input_output_aliases={11: 0, 12: 1},
+        input_output_aliases={9: 0, 10: 1},
         scratch_shapes=[
             pltpu.VMEM((2, depth, ROWS, columns), jnp.float32),
             pltpu.VMEM((2, depth, ROWS, columns), jnp.float32),
             pltpu.VMEM((2, 2, depth, ROWS, columns), jnp.float32),
             pltpu.SemaphoreType.DMA((2, 2, depth)),
         ],
-    )(values, mid, up, down, q_up, q_down, from_low, from_high, own_low, own_high, center, sub_part, cat_part)
+    )(values, mid, q_up, q_down, from_low, from_high, own_low, own_high, center, sub_part, cat_part)
 
     p_low, p_high, inner = lax.optimization_barrier((p_low, p_high, inner))
     ring_planes, known, seen = call(
@@ -593,25 +568,21 @@
         scratch_shapes=[pltpu.VMEM((2, 2, rows, columns), jnp.float32)],
     )(values, p_low, p_high, down, up, near, far, rows_low, rows_high, inner)
 
-    def finish(outermost, high, *args):
-        *pieces, outer = call(
-            functools.partial(last_kernel, outermost),
-            1 << 22,
-            4,
-            name="last" if outermost else "most",
-            out_shape=(f32(3, high, wide),) * count + (f32(2, 2, high, columns),),
-            in_specs=[VMEM] * len(args),
-            out_specs=(VMEM,) * (count + 1),
-            scratch_shapes=[pltpu.VMEM((3, high, columns), jnp.float32)],
-        )(*args)
-        received = [pieces[0]]
-        for shift in range(1, count):
-            received.append(shifted(pieces[shift], "gz", shift))
-        return received, outer
-
-    inner_pieces, inner_rows = finish(False, middle, values, known, p_low, p_high, seen)
-
-    outer_pieces, outer_rows = finish(True, outers, values, known, q_low, q_high, seen)
+    *pieces, outer = call(
+        last_kernel,
+        1 << 22,
+        4,
+        name="last",
+        out_shape=(f32(3, rows, wide),) * count + (f32(2, 2, rows, columns),),
+        in_specs=[VMEM] * 5,
+        out_specs=(VMEM,) * (count + 1),
+        scratch_shapes=[pltpu.VMEM((3, rows, columns), jnp.float32)],
+    )(values, known, q_low, q_high, seen)
+
+    received = [pieces[0]] * count
+    for shift in piece_order(count):
+        pairs = [(i, int(partner(i, shift, count))) for i in range(count)]
+        received[shift] = lax.ppermute(pieces[shift], "gz", pairs)
 
     sub_final, cat_final = call(
         place_kernel,
@@ -619,11 +590,11 @@
         2,
         name="place",
         out_shape=(f32(depth, rows, columns), f32(depth, rows, columns)),
-        in_specs=[VMEM, VMEM, VMEM, HBM, HBM],
+        in_specs=[VMEM, VMEM, HBM, HBM],
         out_specs=(HBM, HBM),
-        input_output_aliases={3: 0, 4: 1},
-        scratch_shapes=[pltpu.SemaphoreType.DMA((16,))],
-    )(ring_planes, inner_rows, outer_rows, sub_part, cat_part)
+        input_output_aliases={2: 0, 3: 1},
+        scratch_shapes=[pltpu.SemaphoreType.DMA((8,))],
+    )(ring_planes, outer, sub_part, cat_part)
 
     image = call(
         shade_kernel,
@@ -631,11 +602,16 @@
         4,
         name="shade",
         out_shape=f32(4, rows, wide),
-        in_specs=[VMEM] * (1 + 2 * count),
+        in_specs=[VMEM] * (1 + count),
         out_specs=VMEM,
         scratch_shapes=[pltpu.VMEM((count, 3, rows, wide), jnp.float32)],
-    )(values, *inner_pieces, *outer_pieces)
+    )(values, *received)
     return sub_final, cat_final, image
+
+
+def piece_order(count):
+    half = count // 2
+    return [half] + [shift for shift in range(count - 1, 0, -1) if shift != half]
 
 
 def solution(mesh):

time: 41.5 us -> 43.7 us (1.053)
  starting transfers between devices: 17.7 us -> 14.3 us
  local copies, waits for them, and re-layouts: 0.02 us -> 3.19 us
  waiting for transfers between devices: 7.41 us -> 10.3 us
  Pallas kernels: 15.4 us -> 14.9 us
    ppermute x12 -> x6, starting transfers between devices: 17.7 us -> 10.7 us  [shifted(): return lax.ppermute(x, axis, ring(lax.axis_size(axis), shift))]
    ppermute x0 -> x3, starting transfers between devices: none -> 3.55 us  [body(): received[shift] = lax.ppermute(pieces[shift], 'gz', pairs)]
    unnamed x8 -> x12, local copies, waits for them, and re-layouts: 0.02 us -> 3.19 us
    ppermute x0 -> x3, waiting for transfers between devices: none -> 3 us  [body(): received[shift] = lax.ppermute(pieces[shift], 'gz', pairs)]
    pallas_call x4 -> x3, Pallas kernels: 1.96 us -> 1.38 us  [the longest x1 1.13 us: body(): call(planes_kernel, 1 << 20, 2, name='planes', out_shape=(f32(2, rows, co...]
    ppermute x12 -> x6, waiting for transfers between devices: 7.41 us -> 7.3 us  [shifted(): return lax.ppermute(x, axis, ring(lax.axis_size(axis), shift))]
  transfers between devices with their start and end apart: 12 -> 9, of which waited for: 6 -> 6; matrix products, arithmetic and copies ran while one was open for 0% -> 0% of each run, Pallas kernels for 31% -> 31%
where the time goes in v5:
time: 43.7 us; the launch traced here: 43.5 us
  Pallas kernels  14.9 us (34%)
  starting transfers between devices  14.3 us (33%)
  waiting for transfers between devices  10.3 us (24%)
  local copies, waits for them, and re-layouts  3.19 us (7%)
  between operations  0.75 us (2%)
    ppermute x6, starting transfers between devices, shifted(): return lax.ppermute(x, axis, ring(lax.axis_size(axis), shift))  10.7 us
    ppermute x6, waiting for transfers between devices, shifted(): return lax.ppermute(x, axis, ring(lax.axis_size(axis), shift))  7.3 us
    pallas_call x1, Pallas kernels, body(): call(second_kernel, 1 << 25, 10, name='second', out_shape=(f32(depth, row...  4.01 us
    ppermute x3, starting transfers between devices, body(): received[shift] = lax.ppermute(pieces[shift], 'gz', pairs)  3.55 us
    unnamed x12, local copies, waits for them, and re-layouts  3.19 us
    ppermute x3, waiting for transfers between devices, body(): received[shift] = lax.ppermute(pieces[shift], 'gz', pairs)  3 us
    pallas_call x1, Pallas kernels, body(): call(center_kernel, 1 << 24, 4, name='center', out_shape=(f32(depth, rows...  2.98 us
    pallas_call x1, Pallas kernels, body(): call(first_kernel, 1 << 24, 2, name='first', out_shape=f32(2, depth, rows...  2.95 us
  transfers between devices with their start and end apart: 9, of which 6 were waited for; matrix products, arithmetic and copies ran while one was open for 0% of the time, Pallas kernels for 31%

profile of v5, /device:TPU:0, one launch (start us, length us, event | category | flops | bytes accessed | tf_op | source)
XLA Modules:
  0.0 43.5 jit_solution(4156341446296705275)
XLA Ops:
  0.6 0.0 copy-start
  0.6 1.6 %copy-done = f32[16,32,1024]{2,1,0:T(8,128)S(1)} copy-done((f32[16,32,1024]{2,1,0:T(8,128)S(1)}, f32[16,32,1024]{2,1,0:T(8,128)}, u32[]{:S(2)}) %copy-start) | copy-done | bytes 2097176
  2.2 0.0 copy-start.2
  2.2 1.6 %copy-done.2 = f32[16,32,1024]{2,1,0:T(8,128)S(1)} copy-done((f32[16,32,1024]{2,1,0:T(8,128)S(1)}, f32[16,32,1024]{2,1,0:T(8,128)}, u32[]{:S(2)}) %copy-start.2) | copy-done | bytes 2097176
  3.8 0.5 %prepare.1 = (f32[2,2,16,1024]{3,2,1,0:T(8,128)S(1)}, f32[2,2,16,1024]{3,2,1,0:T(8,128)S(1)}, f32[2,32,1024]{2,1,0:T(8,128)S(1)}, f32[2,32,1024]{2,1,0:T(8,128)S(1)}) custom-call(f32[16,32,1024]{2,1,0:T(8,128)S(1)} %copy-done, f32[16,32,1024]{2,1,0:T(8,128)S(1)} %copy-done.2), custom_call_target="tpu_custom_call" | custom-call | flops 4194304 | bytes 65536 | tf_op jit(solution)/shard_map/prepare/pallas_call | solution.py:477
  4.3 0.5 %collective-permute-start.2 = (f32[2,2,16,1024]{3,2,1,0:T(8,128)S(1)}, f32[2,2,16,1024]{3,2,1,0:T(8,128)S(1)}, u32[]{:S(2)}, u32[]{:S(2)}) collective-permute-start(f32[2,2,16,1024]{3,2,1,0:T(8,128)S(1)} %get-tuple-element.38.own_high), channel_id=1, source_target_pairs={{0,1},{1,2},{2,3},{3,4},{4,5},{5,6},{6,7},{7,0},{8,9},{9,10},{10,1... | collective-permute-start | bytes 786440 | tf_op jit(solution)/shard_map/ppermute | solution.py:462
  4.8 0.0 copy-start.4
  4.8 0.0 copy-start.5
  4.8 0.0 copy-start.1
  4.8 0.0 copy-start.3
  4.8 4.1 %collective-permute-start.3 = (f32[2,2,16,1024]{3,2,1,0:T(8,128)S(1)}, f32[2,2,16,1024]{3,2,1,0:T(8,128)S(1)}, u32[]{:S(2)}, u32[]{:S(2)}) collective-permute-start(f32[2,2,16,1024]{3,2,1,0:T(8,128)S(1)} %get-tuple-element.39.own_low), channel_id=1, source_target_pairs={{0,7},{1,0},{2,1},{3,2},{4,3},{5,4},{6,5},{7,6},{8,15},{9,8},{10,9... | collective-permute-start | bytes 786440 | tf_op jit(solution)/shard_map/ppermute | solution.py:462
  9.0 1.1 %planes.1 = (f32[2,32,1024]{2,1,0:T(8,128)S(1)}, f32[2,32,1024]{2,1,0:T(8,128)S(1)}) custom-call(f32[16,32,1024]{2,1,0:T(8,128)} %sub.5, f32[16,32,1024]{2,1,0:T(8,128)} %cat.5), custom_call_target="tpu_custom_call" | custom-call | flops 1048576 | bytes 65536 | tf_op jit(solution)/shard_map/planes/pallas_call | solution.py:464
  10.1 2.0 %collective-permute-start = (f32[2,32,1024]{2,1,0:T(8,128)S(1)}, f32[2,32,1024]{2,1,0:T(8,128)S(1)}, u32[]{:S(2)}, u32[]{:S(2)}) collective-permute-start(f32[2,32,1024]{2,1,0:T(8,128)S(1)} %get-tuple-element.34.up), channel_id=1, source_target_pairs={{0,8},{8,16},{16,24},{24,0},{1,9},{9,17},{17,25},{25,1},{2,10},{10... | collective-permute-start | bytes 786440 | tf_op jit(solution)/shard_map/ppermute | solution.py:462
  12.1 1.0 %collective-permute-start.1 = (f32[2,32,1024]{2,1,0:T(8,128)S(1)}, f32[2,32,1024]{2,1,0:T(8,128)S(1)}, u32[]{:S(2)}, u32[]{:S(2)}) collective-permute-start(f32[2,32,1024]{2,1,0:T(8,128)S(1)} %get-tuple-element.35.down), channel_id=1, source_target_pairs={{0,24},{8,0},{16,8},{24,16},{1,25},{9,1},{17,9},{25,17},{2,26},{10... | collective-permute-start | bytes 786440 | tf_op jit(solution)/shard_map/ppermute | solution.py:462
  13.1 0.0 collective-permute-done.2.from_low
  13.1 0.4 %collective-permute-done.3.from_high = f32[2,2,16,1024]{3,2,1,0:T(8,128)S(1)} collective-permute-done((f32[2,2,16,1024]{3,2,1,0:T(8,128)S(1)}, f32[2,2,16,1024]{3,2,1,0:T(8,128)S(1)}, u32[]{:S(2)}, u32[]{:S(2)}) %collective-permute-start.3) | collective-permute-done | bytes 262176 | tf_op jit(solution)/shard_map/ppermute | solution.py:462
  13.6 0.1 rows.1
  13.6 2.0 %collective-permute-start.4 = (f32[2,32,1024]{2,1,0:T(8,128)S(1)}, f32[2,32,1024]{2,1,0:T(8,128)S(1)}, u32[]{:S(2)}, u32[]{:S(2)}) collective-permute-start(f32[2,32,1024]{2,1,0:T(8,128)S(1)} %get-tuple-element.53), channel_id=1, source_target_pairs={{0,8},{8,16},{16,24},{24,0},{1,9},{9,17},{17,25},{25,1},{2,10},{10... | collective-permute-start | bytes 786440 | tf_op jit(solution)/shard_map/ppermute | solution.py:462
  15.7 1.0 %collective-permute-start.5 = (f32[2,32,1024]{2,1,0:T(8,128)S(1)}, f32[2,32,1024]{2,1,0:T(8,128)S(1)}, u32[]{:S(2)}, u32[]{:S(2)}) collective-permute-start(f32[2,32,1024]{2,1,0:T(8,128)S(1)} %get-tuple-element.54), channel_id=1, source_target_pairs={{0,24},{8,0},{16,8},{24,16},{1,25},{9,1},{17,9},{25,17},{2,26},{10... | collective-permute-start | bytes 786440 | tf_op jit(solution)/shard_map/ppermute | solution.py:462
  16.7 0.0 copy-done.4
  16.7 0.0 copy-done.5
  16.7 0.6 %scalars.1.values = f32[8,8,128]{2,1,0:T(8,128)S(1)} custom-call(f32[2]{0:T(128)S(1)} %copy-done.5, f32[2,3]{1,0:T(2,128)S(1)} %bitcast.1), custom_call_target="tpu_custom_call" | custom-call | flops 262144 | bytes 65536 | tf_op jit(solution)/shard_map/scalars/pallas_call | solution.py:498
  17.2 0.0 copy-done.1
  17.3 0.0 copy-done.3
  17.3 3.0 %first.1.mid = f32[2,16,32,1024]{3,2,1,0:T(8,128)S(1)} custom-call(f32[16,32,1024]{2,1,0:T(8,128)S(1)} %copy-done.1, f32[16,32,1024]{2,1,0:T(8,128)S(1)} %copy-done.3), custom_call_target="tpu_custom_call" | custom-call | flops 16777216 | bytes 65536 | tf_op jit(solution)/shard_map/first/pallas_call | solution.py:489
  20.2 3.0 %center.1 = (f32[16,32,1024]{2,1,0:T(8,128)}, f32[16,32,1024]{2,1,0:T(8,128)}, f32[3,32,1024]{2,1,0:T(8,128)S(1)}) custom-call(f32[8,8,128]{2,1,0:T(8,128)S(1)} %scalars.1.values, f32[2,16,32,1024]{3,2,1,0:T(8,128)S(1)} %first.1.mid), custom_call_target="tpu_custom_call" | custom-call | flops 16777216 | bytes 65536 | tf_op jit(solution)/shard_map/center/pallas_call | solution.py:508
  23.2 4.0 %second.1 = (f32[16,32,1024]{2,1,0:T(8,128)}, f32[16,32,1024]{2,1,0:T(8,128)}, f32[3,32,1024]{2,1,0:T(8,128)S(1)}, f32[2,3,32,1024]{3,2,1,0:T(8,128)S(1)}, f32[2...) custom-call(f32[8,8,128]{2,1,0:T(8,128)S(1)} %scalars.1.values, ...), custom_call_target="tpu_custom_call", output_to_operand_aliasing={{0}: (9, {}), {1}: (10, {})} | custom-call | flops 33554432 | bytes 65536 | tf_op jit(solution)/shard_map/second/pallas_call | solution.py:534
  27.2 0.0 collective-permute-done.p_low
  27.2 0.0 collective-permute-done.1.p_high
  27.3 0.8 %rim.1 = (f32[2,2,32,1024]{3,2,1,0:T(8,128)S(1)}, f32[2,2,32,1024]{3,2,1,0:T(8,128)S(1)}, f32[3,32,1024]{2,1,0:T(8,128)S(1)}) custom-call(f32[8,8,128]{2,1,0:T(8,128)S(1)} %scalars.1.values, f32[2,32,1024]{2,1,0:T(8,128)S(1)} %collective-permute-done.p_low, f32[2,32,1024]{2,1,0:T(8,128)S(1)} %collective-permute-done.1.p_high, ...), custom_call_target="tpu_custom_call" | custom-call | flops 8388608 | bytes 65536 | tf_op jit(solution)/shard_map/rim/pallas_call | solution.py:560
  28.1 3.4 %collective-permute-done.4.q_low = f32[2,32,1024]{2,1,0:T(8,128)S(1)} collective-permute-done((f32[2,32,1024]{2,1,0:T(8,128)S(1)}, f32[2,32,1024]{2,1,0:T(8,128)S(1)}, u32[]{:S(2)}, u32[]{:S(2)}) %collective-permute-start.4) | collective-permute-done | bytes 262176 | tf_op jit(solution)/shard_map/ppermute | solution.py:462
  31.5 3.5 %collective-permute-done.5.q_high = f32[2,32,1024]{2,1,0:T(8,128)S(1)} collective-permute-done((f32[2,32,1024]{2,1,0:T(8,128)S(1)}, f32[2,32,1024]{2,1,0:T(8,128)S(1)}, u32[]{:S(2)}, u32[]{:S(2)}) %collective-permute-start.5) | collective-permute-done | bytes 262176 | tf_op jit(solution)/shard_map/ppermute | solution.py:462
  34.9 0.2 last.1
  35.1 1.6 %collective-permute-start.6 = (f32[3,32,256]{2,1,0:T(8,128)S(1)}, f32[3,32,256]{2,1,0:T(8,128)S(1)}, u32[]{:S(2)}, u32[]{:S(2)}) collective-permute-start(f32[3,32,256]{2,1,0:T(8,128)S(1)} %get-tuple-element.62), channel_id=1, source_target_pairs={{0,8},{8,0},{16,24},{24,16},{1,9},{9,1},{17,25},{25,17},{2,10},{10... | collective-permute-start | bytes 294920 | tf_op jit(solution)/shard_map/ppermute | solution.py:585
  36.7 0.5 %collective-permute-start.7 = (f32[3,32,256]{2,1,0:T(8,128)S(1)}, f32[3,32,256]{2,1,0:T(8,128)S(1)}, u32[]{:S(2)}, u32[]{:S(2)}) collective-permute-start(f32[3,32,256]{2,1,0:T(8,128)S(1)} %get-tuple-element.63), channel_id=1, source_target_pairs={{0,16},{8,24},{16,0},{24,8},{1,17},{9,25},{17,1},{25,9},{2,18},{10... | collective-permute-start | bytes 294920 | tf_op jit(solution)/shard_map/ppermute | solution.py:585
  37.2 1.5 %collective-permute-start.8 = (f32[3,32,256]{2,1,0:T(8,128)S(1)}, f32[3,32,256]{2,1,0:T(8,128)S(1)}, u32[]{:S(2)}, u32[]{:S(2)}) collective-permute-start(f32[3,32,256]{2,1,0:T(8,128)S(1)} %get-tuple-element.64), channel_id=1, source_target_pairs={{0,24},{8,16},{16,8},{24,0},{1,25},{9,17},{17,9},{25,1},{2,26},{10... | collective-permute-start | bytes 294920 | tf_op jit(solution)/shard_map/ppermute | solution.py:585
  38.7 1.0 %place.1 = (f32[16,32,1024]{2,1,0:T(8,128)}, f32[16,32,1024]{2,1,0:T(8,128)}) custom-call(f32[2,2,32,1024]{3,2,1,0:T(8,128)S(1)} %get-tuple-element.51.ring, f32[2,2,32,1024]{3,2,1,0:T(8,128)S(1)} %get-tuple-element.56.outer, f32[16,32,1024]{2,1,0:T(8,128)} %get-tuple-element.57.sub_in, ...), custom_call_target="tpu_custom_call", output_to_operand_aliasing={{0}: (2, {}), {1}: (3, {})} | custom-call | flops 4194304 | bytes 65536 | tf_op jit(solution)/shard_map/place/pallas_call | solution.py:587
  39.7 0.1 collective-permute-done.6.pieces_and_rest_1_
  39.8 1.5 %collective-permute-done.7.pieces_and_rest_2_ = f32[3,32,256]{2,1,0:T(8,128)S(1)} collective-permute-done((f32[3,32,256]{2,1,0:T(8,128)S(1)}, f32[3,32,256]{2,1,0:T(8,128)S(1)}, u32[]{:S(2)}, u32[]{:S(2)}) %collective-permute-start.7) | collective-permute-done | bytes 98336 | tf_op jit(solution)/shard_map/ppermute | solution.py:585
  41.3 1.4 %collective-permute-done.8.pieces_and_rest_3_ = f32[3,32,256]{2,1,0:T(8,128)S(1)} collective-permute-done((f32[3,32,256]{2,1,0:T(8,128)S(1)}, f32[3,32,256]{2,1,0:T(8,128)S(1)}, u32[]{:S(2)}, u32[]{:S(2)}) %collective-permute-start.8) | collective-permute-done | bytes 98336 | tf_op jit(solution)/shard_map/ppermute | solution.py:585
  42.7 0.7 %shade.1 = f32[4,32,256]{2,1,0:T(8,128)} custom-call(f32[8,8,128]{2,1,0:T(8,128)S(1)} %scalars.1.values, f32[3,32,256]{2,1,0:T(8,128)S(1)} %get-tuple-element.61.pieces_and_rest_0_, f32[3,32,256]{2,1,0:T(8,128)S(1)} %collective-permute-done.6.pieces_and_rest_1_, f32[3,32,256]{2,1,0:T(8,128)S(1)} %collective-permute-done.7.pieces_and_rest_2_, ...), custom_call_target="tpu_custom_call" | custom-call | flops 1048576 | bytes 65536 | tf_op jit(solution)/shard_map/shade/pallas_call | solution.py:599
Async XLA Ops:
  0.6 1.6 %copy-start = (f32[16,32,1024]{2,1,0:T(8,128)S(1)}, f32[16,32,1024]{2,1,0:T(8,128)}, u32[]{:S(2)}) copy-start(f32[16,32,1024]{2,1,0:T(8,128)} %sub.5) | copy-start | bytes 6291460
  2.2 1.6 %copy-start.2 = (f32[16,32,1024]{2,1,0:T(8,128)S(1)}, f32[16,32,1024]{2,1,0:T(8,128)}, u32[]{:S(2)}) copy-start(f32[16,32,1024]{2,1,0:T(8,128)} %cat.5) | copy-start | bytes 6291460
  4.3 8.8 %collective-permute-start.2 = (f32[2,2,16,1024]{3,2,1,0:T(8,128)S(1)}, f32[2,2,16,1024]{3,2,1,0:T(8,128)S(1)}, u32[]{:S(2)}, u32[]{:S(2)}) collective-permute-start(f32[2,2,16,1024]{3,2,1,0:T(8,128)S(1)} %get-tuple-element.38.own_high), channel_id=1, source_target_pairs={{0,1},{1,2},{2,3},{3,4},{4,5},{5,6},{6,7},{7,0},{8,9},{9,10},{10,1... | collective-permute-start | bytes 786440 | tf_op jit(solution)/shard_map/ppermute | solution.py:462
  4.8 11.8 %copy-start.4 = (f32[3,2]{0,1:T(2,128)S(1)}, f32[3,2]{0,1:T(2,128)}, u32[]{:S(2)}) copy-start(f32[3,2]{0,1:T(2,128)} %param.7) | copy-start | bytes 76
  4.8 11.8 %copy-start.5 = (f32[2]{0:T(128)S(1)}, f32[2]{0:T(128)}, u32[]{:S(2)}) copy-start(f32[2]{0:T(128)} %scale.1) | copy-start | bytes 28
  4.8 12.4 %copy-start.1 = (f32[16,32,1024]{2,1,0:T(8,128)S(1)}, f32[16,32,1024]{2,1,0:T(8,128)}, u32[]{:S(2)}) copy-start(f32[16,32,1024]{2,1,0:T(8,128)} %sub.5) | copy-start | bytes 6291460
  4.8 12.4 %copy-start.3 = (f32[16,32,1024]{2,1,0:T(8,128)S(1)}, f32[16,32,1024]{2,1,0:T(8,128)}, u32[]{:S(2)}) copy-start(f32[16,32,1024]{2,1,0:T(8,128)} %cat.5) | copy-start | bytes 6291460
  4.8 8.7 %collective-permute-start.3 = (f32[2,2,16,1024]{3,2,1,0:T(8,128)S(1)}, f32[2,2,16,1024]{3,2,1,0:T(8,128)S(1)}, u32[]{:S(2)}, u32[]{:S(2)}) collective-permute-start(f32[2,2,16,1024]{3,2,1,0:T(8,128)S(1)} %get-tuple-element.39.own_low), channel_id=1, source_target_pairs={{0,7},{1,0},{2,1},{3,2},{4,3},{5,4},{6,5},{7,6},{8,15},{9,8},{10,9... | collective-permute-start | bytes 786440 | tf_op jit(solution)/shard_map/ppermute | solution.py:462
  10.1 17.1 %collective-permute-start = (f32[2,32,1024]{2,1,0:T(8,128)S(1)}, f32[2,32,1024]{2,1,0:T(8,128)S(1)}, u32[]{:S(2)}, u32[]{:S(2)}) collective-permute-start(f32[2,32,1024]{2,1,0:T(8,128)S(1)} %get-tuple-element.34.up), channel_id=1, source_target_pairs={{0,8},{8,16},{16,24},{24,0},{1,9},{9,17},{17,25},{25,1},{2,10},{10... | collective-permute-start | bytes 786440 | tf_op jit(solution)/shard_map/ppermute | solution.py:462
  12.1 15.2 %collective-permute-start.1 = (f32[2,32,1024]{2,1,0:T(8,128)S(1)}, f32[2,32,1024]{2,1,0:T(8,128)S(1)}, u32[]{:S(2)}, u32[]{:S(2)}) collective-permute-start(f32[2,32,1024]{2,1,0:T(8,128)S(1)} %get-tuple-element.35.down), channel_id=1, source_target_pairs={{0,24},{8,0},{16,8},{24,16},{1,25},{9,1},{17,9},{25,17},{2,26},{10... | collective-permute-start | bytes 786440 | tf_op jit(solution)/shard_map/ppermute | solution.py:462
  13.6 17.8 %collective-permute-start.4 = (f32[2,32,1024]{2,1,0:T(8,128)S(1)}, f32[2,32,1024]{2,1,0:T(8,128)S(1)}, u32[]{:S(2)}, u32[]{:S(2)}) collective-permute-start(f32[2,32,1024]{2,1,0:T(8,128)S(1)} %get-tuple-element.53), channel_id=1, source_target_pairs={{0,8},{8,16},{16,24},{24,0},{1,9},{9,17},{17,25},{25,1},{2,10},{10... | collective-permute-start | bytes 786440 | tf_op jit(solution)/shard_map/ppermute | solution.py:462
  15.7 19.3 %collective-permute-start.5 = (f32[2,32,1024]{2,1,0:T(8,128)S(1)}, f32[2,32,1024]{2,1,0:T(8,128)S(1)}, u32[]{:S(2)}, u32[]{:S(2)}) collective-permute-start(f32[2,32,1024]{2,1,0:T(8,128)S(1)} %get-tuple-element.54), channel_id=1, source_target_pairs={{0,24},{8,0},{16,8},{24,16},{1,25},{9,1},{17,9},{25,17},{2,26},{10... | collective-permute-start | bytes 786440 | tf_op jit(solution)/shard_map/ppermute | solution.py:462
  35.1 4.7 %collective-permute-start.6 = (f32[3,32,256]{2,1,0:T(8,128)S(1)}, f32[3,32,256]{2,1,0:T(8,128)S(1)}, u32[]{:S(2)}, u32[]{:S(2)}) collective-permute-start(f32[3,32,256]{2,1,0:T(8,128)S(1)} %get-tuple-element.62), channel_id=1, source_target_pairs={{0,8},{8,0},{16,24},{24,16},{1,9},{9,1},{17,25},{25,17},{2,10},{10... | collective-permute-start | bytes 294920 | tf_op jit(solution)/shard_map/ppermute | solution.py:585
  36.7 4.6 %collective-permute-start.7 = (f32[3,32,256]{2,1,0:T(8,128)S(1)}, f32[3,32,256]{2,1,0:T(8,128)S(1)}, u32[]{:S(2)}, u32[]{:S(2)}) collective-permute-start(f32[3,32,256]{2,1,0:T(8,128)S(1)} %get-tuple-element.63), channel_id=1, source_target_pairs={{0,16},{8,24},{16,0},{24,8},{1,17},{9,25},{17,1},{25,9},{2,18},{10... | collective-permute-start | bytes 294920 | tf_op jit(solution)/shard_map/ppermute | solution.py:585
  37.2 5.5 %collective-permute-start.8 = (f32[3,32,256]{2,1,0:T(8,128)S(1)}, f32[3,32,256]{2,1,0:T(8,128)S(1)}, u32[]{:S(2)}, u32[]{:S(2)}) collective-permute-start(f32[3,32,256]{2,1,0:T(8,128)S(1)} %get-tuple-element.64), channel_id=1, source_target_pairs={{0,24},{8,16},{16,8},{24,0},{1,25},{9,17},{17,9},{25,1},{2,26},{10... | collective-permute-start | bytes 294920 | tf_op jit(solution)/shard_map/ppermute | solution.py:585

commit v6 on v5

--- a/solution.py
+++ b/solution.py
@@ -63,6 +63,12 @@
     return tile[:, :columns] if columns <= LANES else jnp.concatenate([tile] * (columns // LANES), axis=1)
 
 
+def tile_of(inner, outer, tile, tiles):
+    if 0 < tile < tiles - 1:
+        return inner, span(tile - 1)
+    return outer, span(1 if tile else 0)
+
+
 def planes_kernel(sub, cat, up, down, sems):
     depth = sub.shape[0]
     copies = []
@@ -75,19 +81,21 @@
         copy.wait()
 
 
-def prepare_kernel(sub, cat, low, high, q_up, q_down):
+def prepare_kernel(sub, cat, low, high, q_up, q_down, r_up, r_down):
     depth, rows, _ = sub.shape
+    tiles = rows // ROWS
     fields = (sub, cat)
     for s, field in enumerate(fields):
         for plane in range(depth):
             for row in range(2):
                 low[s, row, plane : plane + 1] = field[plane, row : row + 1]
                 high[s, row, plane : plane + 1] = field[plane, rows - 2 + row : rows - 1 + row]
-    for outer, inner, out in ((depth - 1, depth - 2, q_up), (0, 1, q_down)):
-
-        def store(tile, sub_new, cat_new, out=out):
-            out[0, span(tile), :] = sub_new
-            out[1, span(tile), :] = cat_new
+    for outer, inner, q, r in ((depth - 1, depth - 2, q_up, r_up), (0, 1, q_down, r_down)):
+
+        def store(tile, sub_new, cat_new, q=q, r=r):
+            out, at = tile_of(q, r, tile, tiles)
+            out[0, at, :] = sub_new
+            out[1, at, :] = cat_new
 
         plane_step(
             lambda s, tile, outer=outer: fields[s][outer, span(tile), :],
@@ -190,7 +198,7 @@
 
 
 def second_kernel(
-    values, mid, q_up, q_down, from_low, from_high, own_low, own_high, center, sub_in, cat_in,
+    values, mid, q_up, q_down, r_up, r_down, from_low, from_high, own_low, own_high, center, sub_in, cat_in,
     sub_out, cat_out, seen, near, far, rows_low, rows_high,
     heads, tails, new, sem_out,
 ):
@@ -245,7 +253,9 @@
 
     for s in range(2):
         for tile in range(tiles):
-            first, last = q_down[s, span(tile), :], q_up[s, span(tile), :]
+            down, at = tile_of(q_down, r_down, tile, tiles)
+            up, at = tile_of(q_up, r_up, tile, tiles)
+            first, last = down[s, at, :], up[s, at, :]
             if tile == 0:
                 first, last = with_low(s, 0, first), with_low(s, depth - 1, last)
             if tile == tiles - 1:
@@ -289,22 +299,15 @@
                 put(s, k, end).wait()
 
 
-def rows_kernel(q_up, q_down, from_low, from_high, up, down):
+def rows_kernel(r_up, r_down, from_low, from_high, up, down):
     depth = from_low.shape[2]
-    tiles = q_up.shape[1] // ROWS
-    for plane, q, out in ((depth - 1, q_up, up), (0, q_down, down)):
-        for s in range(2):
-            for tile in range(tiles):
-                value = q[s, span(tile), :]
-                index = lax.broadcasted_iota(jnp.int32, value.shape, 0)
-                for at, edge, row in (
-                    (0, 0, from_low[s, 1, plane : plane + 1]),
-                    (tiles - 1, ROWS - 1, from_high[s, 0, plane : plane + 1]),
-                ):
-                    if tile == at:
-                        beside = jnp.broadcast_to((2.0 * RATES[s]) * row, value.shape)
-                        value = value + jnp.where(index == edge, beside, 0.0)
-                out[s, span(tile), :] = value
+    for plane, r, out in ((depth - 1, r_up, up), (0, r_down, down)):
+        for place, edge, source in ((0, 0, from_low.at[:, 1]), (1, ROWS - 1, from_high.at[:, 0])):
+            for s in range(2):
+                tile = r[s, span(place), :]
+                index = lax.broadcasted_iota(jnp.int32, tile.shape, 0)
+                row = jnp.broadcast_to((2.0 * RATES[s]) * source[s, plane : plane + 1], tile.shape)
+                out[s, span(place), :] = tile + jnp.where(index == edge, row, 0.0)
 
 
 def rim_kernel(
@@ -369,18 +372,20 @@
     return index ^ shift if count & (count - 1) == 0 else (index + count - shift) % count
 
 
-def last_kernel(values, known, q_low, q_high, seen, *rest):
+def last_kernel(values, known, q_low, q_high, r_low, r_high, seen, *rest):
     *pieces, outer, whole = rest
     rows, columns = seen.shape[1:]
     count = len(pieces)
     wide = columns // count
     scales = across_columns(values[0], columns), across_columns(values[1], columns)
-    for tile in range(rows // ROWS):
+    tiles = rows // ROWS
+    for tile in range(tiles):
         at = span(tile)
         planes = []
-        for side, q in enumerate((q_low, q_high)):
+        for side, (q, r) in enumerate(((q_low, r_low), (q_high, r_high))):
+            got, place = tile_of(q, r, tile, tiles)
             for s in range(2):
-                value = known[side, s, at, :] + RATES[s] * q[s, at, :]
+                value = known[side, s, at, :] + RATES[s] * got[s, place, :]
                 outer[s, side, at, :] = value
                 planes.append(value)
         one, two, clear = composite(planes[0], planes[1], *scales, 1.0)
@@ -474,17 +479,19 @@
     p_low = shifted(up, "gz", 1)
     p_high = shifted(down, "gz", -1)
 
-    own_low, own_high, q_up, q_down = call(
+    own_low, own_high, q_up, q_down, r_up, r_down = call(
         prepare_kernel,
         1 << 22,
         2,
         name="prepare",
-        out_shape=(f32(2, 2, depth, columns),) * 2 + (f32(2, rows, columns),) * 2,
+        out_shape=(f32(2, 2, depth, columns),) * 2 + (f32(2, middle, columns),) * 2 + (f32(2, 2 * ROWS, columns),) * 2,
         in_specs=[VMEM] * 2,
-        out_specs=(VMEM,) * 4,
+        out_specs=(VMEM,) * 6,
     )(substrate, catalyst)
     from_low = shifted(own_high, "gx", 1)
     from_high = shifted(own_low, "gx", -1)
+    q_low = shifted(q_up, "gz", 1)
+    q_high = shifted(q_down, "gz", -1)
 
     mid = call(
         first_kernel,
@@ -524,12 +531,12 @@
         1 << 18,
         2,
         name="rows",
-        out_shape=(f32(2, rows, columns),) * 2,
+        out_shape=(f32(2, 2 * ROWS, columns),) * 2,
         in_specs=[VMEM] * 4,
         out_specs=(VMEM,) * 2,
-    )(q_up, q_down, from_low, from_high)
-    q_low = shifted(m_up, "gz", 1)
-    q_high = shifted(m_down, "gz", -1)
+    )(r_up, r_down, from_low, from_high)
+    r_low = shifted(m_up, "gz", 1)
+    r_high = shifted(m_down, "gz", -1)
 
     sub_part, cat_part, inner, near, far, rows_low, rows_high = call(
         second_kernel,
@@ -545,16 +552,16 @@
             f32(2, depth, columns),
             f32(2, depth, columns),
         ),
-        in_specs=[VMEM] * 9 + [HBM, HBM],
+        in_specs=[VMEM] * 11 + [HBM, HBM],
         out_specs=(HBM, HBM) + (VMEM,) * 5,
-        input_output_aliases={9: 0, 10: 1},
+        input_output_aliases={11: 0, 12: 1},
         scratch_shapes=[
             pltpu.VMEM((2, depth, ROWS, columns), jnp.float32),
             pltpu.VMEM((2, depth, ROWS, columns), jnp.float32),
             pltpu.VMEM((2, 2, depth, ROWS, columns), jnp.float32),
             pltpu.SemaphoreType.DMA((2, 2, depth)),
         ],
-    )(values, mid, q_up, q_down, from_low, from_high, own_low, own_high, center, sub_part, cat_part)
+    )(values, mid, q_up, q_down, r_up, r_down, from_low, from_high, own_low, own_high, center, sub_part, cat_part)
 
     p_low, p_high, inner = lax.optimization_barrier((p_low, p_high, inner))
     ring_planes, known, seen = call(
@@ -574,10 +581,10 @@
         4,
         name="last",
         out_shape=(f32(3, rows, wide),) * count + (f32(2, 2, rows, columns),),
-        in_specs=[VMEM] * 5,
+        in_specs=[VMEM] * 7,
         out_specs=(VMEM,) * (count + 1),
         scratch_shapes=[pltpu.VMEM((3, rows, columns), jnp.float32)],
-    )(values, known, q_low, q_high, seen)
+    )(values, known, q_low, q_high, r_low, r_high, seen)
 
     received = [pieces[0]] * count
     for shift in piece_order(count):

time: 43.7 us -> 42.7 us (0.977)
  waiting for transfers between devices: 10.3 us -> 6.95 us
  starting transfers between devices: 14.3 us -> 16.7 us
    ppermute x6 -> x8, waiting for transfers between devices: 7.3 us -> 4.88 us  [shifted(): return lax.ppermute(x, axis, ring(lax.axis_size(axis), shift))]
    ppermute x6 -> x8, starting transfers between devices: 10.7 us -> 13.1 us  [shifted(): return lax.ppermute(x, axis, ring(lax.axis_size(axis), shift))]
    ppermute x3, waiting for transfers between devices: 3 us -> 2.07 us  [body(): received[shift] = lax.ppermute(pieces[shift], 'gz', pairs)]
  transfers between devices with their start and end apart: 9 -> 11, of which waited for: 6 -> 5; matrix products, arithmetic and copies ran while one was open for 0% -> 0% of each run, Pallas kernels for 31% -> 32%
where the time goes in v6:
time: 42.7 us; the launch traced here: 42.5 us
  starting transfers between devices  16.7 us (39%)
  Pallas kernels  14.9 us (35%)
  waiting for transfers between devices  6.95 us (16%)
  local copies, waits for them, and re-layouts  3.19 us (7%)
  between operations  0.77 us (2%)
    ppermute x8, starting transfers between devices, shifted(): return lax.ppermute(x, axis, ring(lax.axis_size(axis), shift))  13.1 us
    ppermute x8, waiting for transfers between devices, shifted(): return lax.ppermute(x, axis, ring(lax.axis_size(axis), shift))  4.88 us
    pallas_call x1, Pallas kernels, body(): call(second_kernel, 1 << 25, 10, name='second', out_shape=(f32(depth, row...  4.02 us
    ppermute x3, starting transfers between devices, body(): received[shift] = lax.ppermute(pieces[shift], 'gz', pairs)  3.55 us
    unnamed x12, local copies, waits for them, and re-layouts  3.19 us
    pallas_call x1, Pallas kernels, body(): call(center_kernel, 1 << 24, 4, name='center', out_shape=(f32(depth, rows...  2.98 us
    pallas_call x1, Pallas kernels, body(): call(first_kernel, 1 << 24, 2, name='first', out_shape=f32(2, depth, rows...  2.95 us
    ppermute x3, waiting for transfers between devices, body(): received[shift] = lax.ppermute(pieces[shift], 'gz', pairs)  2.07 us
  transfers between devices with their start and end apart: 11, of which 5 were waited for; matrix products, arithmetic and copies ran while one was open for 0% of the time, Pallas kernels for 32%

profile of v6, /device:TPU:0, one launch (start us, length us, event | category | flops | bytes accessed | tf_op | source)
XLA Modules:
  0.0 42.5 jit_solution(12774026360768126390)
XLA Ops:
  0.6 0.0 copy-start
  0.6 1.6 %copy-done = f32[16,32,1024]{2,1,0:T(8,128)S(1)} copy-done((f32[16,32,1024]{2,1,0:T(8,128)S(1)}, f32[16,32,1024]{2,1,0:T(8,128)}, u32[]{:S(2)}) %copy-start) | copy-done | bytes 2097176
  2.2 0.0 copy-start.2
  2.2 1.6 %copy-done.2 = f32[16,32,1024]{2,1,0:T(8,128)S(1)} copy-done((f32[16,32,1024]{2,1,0:T(8,128)S(1)}, f32[16,32,1024]{2,1,0:T(8,128)}, u32[]{:S(2)}) %copy-start.2) | copy-done | bytes 2097176
  3.8 0.5 %prepare.1 = (f32[2,2,16,1024]{3,2,1,0:T(8,128)S(1)}, f32[2,2,16,1024]{3,2,1,0:T(8,128)S(1)}, f32[2,16,1024]{2,1,0:T(8,128)S(1)}, f32[2,16,1024]{2,1,0:T(8,128)S...) custom-call(f32[16,32,1024]{2,1,0:T(8,128)S(1)} %copy-done, f32[16,32,1024]{2,1,0:T(8,128)S(1)} %copy-done.2), custom_call_target="tpu_custom_call" | custom-call | flops 4194304 | bytes 65536 | tf_op jit(solution)/shard_map/prepare/pallas_call | solution.py:482
  4.3 0.5 %collective-permute-start.2 = (f32[2,2,16,1024]{3,2,1,0:T(8,128)S(1)}, f32[2,2,16,1024]{3,2,1,0:T(8,128)S(1)}, u32[]{:S(2)}, u32[]{:S(2)}) collective-permute-start(f32[2,2,16,1024]{3,2,1,0:T(8,128)S(1)} %get-tuple-element.42.own_high), channel_id=1, source_target_pairs={{0,1},{1,2},{2,3},{3,4},{4,5},{5,6},{6,7},{7,0},{8,9},{9,10},{10,1... | collective-permute-start | bytes 786440 | tf_op jit(solution)/shard_map/ppermute | solution.py:467
  4.8 0.0 copy-start.4
  4.8 0.0 copy-start.5
  4.8 0.0 copy-start.1
  4.8 0.0 copy-start.3
  4.8 4.1 %collective-permute-start.3 = (f32[2,2,16,1024]{3,2,1,0:T(8,128)S(1)}, f32[2,2,16,1024]{3,2,1,0:T(8,128)S(1)}, u32[]{:S(2)}, u32[]{:S(2)}) collective-permute-start(f32[2,2,16,1024]{3,2,1,0:T(8,128)S(1)} %get-tuple-element.43.own_low), channel_id=1, source_target_pairs={{0,7},{1,0},{2,1},{3,2},{4,3},{5,4},{6,5},{7,6},{8,15},{9,8},{10,9... | collective-permute-start | bytes 786440 | tf_op jit(solution)/shard_map/ppermute | solution.py:467
  9.0 1.1 %planes.1 = (f32[2,32,1024]{2,1,0:T(8,128)S(1)}, f32[2,32,1024]{2,1,0:T(8,128)S(1)}) custom-call(f32[16,32,1024]{2,1,0:T(8,128)} %sub.5, f32[16,32,1024]{2,1,0:T(8,128)} %cat.5), custom_call_target="tpu_custom_call" | custom-call | flops 1048576 | bytes 65536 | tf_op jit(solution)/shard_map/planes/pallas_call | solution.py:469
  10.1 2.0 %collective-permute-start = (f32[2,32,1024]{2,1,0:T(8,128)S(1)}, f32[2,32,1024]{2,1,0:T(8,128)S(1)}, u32[]{:S(2)}, u32[]{:S(2)}) collective-permute-start(f32[2,32,1024]{2,1,0:T(8,128)S(1)} %get-tuple-element.36.up), channel_id=1, source_target_pairs={{0,8},{8,16},{16,24},{24,0},{1,9},{9,17},{17,25},{25,1},{2,10},{10... | collective-permute-start | bytes 786440 | tf_op jit(solution)/shard_map/ppermute | solution.py:467
  12.1 1.0 %collective-permute-start.1 = (f32[2,32,1024]{2,1,0:T(8,128)S(1)}, f32[2,32,1024]{2,1,0:T(8,128)S(1)}, u32[]{:S(2)}, u32[]{:S(2)}) collective-permute-start(f32[2,32,1024]{2,1,0:T(8,128)S(1)} %get-tuple-element.37.down), channel_id=1, source_target_pairs={{0,24},{8,0},{16,8},{24,16},{1,25},{9,1},{17,9},{25,17},{2,26},{10... | collective-permute-start | bytes 786440 | tf_op jit(solution)/shard_map/ppermute | solution.py:467
  13.1 1.0 %collective-permute-start.4 = (f32[2,16,1024]{2,1,0:T(8,128)S(1)}, f32[2,16,1024]{2,1,0:T(8,128)S(1)}, u32[]{:S(2)}, u32[]{:S(2)}) collective-permute-start(f32[2,16,1024]{2,1,0:T(8,128)S(1)} %get-tuple-element.38.q_up), channel_id=1, source_target_pairs={{0,8},{8,16},{16,24},{24,0},{1,9},{9,17},{17,25},{25,1},{2,10},{10... | collective-permute-start | bytes 393224 | tf_op jit(solution)/shard_map/ppermute | solution.py:467
  14.1 0.0 collective-permute-done.2.from_low
  14.1 2.4 %collective-permute-start.5 = (f32[2,16,1024]{2,1,0:T(8,128)S(1)}, f32[2,16,1024]{2,1,0:T(8,128)S(1)}, u32[]{:S(2)}, u32[]{:S(2)}) collective-permute-start(f32[2,16,1024]{2,1,0:T(8,128)S(1)} %get-tuple-element.39.q_down), channel_id=1, source_target_pairs={{0,24},{8,0},{16,8},{24,16},{1,25},{9,1},{17,9},{25,17},{2,26},{10... | collective-permute-start | bytes 393224 | tf_op jit(solution)/shard_map/ppermute | solution.py:467
  16.5 0.0 collective-permute-done.3.from_high
  16.5 0.1 collective-permute-start.6
  16.6 3.6 %collective-permute-done.p_low = f32[2,32,1024]{2,1,0:T(8,128)S(1)} collective-permute-done((f32[2,32,1024]{2,1,0:T(8,128)S(1)}, f32[2,32,1024]{2,1,0:T(8,128)S(1)}, u32[]{:S(2)}, u32[]{:S(2)}) %collective-permute-start) | collective-permute-done | bytes 262176 | tf_op jit(solution)/shard_map/ppermute | solution.py:467
  20.2 2.0 %collective-permute-start.7 = (f32[2,16,1024]{2,1,0:T(8,128)S(1)}, f32[2,16,1024]{2,1,0:T(8,128)S(1)}, u32[]{:S(2)}, u32[]{:S(2)}) collective-permute-start(f32[2,16,1024]{2,1,0:T(8,128)S(1)} %get-tuple-element.58), channel_id=1, source_target_pairs={{0,24},{8,0},{16,8},{24,16},{1,25},{9,1},{17,9},{25,17},{2,26},{10... | collective-permute-start | bytes 393224 | tf_op jit(solution)/shard_map/ppermute | solution.py:467
  22.2 0.0 copy-done.4
  22.2 0.0 copy-done.5
  22.2 0.6 %scalars.1.values = f32[8,8,128]{2,1,0:T(8,128)S(1)} custom-call(f32[2]{0:T(128)S(1)} %copy-done.5, f32[2,3]{1,0:T(2,128)S(1)} %bitcast.1), custom_call_target="tpu_custom_call" | custom-call | flops 262144 | bytes 65536 | tf_op jit(solution)/shard_map/scalars/pallas_call | solution.py:505
  22.8 0.0 copy-done.1
  22.8 0.0 copy-done.3
  22.8 3.0 %first.1.mid = f32[2,16,32,1024]{3,2,1,0:T(8,128)S(1)} custom-call(f32[16,32,1024]{2,1,0:T(8,128)S(1)} %copy-done.1, f32[16,32,1024]{2,1,0:T(8,128)S(1)} %copy-done.3), custom_call_target="tpu_custom_call" | custom-call | flops 16777216 | bytes 65536 | tf_op jit(solution)/shard_map/first/pallas_call | solution.py:496
  25.8 3.0 %center.1 = (f32[16,32,1024]{2,1,0:T(8,128)}, f32[16,32,1024]{2,1,0:T(8,128)}, f32[3,32,1024]{2,1,0:T(8,128)S(1)}) custom-call(f32[8,8,128]{2,1,0:T(8,128)S(1)} %scalars.1.values, f32[2,16,32,1024]{3,2,1,0:T(8,128)S(1)} %first.1.mid), custom_call_target="tpu_custom_call" | custom-call | flops 16777216 | bytes 65536 | tf_op jit(solution)/shard_map/center/pallas_call | solution.py:515
  28.8 4.0 %second.1 = (f32[16,32,1024]{2,1,0:T(8,128)}, f32[16,32,1024]{2,1,0:T(8,128)}, f32[3,32,1024]{2,1,0:T(8,128)S(1)}, f32[2,3,32,1024]{3,2,1,0:T(8,128)S(1)}, f32[2...) custom-call(f32[8,8,128]{2,1,0:T(8,128)S(1)} %scalars.1.values, ...), custom_call_target="tpu_custom_call", output_to_operand_aliasing={{0}: (11, {}), {1}: (12, {})} | custom-call | flops 33554432 | bytes 65536 | tf_op jit(solution)/shard_map/second/pallas_call | solution.py:541
  32.8 0.0 collective-permute-done.1.p_high
  32.8 0.8 %rim.1 = (f32[2,2,32,1024]{3,2,1,0:T(8,128)S(1)}, f32[2,2,32,1024]{3,2,1,0:T(8,128)S(1)}, f32[3,32,1024]{2,1,0:T(8,128)S(1)}) custom-call(f32[8,8,128]{2,1,0:T(8,128)S(1)} %scalars.1.values, f32[2,32,1024]{2,1,0:T(8,128)S(1)} %collective-permute-done.p_low, f32[2,32,1024]{2,1,0:T(8,128)S(1)} %collective-permute-done.1.p_high, ...), custom_call_target="tpu_custom_call" | custom-call | flops 8388608 | bytes 65536 | tf_op jit(solution)/shard_map/rim/pallas_call | solution.py:567
  33.7 0.0 collective-permute-done.4.q_low
  33.7 0.0 collective-permute-done.5.q_high
  33.7 0.0 collective-permute-done.6.r_low
  33.7 1.3 %collective-permute-done.7.r_high = f32[2,16,1024]{2,1,0:T(8,128)S(1)} collective-permute-done((f32[2,16,1024]{2,1,0:T(8,128)S(1)}, f32[2,16,1024]{2,1,0:T(8,128)S(1)}, u32[]{:S(2)}, u32[]{:S(2)}) %collective-permute-start.7) | collective-permute-done | bytes 131104 | tf_op jit(solution)/shard_map/ppermute | solution.py:467
  34.9 0.2 last.1
  35.1 1.5 %collective-permute-start.10 = (f32[3,32,256]{2,1,0:T(8,128)S(1)}, f32[3,32,256]{2,1,0:T(8,128)S(1)}, u32[]{:S(2)}, u32[]{:S(2)}) collective-permute-start(f32[3,32,256]{2,1,0:T(8,128)S(1)} %get-tuple-element.68), channel_id=1, source_target_pairs={{0,24},{8,16},{16,8},{24,0},{1,25},{9,17},{17,9},{25,1},{2,26},{10... | collective-permute-start | bytes 294920 | tf_op jit(solution)/shard_map/ppermute | solution.py:592
  36.6 0.5 %collective-permute-start.8 = (f32[3,32,256]{2,1,0:T(8,128)S(1)}, f32[3,32,256]{2,1,0:T(8,128)S(1)}, u32[]{:S(2)}, u32[]{:S(2)}) collective-permute-start(f32[3,32,256]{2,1,0:T(8,128)S(1)} %get-tuple-element.66), channel_id=1, source_target_pairs={{0,8},{8,0},{16,24},{24,16},{1,9},{9,1},{17,25},{25,17},{2,10},{10... | collective-permute-start | bytes 294920 | tf_op jit(solution)/shard_map/ppermute | solution.py:592
  37.2 1.5 %collective-permute-start.9 = (f32[3,32,256]{2,1,0:T(8,128)S(1)}, f32[3,32,256]{2,1,0:T(8,128)S(1)}, u32[]{:S(2)}, u32[]{:S(2)}) collective-permute-start(f32[3,32,256]{2,1,0:T(8,128)S(1)} %get-tuple-element.67), channel_id=1, source_target_pairs={{0,16},{8,24},{16,0},{24,8},{1,17},{9,25},{17,1},{25,9},{2,18},{10... | collective-permute-start | bytes 294920 | tf_op jit(solution)/shard_map/ppermute | solution.py:592
  38.7 1.0 %place.1 = (f32[16,32,1024]{2,1,0:T(8,128)}, f32[16,32,1024]{2,1,0:T(8,128)}) custom-call(f32[2,2,32,1024]{3,2,1,0:T(8,128)S(1)} %get-tuple-element.55.ring, f32[2,2,32,1024]{3,2,1,0:T(8,128)S(1)} %get-tuple-element.60.outer, f32[16,32,1024]{2,1,0:T(8,128)} %get-tuple-element.61.sub_in, ...), custom_call_target="tpu_custom_call", output_to_operand_aliasing={{0}: (2, {}), {1}: (3, {})} | custom-call | flops 4194304 | bytes 65536 | tf_op jit(solution)/shard_map/place/pallas_call | solution.py:594
  39.7 1.0 %collective-permute-done.10.pieces_and_rest_3_ = f32[3,32,256]{2,1,0:T(8,128)S(1)} collective-permute-done((f32[3,32,256]{2,1,0:T(8,128)S(1)}, f32[3,32,256]{2,1,0:T(8,128)S(1)}, u32[]{:S(2)}, u32[]{:S(2)}) %collective-permute-start.10) | collective-permute-done | bytes 98336 | tf_op jit(solution)/shard_map/ppermute | solution.py:592
  40.7 0.5 %collective-permute-done.8.pieces_and_rest_1_ = f32[3,32,256]{2,1,0:T(8,128)S(1)} collective-permute-done((f32[3,32,256]{2,1,0:T(8,128)S(1)}, f32[3,32,256]{2,1,0:T(8,128)S(1)}, u32[]{:S(2)}, u32[]{:S(2)}) %collective-permute-start.8) | collective-permute-done | bytes 98336 | tf_op jit(solution)/shard_map/ppermute | solution.py:592
  41.3 0.5 %collective-permute-done.9.pieces_and_rest_2_ = f32[3,32,256]{2,1,0:T(8,128)S(1)} collective-permute-done((f32[3,32,256]{2,1,0:T(8,128)S(1)}, f32[3,32,256]{2,1,0:T(8,128)S(1)}, u32[]{:S(2)}, u32[]{:S(2)}) %collective-permute-start.9) | collective-permute-done | bytes 98336 | tf_op jit(solution)/shard_map/ppermute | solution.py:592
  41.8 0.7 %shade.1 = f32[4,32,256]{2,1,0:T(8,128)} custom-call(f32[8,8,128]{2,1,0:T(8,128)S(1)} %scalars.1.values, f32[3,32,256]{2,1,0:T(8,128)S(1)} %get-tuple-element.65.pieces_and_rest_0_, f32[3,32,256]{2,1,0:T(8,128)S(1)} %collective-permute-done.8.pieces_and_rest_1_, f32[3,32,256]{2,1,0:T(8,128)S(1)} %collective-permute-done.9.pieces_and_rest_2_, ...), custom_call_target="tpu_custom_call" | custom-call | flops 1048576 | bytes 65536 | tf_op jit(solution)/shard_map/shade/pallas_call | solution.py:606
  (1 shorter events, 0.0 us)
Async XLA Ops:
  0.6 1.6 %copy-start = (f32[16,32,1024]{2,1,0:T(8,128)S(1)}, f32[16,32,1024]{2,1,0:T(8,128)}, u32[]{:S(2)}) copy-start(f32[16,32,1024]{2,1,0:T(8,128)} %sub.5) | copy-start | bytes 6291460
  2.2 1.6 %copy-start.2 = (f32[16,32,1024]{2,1,0:T(8,128)S(1)}, f32[16,32,1024]{2,1,0:T(8,128)}, u32[]{:S(2)}) copy-start(f32[16,32,1024]{2,1,0:T(8,128)} %cat.5) | copy-start | bytes 6291460
  4.3 9.8 %collective-permute-start.2 = (f32[2,2,16,1024]{3,2,1,0:T(8,128)S(1)}, f32[2,2,16,1024]{3,2,1,0:T(8,128)S(1)}, u32[]{:S(2)}, u32[]{:S(2)}) collective-permute-start(f32[2,2,16,1024]{3,2,1,0:T(8,128)S(1)} %get-tuple-element.42.own_high), channel_id=1, source_target_pairs={{0,1},{1,2},{2,3},{3,4},{4,5},{5,6},{6,7},{7,0},{8,9},{9,10},{10,1... | collective-permute-start | bytes 786440 | tf_op jit(solution)/shard_map/ppermute | solution.py:467
  4.8 17.4 %copy-start.4 = (f32[3,2]{0,1:T(2,128)S(1)}, f32[3,2]{0,1:T(2,128)}, u32[]{:S(2)}) copy-start(f32[3,2]{0,1:T(2,128)} %param.7) | copy-start | bytes 76
  4.8 17.4 %copy-start.5 = (f32[2]{0:T(128)S(1)}, f32[2]{0:T(128)}, u32[]{:S(2)}) copy-start(f32[2]{0:T(128)} %scale.1) | copy-start | bytes 28
  4.8 18.0 %copy-start.1 = (f32[16,32,1024]{2,1,0:T(8,128)S(1)}, f32[16,32,1024]{2,1,0:T(8,128)}, u32[]{:S(2)}) copy-start(f32[16,32,1024]{2,1,0:T(8,128)} %sub.5) | copy-start | bytes 6291460
  4.8 18.0 %copy-start.3 = (f32[16,32,1024]{2,1,0:T(8,128)S(1)}, f32[16,32,1024]{2,1,0:T(8,128)}, u32[]{:S(2)}) copy-start(f32[16,32,1024]{2,1,0:T(8,128)} %cat.5) | copy-start | bytes 6291460
  4.8 11.7 %collective-permute-start.3 = (f32[2,2,16,1024]{3,2,1,0:T(8,128)S(1)}, f32[2,2,16,1024]{3,2,1,0:T(8,128)S(1)}, u32[]{:S(2)}, u32[]{:S(2)}) collective-permute-start(f32[2,2,16,1024]{3,2,1,0:T(8,128)S(1)} %get-tuple-element.43.own_low), channel_id=1, source_target_pairs={{0,7},{1,0},{2,1},{3,2},{4,3},{5,4},{6,5},{7,6},{8,15},{9,8},{10,9... | collective-permute-start | bytes 786440 | tf_op jit(solution)/shard_map/ppermute | solution.py:467
  10.1 10.1 %collective-permute-start = (f32[2,32,1024]{2,1,0:T(8,128)S(1)}, f32[2,32,1024]{2,1,0:T(8,128)S(1)}, u32[]{:S(2)}, u32[]{:S(2)}) collective-permute-start(f32[2,32,1024]{2,1,0:T(8,128)S(1)} %get-tuple-element.36.up), channel_id=1, source_target_pairs={{0,8},{8,16},{16,24},{24,0},{1,9},{9,17},{17,25},{25,1},{2,10},{10... | collective-permute-start | bytes 786440 | tf_op jit(solution)/shard_map/ppermute | solution.py:467
  12.1 20.7 %collective-permute-start.1 = (f32[2,32,1024]{2,1,0:T(8,128)S(1)}, f32[2,32,1024]{2,1,0:T(8,128)S(1)}, u32[]{:S(2)}, u32[]{:S(2)}) collective-permute-start(f32[2,32,1024]{2,1,0:T(8,128)S(1)} %get-tuple-element.37.down), channel_id=1, source_target_pairs={{0,24},{8,0},{16,8},{24,16},{1,25},{9,1},{17,9},{25,17},{2,26},{10... | collective-permute-start | bytes 786440 | tf_op jit(solution)/shard_map/ppermute | solution.py:467
  13.1 20.5 %collective-permute-start.4 = (f32[2,16,1024]{2,1,0:T(8,128)S(1)}, f32[2,16,1024]{2,1,0:T(8,128)S(1)}, u32[]{:S(2)}, u32[]{:S(2)}) collective-permute-start(f32[2,16,1024]{2,1,0:T(8,128)S(1)} %get-tuple-element.38.q_up), channel_id=1, source_target_pairs={{0,8},{8,16},{16,24},{24,0},{1,9},{9,17},{17,25},{25,1},{2,10},{10... | collective-permute-start | bytes 393224 | tf_op jit(solution)/shard_map/ppermute | solution.py:467
  14.1 19.5 %collective-permute-start.5 = (f32[2,16,1024]{2,1,0:T(8,128)S(1)}, f32[2,16,1024]{2,1,0:T(8,128)S(1)}, u32[]{:S(2)}, u32[]{:S(2)}) collective-permute-start(f32[2,16,1024]{2,1,0:T(8,128)S(1)} %get-tuple-element.39.q_down), channel_id=1, source_target_pairs={{0,24},{8,0},{16,8},{24,16},{1,25},{9,1},{17,9},{25,17},{2,26},{10... | collective-permute-start | bytes 393224 | tf_op jit(solution)/shard_map/ppermute | solution.py:467
  16.5 17.1 %collective-permute-start.6 = (f32[2,16,1024]{2,1,0:T(8,128)S(1)}, f32[2,16,1024]{2,1,0:T(8,128)S(1)}, u32[]{:S(2)}, u32[]{:S(2)}) collective-permute-start(f32[2,16,1024]{2,1,0:T(8,128)S(1)} %get-tuple-element.57), channel_id=1, source_target_pairs={{0,8},{8,16},{16,24},{24,0},{1,9},{9,17},{17,25},{25,1},{2,10},{10... | collective-permute-start | bytes 393224 | tf_op jit(solution)/shard_map/ppermute | solution.py:467
  20.2 14.7 %collective-permute-start.7 = (f32[2,16,1024]{2,1,0:T(8,128)S(1)}, f32[2,16,1024]{2,1,0:T(8,128)S(1)}, u32[]{:S(2)}, u32[]{:S(2)}) collective-permute-start(f32[2,16,1024]{2,1,0:T(8,128)S(1)} %get-tuple-element.58), channel_id=1, source_target_pairs={{0,24},{8,0},{16,8},{24,16},{1,25},{9,1},{17,9},{25,17},{2,26},{10... | collective-permute-start | bytes 393224 | tf_op jit(solution)/shard_map/ppermute | solution.py:467
  35.1 5.6 %collective-permute-start.10 = (f32[3,32,256]{2,1,0:T(8,128)S(1)}, f32[3,32,256]{2,1,0:T(8,128)S(1)}, u32[]{:S(2)}, u32[]{:S(2)}) collective-permute-start(f32[3,32,256]{2,1,0:T(8,128)S(1)} %get-tuple-element.68), channel_id=1, source_target_pairs={{0,24},{8,16},{16,8},{24,0},{1,25},{9,17},{17,9},{25,1},{2,26},{10... | collective-permute-start | bytes 294920 | tf_op jit(solution)/shard_map/ppermute | solution.py:592
  36.6 4.6 %collective-permute-start.8 = (f32[3,32,256]{2,1,0:T(8,128)S(1)}, f32[3,32,256]{2,1,0:T(8,128)S(1)}, u32[]{:S(2)}, u32[]{:S(2)}) collective-permute-start(f32[3,32,256]{2,1,0:T(8,128)S(1)} %get-tuple-element.66), channel_id=1, source_target_pairs={{0,8},{8,0},{16,24},{24,16},{1,9},{9,1},{17,25},{25,17},{2,10},{10... | collective-permute-start | bytes 294920 | tf_op jit(solution)/shard_map/ppermute | solution.py:592
  37.2 4.6 %collective-permute-start.9 = (f32[3,32,256]{2,1,0:T(8,128)S(1)}, f32[3,32,256]{2,1,0:T(8,128)S(1)}, u32[]{:S(2)}, u32[]{:S(2)}) collective-permute-start(f32[3,32,256]{2,1,0:T(8,128)S(1)} %get-tuple-element.67), channel_id=1, source_target_pairs={{0,16},{8,24},{16,0},{24,8},{1,17},{9,25},{17,1},{25,9},{2,18},{10... | collective-permute-start | bytes 294920 | tf_op jit(solution)/shard_map/ppermute | solution.py:592

commit v7 on v6

--- a/solution.py
+++ b/solution.py
@@ -372,50 +372,78 @@
     return index ^ shift if count & (count - 1) == 0 else (index + count - shift) % count
 
 
-def last_kernel(values, known, q_low, q_high, r_low, r_high, seen, *rest):
-    *pieces, outer, whole = rest
-    rows, columns = seen.shape[1:]
-    count = len(pieces)
-    wide = columns // count
+def finish(values, known, seen, low, high, tiles, outer, whole, where):
+    columns = seen.shape[2]
     scales = across_columns(values[0], columns), across_columns(values[1], columns)
-    tiles = rows // ROWS
-    for tile in range(tiles):
-        at = span(tile)
+    for place, tile in enumerate(tiles):
+        at, to = span(tile), span(place)
         planes = []
-        for side, (q, r) in enumerate(((q_low, r_low), (q_high, r_high))):
-            got, place = tile_of(q, r, tile, tiles)
+        for side, q in enumerate((low, high)):
             for s in range(2):
-                value = known[side, s, at, :] + RATES[s] * got[s, place, :]
-                outer[s, side, at, :] = value
+                value = known[side, s, at, :] + RATES[s] * q[s, to, :]
+                outer[s, side, to, :] = value
                 planes.append(value)
         one, two, clear = composite(planes[0], planes[1], *scales, 1.0)
         sub = one + clear * seen[0, at, :]
         cat = two + clear * seen[1, at, :]
         clear = clear * seen[2, at, :]
         one, two, clear = composite(planes[2], planes[3], *scales, clear)
-        whole[0, at, :] = sub + one
-        whole[1, at, :] = cat + two
-        whole[2, at, :] = clear
+        whole[0, where(tile), :] = sub + one
+        whole[1, where(tile), :] = cat + two
+        whole[2, where(tile), :] = clear
+
+
+def cut(whole, rows, piece, to, target, count):
+    wide = whole.shape[2] // count
+    if wide % LANES == 0:
+        piece[:, to, :] = whole[:, rows, pl.ds(pl.multiple_of(target * wide, LANES), wide)]
+        return
+    for other in range(count):
+
+        @pl.when(target == other)
+        def _(other=other):
+            piece[:, to, :] = whole[:, rows, other * wide : (other + 1) * wide]
+
+
+def most_kernel(count, values, known, q_low, q_high, seen, piece, outer, whole):
+    tiles = seen.shape[1] // ROWS
+    finish(values, known, seen, q_low, q_high, range(1, tiles - 1), outer, whole, lambda tile: span(tile - 1))
+    everything = pl.ds(0, piece.shape[1])
+    cut(whole, everything, piece, everything, partner(lax.axis_index("gz"), count // 2, count), count)
+
+
+def last_kernel(values, known, r_low, r_high, seen, most, *rest):
+    *pieces, outer, whole = rest
+    rows = seen.shape[1]
+    tiles = rows // ROWS
+    count = len(pieces)
+    finish(values, known, seen, r_low, r_high, (0, tiles - 1), outer, whole, span)
+    inside = pl.ds(ROWS, rows - 2 * ROWS)
+    whole[:, inside, :] = most[...]
     me = lax.axis_index("gz")
     for shift, piece in enumerate(pieces):
         target = partner(me, shift, count)
-        if wide % LANES == 0:
-            piece[...] = whole[:, :, pl.ds(pl.multiple_of(target * wide, LANES), wide)]
+        if piece.shape[1] == rows:
+            everything = pl.ds(0, rows)
+            cut(whole, everything, piece, everything, target, count)
         else:
-            for other in range(count):
-
-                @pl.when(target == other)
-                def _(piece=piece, other=other):
-                    piece[...] = whole[:, :, other * wide : (other + 1) * wide]
-
-
-def shade_kernel(values, *pieces_and_rest):
+            cut(whole, pl.ds(0, ROWS), piece, span(0), target, count)
+            cut(whole, pl.ds(rows - ROWS, ROWS), piece, span(1), target, count)
+
+
+def shade_kernel(values, half, *pieces_and_rest):
     *pieces, image, slabs = pieces_and_rest
     count = len(pieces)
     rows, wide = image.shape[1:]
     me = lax.axis_index("gz")
     for shift, piece in enumerate(pieces):
-        slabs[origin(me, shift, count)] = piece[...]
+        slab = origin(me, shift, count)
+        if piece.shape[1] == rows:
+            slabs[slab] = piece[...]
+        else:
+            slabs[slab, :, pl.ds(ROWS, rows - 2 * ROWS), :] = half[...]
+            slabs[slab, :, span(0), :] = piece[:, :ROWS]
+            slabs[slab, :, pl.ds(rows - ROWS, ROWS), :] = piece[:, ROWS:]
     for tile in range(rows // ROWS):
         at = span(tile)
         sub, cat, clear = slabs[0, 0, at, :], slabs[0, 1, at, :], slabs[0, 2, at, :]
@@ -430,14 +458,20 @@
         image[3, at, :] = 1.0 - clear
 
 
-def place_kernel(ring, outer, sub_in, cat_in, sub_out, cat_out, sems):
+def place_kernel(ring, inner, outer, sub_in, cat_in, sub_out, cat_out, sems):
     del sub_in, cat_in
-    depth = sub_out.shape[0]
+    depth, rows, _ = sub_out.shape
     copies = []
     for s, out in enumerate((sub_out, cat_out)):
         for side in range(2):
-            for at, source in ((side * (depth - 1), outer), (1 + side * (depth - 3), ring)):
-                copies.append(pltpu.make_async_copy(source.at[s, side], out.at[at], sems.at[len(copies)]))
+            plane = side * (depth - 1)
+            for source, target in (
+                (ring.at[s, side], out.at[1 + side * (depth - 3)]),
+                (inner.at[s, side], out.at[plane, pl.ds(ROWS, rows - 2 * ROWS)]),
+                (outer.at[s, side, span(0)], out.at[plane, span(0)]),
+                (outer.at[s, side, span(1)], out.at[plane, pl.ds(rows - ROWS, ROWS)]),
+            ):
+                copies.append(pltpu.make_async_copy(source, target, sems.at[len(copies)]))
     for copy in copies:
         copy.start()
     for copy in copies:
@@ -575,21 +609,37 @@
         scratch_shapes=[pltpu.VMEM((2, 2, rows, columns), jnp.float32)],
     )(values, p_low, p_high, down, up, near, far, rows_low, rows_high, inner)
 
-    *pieces, outer = call(
+    half = count // 2
+    half_piece, inner_rows, most = call(
+        functools.partial(most_kernel, count),
+        1 << 22,
+        2,
+        name="most",
+        out_shape=(f32(3, middle, wide), f32(2, 2, middle, columns), f32(3, middle, columns)),
+        in_specs=[VMEM] * 5,
+        out_specs=(VMEM,) * 3,
+    )(values, known, q_low, q_high, seen)
+
+    def paired(piece, shift):
+        return lax.ppermute(piece, "gz", [(i, int(partner(i, shift, count))) for i in range(count)])
+
+    half_piece = paired(half_piece, half)
+
+    *pieces, outer_rows = call(
         last_kernel,
         1 << 22,
         4,
         name="last",
-        out_shape=(f32(3, rows, wide),) * count + (f32(2, 2, rows, columns),),
-        in_specs=[VMEM] * 7,
+        out_shape=tuple(f32(3, 2 * ROWS if shift == half else rows, wide) for shift in range(count))
+        + (f32(2, 2, 2 * ROWS, columns),),
+        in_specs=[VMEM] * 6,
         out_specs=(VMEM,) * (count + 1),
         scratch_shapes=[pltpu.VMEM((3, rows, columns), jnp.float32)],
-    )(values, known, q_low, q_high, r_low, r_high, seen)
+    )(values, known, r_low, r_high, seen, most)
 
     received = [pieces[0]] * count
-    for shift in piece_order(count):
-        pairs = [(i, int(partner(i, shift, count))) for i in range(count)]
-        received[shift] = lax.ppermute(pieces[shift], "gz", pairs)
+    for shift in range(count - 1, 0, -1):
+        received[shift] = paired(pieces[shift], shift)
 
     sub_final, cat_final = call(
         place_kernel,
@@ -597,11 +647,11 @@
         2,
         name="place",
         out_shape=(f32(depth, rows, columns), f32(depth, rows, columns)),
-        in_specs=[VMEM, VMEM, HBM, HBM],
+        in_specs=[VMEM, VMEM, VMEM, HBM, HBM],
         out_specs=(HBM, HBM),
-        input_output_aliases={2: 0, 3: 1},
-        scratch_shapes=[pltpu.SemaphoreType.DMA((8,))],
-    )(ring_planes, outer, sub_part, cat_part)
+        input_output_aliases={3: 0, 4: 1},
+        scratch_shapes=[pltpu.SemaphoreType.DMA((16,))],
+    )(ring_planes, inner_rows, outer_rows, sub_part, cat_part)
 
     image = call(
         shade_kernel,
@@ -609,16 +659,11 @@
         4,
         name="shade",
         out_shape=f32(4, rows, wide),
-        in_specs=[VMEM] * (1 + count),
+        in_specs=[VMEM] * (2 + count),
         out_specs=VMEM,
         scratch_shapes=[pltpu.VMEM((count, 3, rows, wide), jnp.float32)],
-    )(values, *received)
+    )(values, half_piece, *received)
     return sub_final, cat_final, image
-
-
-def piece_order(count):
-    half = count // 2
-    return [half] + [shift for shift in range(count - 1, 0, -1) if shift != half]
 
 
 def solution(mesh):

time: 42.7 us -> 43.7 us (1.023)
  starting transfers between devices: 16.7 us -> 17.2 us
    ppermute x3 -> x4, starting transfers between devices: 3.55 us -> 4.06 us  [paired(): lax.ppermute(piece, 'gz', [(i, int(partner(i, shift, count))) for i in ra...]
    ppermute x3 -> x4, waiting for transfers between devices: 2.07 us -> 2.49 us  [paired(): lax.ppermute(piece, 'gz', [(i, int(partner(i, shift, count))) for i in ra...]
  transfers between devices with their start and end apart: 11 -> 12, of which waited for: 5 -> 4; matrix products, arithmetic and copies ran while one was open for 0% -> 0% of each run, Pallas kernels for 32% -> 31%
where the time goes in v7:
time: 43.7 us; the launch traced here: 43.5 us
  starting transfers between devices  17.2 us (39%)
  Pallas kernels  15 us (34%)
  waiting for transfers between devices  7.27 us (17%)
  local copies, waits for them, and re-layouts  3.19 us (7%)
  between operations  0.78 us (2%)
    ppermute x8, starting transfers between devices, shifted(): return lax.ppermute(x, axis, ring(lax.axis_size(axis), shift))  13.1 us
    ppermute x8, waiting for transfers between devices, shifted(): return lax.ppermute(x, axis, ring(lax.axis_size(axis), shift))  4.77 us
    ppermute x4, starting transfers between devices, paired(): lax.ppermute(piece, 'gz', [(i, int(partner(i, shift, count))) for i in ra...  4.06 us
    pallas_call x1, Pallas kernels, body(): call(second_kernel, 1 << 25, 10, name='second', out_shape=(f32(depth, row...  4.02 us
    unnamed x12, local copies, waits for them, and re-layouts  3.19 us
    pallas_call x1, Pallas kernels, body(): call(center_kernel, 1 << 24, 4, name='center', out_shape=(f32(depth, rows...  2.98 us
    pallas_call x1, Pallas kernels, body(): call(first_kernel, 1 << 24, 2, name='first', out_shape=f32(2, depth, rows...  2.95 us
    ppermute x4, waiting for transfers between devices, paired(): lax.ppermute(piece, 'gz', [(i, int(partner(i, shift, count))) for i in ra...  2.49 us
  transfers between devices with their start and end apart: 12, of which 4 were waited for; matrix products, arithmetic and copies ran while one was open for 0% of the time, Pallas kernels for 31%

profile of v7, /device:TPU:0, one launch (start us, length us, event | category | flops | bytes accessed | tf_op | source)
XLA Modules:
  0.0 43.5 jit_solution(9264075704513569144)
XLA Ops:
  0.6 0.0 copy-start
  0.6 1.6 %copy-done = f32[16,32,1024]{2,1,0:T(8,128)S(1)} copy-done((f32[16,32,1024]{2,1,0:T(8,128)S(1)}, f32[16,32,1024]{2,1,0:T(8,128)}, u32[]{:S(2)}) %copy-start) | copy-done | bytes 2097176
  2.2 0.0 copy-start.2
  2.2 1.6 %copy-done.2 = f32[16,32,1024]{2,1,0:T(8,128)S(1)} copy-done((f32[16,32,1024]{2,1,0:T(8,128)S(1)}, f32[16,32,1024]{2,1,0:T(8,128)}, u32[]{:S(2)}) %copy-start.2) | copy-done | bytes 2097176
  3.8 0.5 %prepare.1 = (f32[2,2,16,1024]{3,2,1,0:T(8,128)S(1)}, f32[2,2,16,1024]{3,2,1,0:T(8,128)S(1)}, f32[2,16,1024]{2,1,0:T(8,128)S(1)}, f32[2,16,1024]{2,1,0:T(8,128)S...) custom-call(f32[16,32,1024]{2,1,0:T(8,128)S(1)} %copy-done, f32[16,32,1024]{2,1,0:T(8,128)S(1)} %copy-done.2), custom_call_target="tpu_custom_call" | custom-call | flops 4194304 | bytes 65536 | tf_op jit(solution)/shard_map/prepare/pallas_call | solution.py:516
  4.3 0.5 %collective-permute-start.2 = (f32[2,2,16,1024]{3,2,1,0:T(8,128)S(1)}, f32[2,2,16,1024]{3,2,1,0:T(8,128)S(1)}, u32[]{:S(2)}, u32[]{:S(2)}) collective-permute-start(f32[2,2,16,1024]{3,2,1,0:T(8,128)S(1)} %get-tuple-element.45.own_high), channel_id=1, source_target_pairs={{0,1},{1,2},{2,3},{3,4},{4,5},{5,6},{6,7},{7,0},{8,9},{9,10},{10,1... | collective-permute-start | bytes 786440 | tf_op jit(solution)/shard_map/ppermute | solution.py:501
  4.8 0.0 copy-start.4
  4.8 0.0 copy-start.5
  4.8 0.0 copy-start.1
  4.8 0.0 copy-start.3
  4.8 4.1 %collective-permute-start.3 = (f32[2,2,16,1024]{3,2,1,0:T(8,128)S(1)}, f32[2,2,16,1024]{3,2,1,0:T(8,128)S(1)}, u32[]{:S(2)}, u32[]{:S(2)}) collective-permute-start(f32[2,2,16,1024]{3,2,1,0:T(8,128)S(1)} %get-tuple-element.46.own_low), channel_id=1, source_target_pairs={{0,7},{1,0},{2,1},{3,2},{4,3},{5,4},{6,5},{7,6},{8,15},{9,8},{10,9... | collective-permute-start | bytes 786440 | tf_op jit(solution)/shard_map/ppermute | solution.py:501
  9.0 1.1 %planes.1 = (f32[2,32,1024]{2,1,0:T(8,128)S(1)}, f32[2,32,1024]{2,1,0:T(8,128)S(1)}) custom-call(f32[16,32,1024]{2,1,0:T(8,128)} %sub.5, f32[16,32,1024]{2,1,0:T(8,128)} %cat.5), custom_call_target="tpu_custom_call" | custom-call | flops 1048576 | bytes 65536 | tf_op jit(solution)/shard_map/planes/pallas_call | solution.py:503
  10.1 2.0 %collective-permute-start = (f32[2,32,1024]{2,1,0:T(8,128)S(1)}, f32[2,32,1024]{2,1,0:T(8,128)S(1)}, u32[]{:S(2)}, u32[]{:S(2)}) collective-permute-start(f32[2,32,1024]{2,1,0:T(8,128)S(1)} %get-tuple-element.39.up), channel_id=1, source_target_pairs={{0,8},{8,16},{16,24},{24,0},{1,9},{9,17},{17,25},{25,1},{2,10},{10... | collective-permute-start | bytes 786440 | tf_op jit(solution)/shard_map/ppermute | solution.py:501
  12.1 1.0 %collective-permute-start.1 = (f32[2,32,1024]{2,1,0:T(8,128)S(1)}, f32[2,32,1024]{2,1,0:T(8,128)S(1)}, u32[]{:S(2)}, u32[]{:S(2)}) collective-permute-start(f32[2,32,1024]{2,1,0:T(8,128)S(1)} %get-tuple-element.40.down), channel_id=1, source_target_pairs={{0,24},{8,0},{16,8},{24,16},{1,25},{9,1},{17,9},{25,17},{2,26},{10... | collective-permute-start | bytes 786440 | tf_op jit(solution)/shard_map/ppermute | solution.py:501
  13.1 1.0 %collective-permute-start.4 = (f32[2,16,1024]{2,1,0:T(8,128)S(1)}, f32[2,16,1024]{2,1,0:T(8,128)S(1)}, u32[]{:S(2)}, u32[]{:S(2)}) collective-permute-start(f32[2,16,1024]{2,1,0:T(8,128)S(1)} %get-tuple-element.41.q_up), channel_id=1, source_target_pairs={{0,8},{8,16},{16,24},{24,0},{1,9},{9,17},{17,25},{25,1},{2,10},{10... | collective-permute-start | bytes 393224 | tf_op jit(solution)/shard_map/ppermute | solution.py:501
  14.1 0.0 collective-permute-done.2.from_low
  14.1 2.4 %collective-permute-start.5 = (f32[2,16,1024]{2,1,0:T(8,128)S(1)}, f32[2,16,1024]{2,1,0:T(8,128)S(1)}, u32[]{:S(2)}, u32[]{:S(2)}) collective-permute-start(f32[2,16,1024]{2,1,0:T(8,128)S(1)} %get-tuple-element.42.q_down), channel_id=1, source_target_pairs={{0,24},{8,0},{16,8},{24,16},{1,25},{9,1},{17,9},{25,17},{2,26},{10... | collective-permute-start | bytes 393224 | tf_op jit(solution)/shard_map/ppermute | solution.py:501
  16.5 0.0 collective-permute-done.3.from_high
  16.5 0.1 collective-permute-start.6
  16.6 3.6 %collective-permute-done.p_low = f32[2,32,1024]{2,1,0:T(8,128)S(1)} collective-permute-done((f32[2,32,1024]{2,1,0:T(8,128)S(1)}, f32[2,32,1024]{2,1,0:T(8,128)S(1)}, u32[]{:S(2)}, u32[]{:S(2)}) %collective-permute-start) | collective-permute-done | bytes 262176 | tf_op jit(solution)/shard_map/ppermute | solution.py:501
  20.2 2.0 %collective-permute-start.7 = (f32[2,16,1024]{2,1,0:T(8,128)S(1)}, f32[2,16,1024]{2,1,0:T(8,128)S(1)}, u32[]{:S(2)}, u32[]{:S(2)}) collective-permute-start(f32[2,16,1024]{2,1,0:T(8,128)S(1)} %get-tuple-element.63), channel_id=1, source_target_pairs={{0,24},{8,0},{16,8},{24,16},{1,25},{9,1},{17,9},{25,17},{2,26},{10... | collective-permute-start | bytes 393224 | tf_op jit(solution)/shard_map/ppermute | solution.py:501
  22.2 0.0 copy-done.4
  22.2 0.0 copy-done.5
  22.2 0.6 %scalars.1.values = f32[8,8,128]{2,1,0:T(8,128)S(1)} custom-call(f32[2]{0:T(128)S(1)} %copy-done.5, f32[2,3]{1,0:T(2,128)S(1)} %bitcast.1), custom_call_target="tpu_custom_call" | custom-call | flops 262144 | bytes 65536 | tf_op jit(solution)/shard_map/scalars/pallas_call | solution.py:539
  22.8 0.0 copy-done.1
  22.8 0.0 copy-done.3
  22.8 3.0 %first.1.mid = f32[2,16,32,1024]{3,2,1,0:T(8,128)S(1)} custom-call(f32[16,32,1024]{2,1,0:T(8,128)S(1)} %copy-done.1, f32[16,32,1024]{2,1,0:T(8,128)S(1)} %copy-done.3), custom_call_target="tpu_custom_call" | custom-call | flops 16777216 | bytes 65536 | tf_op jit(solution)/shard_map/first/pallas_call | solution.py:530
  25.8 3.0 %center.1 = (f32[16,32,1024]{2,1,0:T(8,128)}, f32[16,32,1024]{2,1,0:T(8,128)}, f32[3,32,1024]{2,1,0:T(8,128)S(1)}) custom-call(f32[8,8,128]{2,1,0:T(8,128)S(1)} %scalars.1.values, f32[2,16,32,1024]{3,2,1,0:T(8,128)S(1)} %first.1.mid), custom_call_target="tpu_custom_call" | custom-call | flops 16777216 | bytes 65536 | tf_op jit(solution)/shard_map/center/pallas_call | solution.py:549
  28.8 4.0 %second.1 = (f32[16,32,1024]{2,1,0:T(8,128)}, f32[16,32,1024]{2,1,0:T(8,128)}, f32[3,32,1024]{2,1,0:T(8,128)S(1)}, f32[2,3,32,1024]{3,2,1,0:T(8,128)S(1)}, f32[2...) custom-call(f32[8,8,128]{2,1,0:T(8,128)S(1)} %scalars.1.values, ...), custom_call_target="tpu_custom_call", output_to_operand_aliasing={{0}: (11, {}), {1}: (12, {})} | custom-call | flops 33554432 | bytes 65536 | tf_op jit(solution)/shard_map/second/pallas_call | solution.py:575
  32.8 0.0 collective-permute-done.1.p_high
  32.8 0.8 %rim.1 = (f32[2,2,32,1024]{3,2,1,0:T(8,128)S(1)}, f32[2,2,32,1024]{3,2,1,0:T(8,128)S(1)}, f32[3,32,1024]{2,1,0:T(8,128)S(1)}) custom-call(f32[8,8,128]{2,1,0:T(8,128)S(1)} %scalars.1.values, f32[2,32,1024]{2,1,0:T(8,128)S(1)} %collective-permute-done.p_low, f32[2,32,1024]{2,1,0:T(8,128)S(1)} %collective-permute-done.1.p_high, ...), custom_call_target="tpu_custom_call" | custom-call | flops 8388608 | bytes 65536 | tf_op jit(solution)/shard_map/rim/pallas_call | solution.py:601
  33.7 0.0 collective-permute-done.4.q_low
  33.7 0.0 collective-permute-done.5.q_high
  33.7 0.1 most.1
  33.8 0.0 collective-permute-done.6.r_low
  33.8 1.2 %collective-permute-done.7.r_high = f32[2,16,1024]{2,1,0:T(8,128)S(1)} collective-permute-done((f32[2,16,1024]{2,1,0:T(8,128)S(1)}, f32[2,16,1024]{2,1,0:T(8,128)S(1)}, u32[]{:S(2)}, u32[]{:S(2)}) %collective-permute-start.7) | collective-permute-done | bytes 131104 | tf_op jit(solution)/shard_map/ppermute | solution.py:501
  34.9 0.1 last.1
  35.1 1.5 %collective-permute-start.11 = (f32[3,32,256]{2,1,0:T(8,128)S(1)}, f32[3,32,256]{2,1,0:T(8,128)S(1)}, u32[]{:S(2)}, u32[]{:S(2)}) collective-permute-start(f32[3,32,256]{2,1,0:T(8,128)S(1)} %get-tuple-element.74), channel_id=1, source_target_pairs={{0,24},{8,16},{16,8},{24,0},{1,25},{9,17},{17,9},{25,1},{2,26},{10... | collective-permute-start | bytes 294920 | tf_op jit(solution)/shard_map/ppermute | solution.py:624
  36.6 0.5 %collective-permute-start.9 = (f32[3,32,256]{2,1,0:T(8,128)S(1)}, f32[3,32,256]{2,1,0:T(8,128)S(1)}, u32[]{:S(2)}, u32[]{:S(2)}) collective-permute-start(f32[3,32,256]{2,1,0:T(8,128)S(1)} %get-tuple-element.72), channel_id=1, source_target_pairs={{0,8},{8,0},{16,24},{24,16},{1,9},{9,1},{17,25},{25,17},{2,10},{10... | collective-permute-start | bytes 294920 | tf_op jit(solution)/shard_map/ppermute | solution.py:624
  37.1 1.5 %collective-permute-start.8 = (f32[3,16,256]{2,1,0:T(8,128)S(1)}, f32[3,16,256]{2,1,0:T(8,128)S(1)}, u32[]{:S(2)}, u32[]{:S(2)}) collective-permute-start(f32[3,16,256]{2,1,0:T(8,128)S(1)} %get-tuple-element.70), channel_id=1, source_target_pairs={{0,16},{8,24},{16,0},{24,8},{1,17},{9,25},{17,1},{25,9},{2,18},{10... | collective-permute-start | bytes 147464 | tf_op jit(solution)/shard_map/ppermute | solution.py:624
  38.6 0.5 %collective-permute-start.10 = (f32[3,16,256]{2,1,0:T(8,128)S(1)}, f32[3,16,256]{2,1,0:T(8,128)S(1)}, u32[]{:S(2)}, u32[]{:S(2)}) collective-permute-start(f32[3,16,256]{2,1,0:T(8,128)S(1)} %get-tuple-element.73), channel_id=1, source_target_pairs={{0,16},{8,24},{16,0},{24,8},{1,17},{9,25},{17,1},{25,9},{2,18},{10... | collective-permute-start | bytes 147464 | tf_op jit(solution)/shard_map/ppermute | solution.py:624
  39.1 1.1 %place.1 = (f32[16,32,1024]{2,1,0:T(8,128)}, f32[16,32,1024]{2,1,0:T(8,128)}) custom-call(f32[2,2,32,1024]{3,2,1,0:T(8,128)S(1)} %get-tuple-element.58.ring, f32[2,2,16,1024]{3,2,1,0:T(8,128)S(1)} %get-tuple-element.61.inner, f32[2,2,16,1024]{3,2,1,0:T(8,128)S(1)} %get-tuple-element.65.outer, ...), custom_call_target="tpu_custom_call", output_to_operand_aliasing={{0}: (3, {}), {1}: (4, {})} | custom-call | flops 4194304 | bytes 65536 | tf_op jit(solution)/shard_map/place/pallas_call | solution.py:644
  40.2 1.0 %collective-permute-done.8.half = f32[3,16,256]{2,1,0:T(8,128)S(1)} collective-permute-done((f32[3,16,256]{2,1,0:T(8,128)S(1)}, f32[3,16,256]{2,1,0:T(8,128)S(1)}, u32[]{:S(2)}, u32[]{:S(2)}) %collective-permute-start.8) | collective-permute-done | bytes 49184 | tf_op jit(solution)/shard_map/ppermute | solution.py:624
  41.2 1.5 %collective-permute-done.10.pieces_and_rest_2_ = f32[3,16,256]{2,1,0:T(8,128)S(1)} collective-permute-done((f32[3,16,256]{2,1,0:T(8,128)S(1)}, f32[3,16,256]{2,1,0:T(8,128)S(1)}, u32[]{:S(2)}, u32[]{:S(2)}) %collective-permute-start.10) | collective-permute-done | bytes 49184 | tf_op jit(solution)/shard_map/ppermute | solution.py:624
  42.7 0.0 collective-permute-done.11.pieces_and_rest_3_
  42.7 0.0 collective-permute-done.9.pieces_and_rest_1_
  42.7 0.7 %shade.1 = f32[4,32,256]{2,1,0:T(8,128)} custom-call(f32[8,8,128]{2,1,0:T(8,128)S(1)} %scalars.1.values, f32[3,16,256]{2,1,0:T(8,128)S(1)} %collective-permute-done.8.half, f32[3,32,256]{2,1,0:T(8,128)S(1)} %get-tuple-element.71.pieces_and_rest_0_, f32[3,32,256]{2,1,0:T(8,128)S(1)} %collective-permute-done.9.pieces_and_rest_1_, ...), custom_call_target="tpu_custom_call" | custom-call | flops 1048576 | bytes 65536 | tf_op jit(solution)/shard_map/shade/pallas_call | solution.py:656
  (1 shorter events, 0.0 us)
Async XLA Ops:
  0.6 1.6 %copy-start = (f32[16,32,1024]{2,1,0:T(8,128)S(1)}, f32[16,32,1024]{2,1,0:T(8,128)}, u32[]{:S(2)}) copy-start(f32[16,32,1024]{2,1,0:T(8,128)} %sub.5) | copy-start | bytes 6291460
  2.2 1.6 %copy-start.2 = (f32[16,32,1024]{2,1,0:T(8,128)S(1)}, f32[16,32,1024]{2,1,0:T(8,128)}, u32[]{:S(2)}) copy-start(f32[16,32,1024]{2,1,0:T(8,128)} %cat.5) | copy-start | bytes 6291460
  4.3 9.8 %collective-permute-start.2 = (f32[2,2,16,1024]{3,2,1,0:T(8,128)S(1)}, f32[2,2,16,1024]{3,2,1,0:T(8,128)S(1)}, u32[]{:S(2)}, u32[]{:S(2)}) collective-permute-start(f32[2,2,16,1024]{3,2,1,0:T(8,128)S(1)} %get-tuple-element.45.own_high), channel_id=1, source_target_pairs={{0,1},{1,2},{2,3},{3,4},{4,5},{5,6},{6,7},{7,0},{8,9},{9,10},{10,1... | collective-permute-start | bytes 786440 | tf_op jit(solution)/shard_map/ppermute | solution.py:501
  4.8 17.4 %copy-start.4 = (f32[3,2]{0,1:T(2,128)S(1)}, f32[3,2]{0,1:T(2,128)}, u32[]{:S(2)}) copy-start(f32[3,2]{0,1:T(2,128)} %param.7) | copy-start | bytes 76
  4.8 17.4 %copy-start.5 = (f32[2]{0:T(128)S(1)}, f32[2]{0:T(128)}, u32[]{:S(2)}) copy-start(f32[2]{0:T(128)} %scale.1) | copy-start | bytes 28
  4.8 18.0 %copy-start.1 = (f32[16,32,1024]{2,1,0:T(8,128)S(1)}, f32[16,32,1024]{2,1,0:T(8,128)}, u32[]{:S(2)}) copy-start(f32[16,32,1024]{2,1,0:T(8,128)} %sub.5) | copy-start | bytes 6291460
  4.8 18.0 %copy-start.3 = (f32[16,32,1024]{2,1,0:T(8,128)S(1)}, f32[16,32,1024]{2,1,0:T(8,128)}, u32[]{:S(2)}) copy-start(f32[16,32,1024]{2,1,0:T(8,128)} %cat.5) | copy-start | bytes 6291460
  4.8 11.7 %collective-permute-start.3 = (f32[2,2,16,1024]{3,2,1,0:T(8,128)S(1)}, f32[2,2,16,1024]{3,2,1,0:T(8,128)S(1)}, u32[]{:S(2)}, u32[]{:S(2)}) collective-permute-start(f32[2,2,16,1024]{3,2,1,0:T(8,128)S(1)} %get-tuple-element.46.own_low), channel_id=1, source_target_pairs={{0,7},{1,0},{2,1},{3,2},{4,3},{5,4},{6,5},{7,6},{8,15},{9,8},{10,9... | collective-permute-start | bytes 786440 | tf_op jit(solution)/shard_map/ppermute | solution.py:501
  10.1 10.1 %collective-permute-start = (f32[2,32,1024]{2,1,0:T(8,128)S(1)}, f32[2,32,1024]{2,1,0:T(8,128)S(1)}, u32[]{:S(2)}, u32[]{:S(2)}) collective-permute-start(f32[2,32,1024]{2,1,0:T(8,128)S(1)} %get-tuple-element.39.up), channel_id=1, source_target_pairs={{0,8},{8,16},{16,24},{24,0},{1,9},{9,17},{17,25},{25,1},{2,10},{10... | collective-permute-start | bytes 786440 | tf_op jit(solution)/shard_map/ppermute | solution.py:501
  12.1 20.7 %collective-permute-start.1 = (f32[2,32,1024]{2,1,0:T(8,128)S(1)}, f32[2,32,1024]{2,1,0:T(8,128)S(1)}, u32[]{:S(2)}, u32[]{:S(2)}) collective-permute-start(f32[2,32,1024]{2,1,0:T(8,128)S(1)} %get-tuple-element.40.down), channel_id=1, source_target_pairs={{0,24},{8,0},{16,8},{24,16},{1,25},{9,1},{17,9},{25,17},{2,26},{10... | collective-permute-start | bytes 786440 | tf_op jit(solution)/shard_map/ppermute | solution.py:501
  13.1 20.5 %collective-permute-start.4 = (f32[2,16,1024]{2,1,0:T(8,128)S(1)}, f32[2,16,1024]{2,1,0:T(8,128)S(1)}, u32[]{:S(2)}, u32[]{:S(2)}) collective-permute-start(f32[2,16,1024]{2,1,0:T(8,128)S(1)} %get-tuple-element.41.q_up), channel_id=1, source_target_pairs={{0,8},{8,16},{16,24},{24,0},{1,9},{9,17},{17,25},{25,1},{2,10},{10... | collective-permute-start | bytes 393224 | tf_op jit(solution)/shard_map/ppermute | solution.py:501
  14.1 19.5 %collective-permute-start.5 = (f32[2,16,1024]{2,1,0:T(8,128)S(1)}, f32[2,16,1024]{2,1,0:T(8,128)S(1)}, u32[]{:S(2)}, u32[]{:S(2)}) collective-permute-start(f32[2,16,1024]{2,1,0:T(8,128)S(1)} %get-tuple-element.42.q_down), channel_id=1, source_target_pairs={{0,24},{8,0},{16,8},{24,16},{1,25},{9,1},{17,9},{25,17},{2,26},{10... | collective-permute-start | bytes 393224 | tf_op jit(solution)/shard_map/ppermute | solution.py:501
  16.5 17.2 %collective-permute-start.6 = (f32[2,16,1024]{2,1,0:T(8,128)S(1)}, f32[2,16,1024]{2,1,0:T(8,128)S(1)}, u32[]{:S(2)}, u32[]{:S(2)}) collective-permute-start(f32[2,16,1024]{2,1,0:T(8,128)S(1)} %get-tuple-element.62), channel_id=1, source_target_pairs={{0,8},{8,16},{16,24},{24,0},{1,9},{9,17},{17,25},{25,1},{2,10},{10... | collective-permute-start | bytes 393224 | tf_op jit(solution)/shard_map/ppermute | solution.py:501
  20.2 14.7 %collective-permute-start.7 = (f32[2,16,1024]{2,1,0:T(8,128)S(1)}, f32[2,16,1024]{2,1,0:T(8,128)S(1)}, u32[]{:S(2)}, u32[]{:S(2)}) collective-permute-start(f32[2,16,1024]{2,1,0:T(8,128)S(1)} %get-tuple-element.63), channel_id=1, source_target_pairs={{0,24},{8,0},{16,8},{24,16},{1,25},{9,1},{17,9},{25,17},{2,26},{10... | collective-permute-start | bytes 393224 | tf_op jit(solution)/shard_map/ppermute | solution.py:501
  35.1 7.6 %collective-permute-start.11 = (f32[3,32,256]{2,1,0:T(8,128)S(1)}, f32[3,32,256]{2,1,0:T(8,128)S(1)}, u32[]{:S(2)}, u32[]{:S(2)}) collective-permute-start(f32[3,32,256]{2,1,0:T(8,128)S(1)} %get-tuple-element.74), channel_id=1, source_target_pairs={{0,24},{8,16},{16,8},{24,0},{1,25},{9,17},{17,9},{25,1},{2,26},{10... | collective-permute-start | bytes 294920 | tf_op jit(solution)/shard_map/ppermute | solution.py:624
  36.6 6.1 %collective-permute-start.9 = (f32[3,32,256]{2,1,0:T(8,128)S(1)}, f32[3,32,256]{2,1,0:T(8,128)S(1)}, u32[]{:S(2)}, u32[]{:S(2)}) collective-permute-start(f32[3,32,256]{2,1,0:T(8,128)S(1)} %get-tuple-element.72), channel_id=1, source_target_pairs={{0,8},{8,0},{16,24},{24,16},{1,9},{9,1},{17,25},{25,17},{2,10},{10... | collective-permute-start | bytes 294920 | tf_op jit(solution)/shard_map/ppermute | solution.py:624
  37.1 4.1 %collective-permute-start.8 = (f32[3,16,256]{2,1,0:T(8,128)S(1)}, f32[3,16,256]{2,1,0:T(8,128)S(1)}, u32[]{:S(2)}, u32[]{:S(2)}) collective-permute-start(f32[3,16,256]{2,1,0:T(8,128)S(1)} %get-tuple-element.70), channel_id=1, source_target_pairs={{0,16},{8,24},{16,0},{24,8},{1,17},{9,25},{17,1},{25,9},{2,18},{10... | collective-permute-start | bytes 147464 | tf_op jit(solution)/shard_map/ppermute | solution.py:624
  38.6 4.1 %collective-permute-start.10 = (f32[3,16,256]{2,1,0:T(8,128)S(1)}, f32[3,16,256]{2,1,0:T(8,128)S(1)}, u32[]{:S(2)}, u32[]{:S(2)}) collective-permute-start(f32[3,16,256]{2,1,0:T(8,128)S(1)} %get-tuple-element.73), channel_id=1, source_target_pairs={{0,16},{8,24},{16,0},{24,8},{1,17},{9,25},{17,1},{25,9},{2,18},{10... | collective-permute-start | bytes 147464 | tf_op jit(solution)/shard_map/ppermute | solution.py:624

commit v8 on v7

--- a/solution.py
+++ b/solution.py
@@ -113,17 +113,15 @@
     return weight * sub, weight * cat, clear * keep
 
 
-def scalars_kernel(share, scale, emission, values):
-    shape = values.shape[1:]
-    for s in range(2):
-        values[s] = jnp.full(shape, scale[s] * share, jnp.float32)
-        for channel in range(3):
-            values[2 + channel * 2 + s] = jnp.full(shape, emission[s, channel], jnp.float32)
-
-
-def first_kernel(sub, cat, mid):
+def first_kernel(share, scale_hbm, emission_hbm, sub, cat, mid, values, scale, emission, sems):
     depth, rows, _ = sub.shape
     old = (sub, cat)
+    copies = [
+        pltpu.make_async_copy(scale_hbm, scale, sems.at[0]),
+        pltpu.make_async_copy(emission_hbm, emission, sems.at[1]),
+    ]
+    for copy in copies:
+        copy.start()
 
     @pl.loop(1, depth - 1)
     def _(k):
@@ -139,6 +137,14 @@
             lambda s, tile: old[s][k - 1, span(tile), :] + old[s][k + 1, span(tile), :],
             store,
         )
+
+    for copy in copies:
+        copy.wait()
+    shape = values.shape[1:]
+    for s in range(2):
+        values[s] = jnp.full(shape, scale[s] * share, jnp.float32)
+        for channel in range(3):
+            values[2 + channel * 2 + s] = jnp.full(shape, emission[s, channel], jnp.float32)
 
 
 def image_step(k, load, tiles, only, low_rows, high_rows, scales, seen, keep):
@@ -167,16 +173,10 @@
     seen[2] = jnp.ones(seen.shape[1:], jnp.float32)
 
 
-def center_kernel(values, mid, sub_out, cat_out, seen, new, sem_out):
-    depth, rows, columns = sub_out.shape
-    outputs = (sub_out, cat_out)
+def center_kernel(values, mid, new, seen):
+    depth, rows, columns = mid.shape[1:]
     tiles = rows // ROWS
     scales = across_columns(values[0], columns), across_columns(values[1], columns)
-    inside = pl.ds(ROWS, rows - 2 * ROWS)
-
-    def put(s, k):
-        return pltpu.make_async_copy(new.at[s, k], outputs[s].at[k, inside], sem_out.at[s, k])
-
     clear_image(seen)
 
     @pl.loop(2, depth - 2)
@@ -188,29 +188,23 @@
         image_step(
             k, lambda s, k, tile: mid[s, k, span(tile), :], tiles, range(1, tiles - 1), None, None, scales, seen, keep
         )
-        for s in range(2):
-            put(s, k).start()
-
-    @pl.loop(2, depth - 2)
-    def _(k):
-        for s in range(2):
-            put(s, k).wait()
 
 
 def second_kernel(
-    values, mid, q_up, q_down, r_up, r_down, from_low, from_high, own_low, own_high, center, sub_in, cat_in,
-    sub_out, cat_out, seen, near, far, rows_low, rows_high,
-    heads, tails, new, sem_out,
+    values, mid, q_up, q_down, r_up, r_down, from_low, from_high, own_low, own_high, center, done,
+    sub_out, cat_out, new, seen, near, far, rows_low, rows_high,
+    heads, tails, sems,
 ):
-    del sub_in, cat_in
     depth, rows, columns = sub_out.shape
-    outputs = (sub_out, cat_out)
     tiles = rows // ROWS
     scales = across_columns(values[0], columns), across_columns(values[1], columns)
-
-    def put(s, k, end):
-        at = pl.ds(end * (rows - ROWS), ROWS)
-        return pltpu.make_async_copy(new.at[s, end, k], outputs[s].at[k, at], sem_out.at[s, end, k])
+    planes = pl.ds(2, depth - 4)
+    copies = [
+        pltpu.make_async_copy(done.at[s, planes], out.at[planes, pl.ds(ROWS, rows - 2 * ROWS)], sems.at[s])
+        for s, out in enumerate((sub_out, cat_out))
+    ]
+    for copy in copies:
+        copy.start()
 
     which = lax.broadcasted_iota(jnp.int32, (depth, columns), 0)
     for got, at, own, at_own, out in (
@@ -288,15 +282,9 @@
             seen,
             keep,
         )
-        for s in range(2):
-            for end in range(2):
-                put(s, k, end).start()
-
-    @pl.loop(2, depth - 2)
-    def _(k):
-        for s in range(2):
-            for end in range(2):
-                put(s, k, end).wait()
+
+    for copy in copies:
+        copy.wait()
 
 
 def rows_kernel(r_up, r_down, from_low, from_high, up, down):
@@ -458,11 +446,15 @@
         image[3, at, :] = 1.0 - clear
 
 
-def place_kernel(ring, inner, outer, sub_in, cat_in, sub_out, cat_out, sems):
+def place_kernel(new, ring, inner, outer, sub_in, cat_in, sub_out, cat_out, sems):
     del sub_in, cat_in
     depth, rows, _ = sub_out.shape
+    planes = pl.ds(2, depth - 4)
     copies = []
     for s, out in enumerate((sub_out, cat_out)):
+        for end in range(2):
+            target = out.at[planes, pl.ds(end * (rows - ROWS), ROWS)]
+            copies.append(pltpu.make_async_copy(new.at[s, end, planes], target, sems.at[len(copies)]))
         for side in range(2):
             plane = side * (depth - 1)
             for source, target in (
@@ -527,37 +519,28 @@
     q_low = shifted(q_up, "gz", 1)
     q_high = shifted(q_down, "gz", -1)
 
-    mid = call(
-        first_kernel,
+    mid, values = call(
+        functools.partial(first_kernel, share),
         1 << 24,
         2,
         name="first",
-        out_shape=f32(2, depth, rows, columns),
-        in_specs=[VMEM, VMEM],
-        out_specs=VMEM,
-    )(substrate, catalyst)
-    values = call(
-        functools.partial(scalars_kernel, share),
-        1 << 18,
-        2,
-        name="scalars",
-        out_shape=f32(8, ROWS, LANES),
-        in_specs=[SMEM, SMEM],
-        out_specs=VMEM,
-    )(extinction, emission.T)
-
-    sub_part, cat_part, center = call(
+        out_shape=(f32(2, depth, rows, columns), f32(8, ROWS, LANES)),
+        in_specs=[HBM, HBM, VMEM, VMEM],
+        out_specs=(VMEM, VMEM),
+        scratch_shapes=[
+            pltpu.SMEM((2,), jnp.float32),
+            pltpu.SMEM((2, 3), jnp.float32),
+            pltpu.SemaphoreType.DMA((2,)),
+        ],
+    )(hbm(extinction), hbm(emission.T), substrate, catalyst)
+    done, center = call(
         center_kernel,
         1 << 24,
-        4,
+        2,
         name="center",
-        out_shape=(f32(depth, rows, columns), f32(depth, rows, columns), f32(3, rows, columns)),
+        out_shape=(f32(2, depth, middle, columns), f32(3, rows, columns)),
         in_specs=[VMEM, VMEM],
-        out_specs=(HBM, HBM, VMEM),
-        scratch_shapes=[
-            pltpu.VMEM((2, depth, middle, columns), jnp.float32),
-            pltpu.SemaphoreType.DMA((2, depth)),
-        ],
+        out_specs=(VMEM, VMEM),
     )(values, mid)
 
     m_up, m_down = call(
@@ -572,30 +555,29 @@
     r_low = shifted(m_up, "gz", 1)
     r_high = shifted(m_down, "gz", -1)
 
-    sub_part, cat_part, inner, near, far, rows_low, rows_high = call(
+    sub_part, cat_part, new, inner, near, far, rows_low, rows_high = call(
         second_kernel,
         1 << 25,
-        10,
+        4,
         name="second",
         out_shape=(
             f32(depth, rows, columns),
             f32(depth, rows, columns),
+            f32(2, 2, depth, ROWS, columns),
             f32(3, rows, columns),
             f32(2, 3, rows, columns),
             f32(2, 3, rows, columns),
             f32(2, depth, columns),
             f32(2, depth, columns),
         ),
-        in_specs=[VMEM] * 11 + [HBM, HBM],
-        out_specs=(HBM, HBM) + (VMEM,) * 5,
-        input_output_aliases={11: 0, 12: 1},
+        in_specs=[VMEM] * 12,
+        out_specs=(HBM, HBM) + (VMEM,) * 6,
         scratch_shapes=[
             pltpu.VMEM((2, depth, ROWS, columns), jnp.float32),
             pltpu.VMEM((2, depth, ROWS, columns), jnp.float32),
-            pltpu.VMEM((2, 2, depth, ROWS, columns), jnp.float32),
-            pltpu.SemaphoreType.DMA((2, 2, depth)),
+            pltpu.SemaphoreType.DMA((2,)),
         ],
-    )(values, mid, q_up, q_down, r_up, r_down, from_low, from_high, own_low, own_high, center, sub_part, cat_part)
+    )(values, mid, q_up, q_down, r_up, r_down, from_low, from_high, own_low, own_high, center, done)
 
     p_low, p_high, inner = lax.optimization_barrier((p_low, p_high, inner))
     ring_planes, known, seen = call(
@@ -647,11 +629,11 @@
         2,
         name="place",
         out_shape=(f32(depth, rows, columns), f32(depth, rows, columns)),
-        in_specs=[VMEM, VMEM, VMEM, HBM, HBM],
+        in_specs=[VMEM, VMEM, VMEM, VMEM, HBM, HBM],
         out_specs=(HBM, HBM),
-        input_output_aliases={3: 0, 4: 1},
-        scratch_shapes=[pltpu.SemaphoreType.DMA((16,))],
-    )(ring_planes, inner_rows, outer_rows, sub_part, cat_part)
+        input_output_aliases={4: 0, 5: 1},
+        scratch_shapes=[pltpu.SemaphoreType.DMA((20,))],
+    )(new, ring_planes, inner_rows, outer_rows, sub_part, cat_part)
 
     image = call(
         shade_kernel,

time: 43.7 us -> 43.6 us (level)
  Pallas kernels: 15 us -> 12.9 us
  waiting for transfers between devices: 7.27 us -> 9.3 us
    pallas_call x4 -> x3, Pallas kernels: 10.5 us -> 7.9 us  [the longest x1 3 us: body(): call(functools.partial(first_kernel, share), 1 << 24, 2, name='first', ou...]
    ppermute x8, waiting for transfers between devices: 4.77 us -> 7.36 us  [shifted(): return lax.ppermute(x, axis, ring(lax.axis_size(axis), shift))]
    ppermute x4, waiting for transfers between devices: 2.49 us -> 1.94 us  [paired(): lax.ppermute(piece, 'gz', [(i, int(partner(i, shift, count))) for i in ra...]
    pallas_call x1, Pallas kernels: 1.08 us -> 1.64 us  [body(): call(place_kernel, 1 << 22, 2, name='place', out_shape=(f32(depth, rows,...]
    unnamed x12 -> x8, local copies, waits for them, and re-layouts: 3.19 us -> 3.18 us
  transfers between devices with their start and end apart: 12 -> 12, of which waited for: 4 -> 6; matrix products, arithmetic and copies ran while one was open for 0% -> 0% of each run, Pallas kernels for 31% -> 27%
where the time goes in v8:
time: 43.6 us; the launch traced here: 43.4 us
  starting transfers between devices  17.2 us (39%)
  Pallas kernels  12.9 us (30%)
  waiting for transfers between devices  9.3 us (21%)
  local copies, waits for them, and re-layouts  3.18 us (7%)
  between operations  0.74 us (2%)
    ppermute x8, starting transfers between devices, shifted(): return lax.ppermute(x, axis, ring(lax.axis_size(axis), shift))  13.2 us
    ppermute x8, waiting for transfers between devices, shifted(): return lax.ppermute(x, axis, ring(lax.axis_size(axis), shift))  7.36 us
    ppermute x4, starting transfers between devices, paired(): lax.ppermute(piece, 'gz', [(i, int(partner(i, shift, count))) for i in ra...  4.06 us
    unnamed x8, local copies, waits for them, and re-layouts  3.18 us
    pallas_call x1, Pallas kernels, body(): call(functools.partial(first_kernel, share), 1 << 24, 2, name='first', ou...  3 us
    pallas_call x1, Pallas kernels, body(): call(second_kernel, 1 << 25, 4, name='second', out_shape=(f32(depth, rows...  2.84 us
    pallas_call x1, Pallas kernels, body(): call(center_kernel, 1 << 24, 2, name='center', out_shape=(f32(2, depth, m...  2.06 us
    ppermute x4, waiting for transfers between devices, paired(): lax.ppermute(piece, 'gz', [(i, int(partner(i, shift, count))) for i in ra...  1.94 us
  transfers between devices with their start and end apart: 12, of which 6 were waited for; matrix products, arithmetic and copies ran while one was open for 0% of the time, Pallas kernels for 27%

profile of v8, /device:TPU:0, one launch (start us, length us, event | category | flops | bytes accessed | tf_op | source)
XLA Modules:
  0.0 43.4 jit_solution(13957873440589893227)
XLA Ops:
  0.6 0.0 copy-start
  0.6 1.6 %copy-done = f32[16,32,1024]{2,1,0:T(8,128)S(1)} copy-done((f32[16,32,1024]{2,1,0:T(8,128)S(1)}, f32[16,32,1024]{2,1,0:T(8,128)}, u32[]{:S(2)}) %copy-start) | copy-done | bytes 2097176
  2.2 0.0 copy-start.2
  2.2 1.6 %copy-done.2 = f32[16,32,1024]{2,1,0:T(8,128)S(1)} copy-done((f32[16,32,1024]{2,1,0:T(8,128)S(1)}, f32[16,32,1024]{2,1,0:T(8,128)}, u32[]{:S(2)}) %copy-start.2) | copy-done | bytes 2097176
  3.8 0.5 %prepare.1 = (f32[2,2,16,1024]{3,2,1,0:T(8,128)S(1)}, f32[2,2,16,1024]{3,2,1,0:T(8,128)S(1)}, f32[2,16,1024]{2,1,0:T(8,128)S(1)}, f32[2,16,1024]{2,1,0:T(8,128)S...) custom-call(f32[16,32,1024]{2,1,0:T(8,128)S(1)} %copy-done, f32[16,32,1024]{2,1,0:T(8,128)S(1)} %copy-done.2), custom_call_target="tpu_custom_call" | custom-call | flops 4194304 | bytes 65536 | tf_op jit(solution)/shard_map/prepare/pallas_call | solution.py:508
  4.3 0.5 %collective-permute-start = (f32[2,2,16,1024]{3,2,1,0:T(8,128)S(1)}, f32[2,2,16,1024]{3,2,1,0:T(8,128)S(1)}, u32[]{:S(2)}, u32[]{:S(2)}) collective-permute-start(f32[2,2,16,1024]{3,2,1,0:T(8,128)S(1)} %get-tuple-element.47.own_high), channel_id=1, source_target_pairs={{0,1},{1,2},{2,3},{3,4},{4,5},{5,6},{6,7},{7,0},{8,9},{9,10},{10,1... | collective-permute-start | bytes 786440 | tf_op jit(solution)/shard_map/ppermute | solution.py:493
  4.8 0.0 copy-start.1
  4.8 0.0 copy-start.3
  4.8 4.1 %collective-permute-start.1 = (f32[2,2,16,1024]{3,2,1,0:T(8,128)S(1)}, f32[2,2,16,1024]{3,2,1,0:T(8,128)S(1)}, u32[]{:S(2)}, u32[]{:S(2)}) collective-permute-start(f32[2,2,16,1024]{3,2,1,0:T(8,128)S(1)} %get-tuple-element.48.own_low), channel_id=1, source_target_pairs={{0,7},{1,0},{2,1},{3,2},{4,3},{5,4},{6,5},{7,6},{8,15},{9,8},{10,9... | collective-permute-start | bytes 786440 | tf_op jit(solution)/shard_map/ppermute | solution.py:493
  8.9 1.1 %planes.1 = (f32[2,32,1024]{2,1,0:T(8,128)S(1)}, f32[2,32,1024]{2,1,0:T(8,128)S(1)}) custom-call(f32[16,32,1024]{2,1,0:T(8,128)} %sub.5, f32[16,32,1024]{2,1,0:T(8,128)} %cat.5), custom_call_target="tpu_custom_call" | custom-call | flops 1048576 | bytes 65536 | tf_op jit(solution)/shard_map/planes/pallas_call | solution.py:495
  10.1 2.0 %collective-permute-start.2 = (f32[2,32,1024]{2,1,0:T(8,128)S(1)}, f32[2,32,1024]{2,1,0:T(8,128)S(1)}, u32[]{:S(2)}, u32[]{:S(2)}) collective-permute-start(f32[2,32,1024]{2,1,0:T(8,128)S(1)} %get-tuple-element.52.up), channel_id=1, source_target_pairs={{0,8},{8,16},{16,24},{24,0},{1,9},{9,17},{17,25},{25,1},{2,10},{10... | collective-permute-start | bytes 786440 | tf_op jit(solution)/shard_map/ppermute | solution.py:493
  12.0 1.0 %collective-permute-start.3 = (f32[2,32,1024]{2,1,0:T(8,128)S(1)}, f32[2,32,1024]{2,1,0:T(8,128)S(1)}, u32[]{:S(2)}, u32[]{:S(2)}) collective-permute-start(f32[2,32,1024]{2,1,0:T(8,128)S(1)} %get-tuple-element.53.down), channel_id=1, source_target_pairs={{0,24},{8,0},{16,8},{24,16},{1,25},{9,1},{17,9},{25,17},{2,26},{10... | collective-permute-start | bytes 786440 | tf_op jit(solution)/shard_map/ppermute | solution.py:493
  13.1 1.0 %collective-permute-start.4 = (f32[2,16,1024]{2,1,0:T(8,128)S(1)}, f32[2,16,1024]{2,1,0:T(8,128)S(1)}, u32[]{:S(2)}, u32[]{:S(2)}) collective-permute-start(f32[2,16,1024]{2,1,0:T(8,128)S(1)} %get-tuple-element.43.q_up), channel_id=1, source_target_pairs={{0,8},{8,16},{16,24},{24,0},{1,9},{9,17},{17,25},{25,1},{2,10},{10... | collective-permute-start | bytes 393224 | tf_op jit(solution)/shard_map/ppermute | solution.py:493
  14.1 0.0 collective-permute-done.from_low
  14.1 2.5 %collective-permute-start.5 = (f32[2,16,1024]{2,1,0:T(8,128)S(1)}, f32[2,16,1024]{2,1,0:T(8,128)S(1)}, u32[]{:S(2)}, u32[]{:S(2)}) collective-permute-start(f32[2,16,1024]{2,1,0:T(8,128)S(1)} %get-tuple-element.44.q_down), channel_id=1, source_target_pairs={{0,24},{8,0},{16,8},{24,16},{1,25},{9,1},{17,9},{25,17},{2,26},{10... | collective-permute-start | bytes 393224 | tf_op jit(solution)/shard_map/ppermute | solution.py:493
  16.6 0.0 collective-permute-done.1.from_high
  16.6 0.1 collective-permute-start.6
  16.7 3.5 %collective-permute-done.2.p_low = f32[2,32,1024]{2,1,0:T(8,128)S(1)} collective-permute-done((f32[2,32,1024]{2,1,0:T(8,128)S(1)}, f32[2,32,1024]{2,1,0:T(8,128)S(1)}, u32[]{:S(2)}, u32[]{:S(2)}) %collective-permute-start.2) | collective-permute-done | bytes 262176 | tf_op jit(solution)/shard_map/ppermute | solution.py:493
  20.2 2.0 %collective-permute-start.7 = (f32[2,16,1024]{2,1,0:T(8,128)S(1)}, f32[2,16,1024]{2,1,0:T(8,128)S(1)}, u32[]{:S(2)}, u32[]{:S(2)}) collective-permute-start(f32[2,16,1024]{2,1,0:T(8,128)S(1)} %get-tuple-element.67), channel_id=1, source_target_pairs={{0,24},{8,0},{16,8},{24,16},{1,25},{9,1},{17,9},{25,17},{2,26},{10... | collective-permute-start | bytes 393224 | tf_op jit(solution)/shard_map/ppermute | solution.py:493
  22.2 0.0 copy-done.1
  22.2 0.0 copy-done.3
  22.2 3.0 %first.1 = (f32[2,16,32,1024]{3,2,1,0:T(8,128)S(1)}, f32[8,8,128]{2,1,0:T(8,128)S(1)}) custom-call(f32[2]{0:T(128)} %scale_hbm.1, f32[2,3]{1,0:T(2,128)} %bitcast.1, f32[16,32,1024]{2,1,0:T(8,128)S(1)} %copy-done.1, f32[16,32,1024]{2,1,0:T(8,128)S(1)} %copy-done.3), custom_call_target="tpu_custom_call" | custom-call | flops 16777216 | bytes 65536 | tf_op jit(solution)/shard_map/first/pallas_call | solution.py:522
  25.2 2.1 %center.1 = (f32[2,16,16,1024]{3,2,1,0:T(8,128)S(1)}, f32[3,32,1024]{2,1,0:T(8,128)S(1)}) custom-call(f32[8,8,128]{2,1,0:T(8,128)S(1)} %get-tuple-element.41.values, f32[2,16,32,1024]{3,2,1,0:T(8,128)S(1)} %get-tuple-element.42.mid), custom_call_target="tpu_custom_call" | custom-call | flops 16777216 | bytes 65536 | tf_op jit(solution)/shard_map/center/pallas_call | solution.py:536
  27.3 2.8 %second.1 = (f32[16,32,1024]{2,1,0:T(8,128)}, f32[16,32,1024]{2,1,0:T(8,128)}, f32[2,2,16,8,1024]{4,3,2,1,0:T(8,128)S(1)}, f32[3,32,1024]{2,1,0:T(8,128)S(1)}, f...) custom-call(f32[8,8,128]{2,1,0:T(8,128)S(1)} %get-tuple-element.41.v, ...), custom_call_target="tpu_custom_call" | custom-call | flops 33554432 | bytes 65536 | tf_op jit(solution)/shard_map/second/pallas_call | solution.py:558
  30.1 0.0 collective-permute-done.3.p_high
  30.1 0.8 %rim.1 = (f32[2,2,32,1024]{3,2,1,0:T(8,128)S(1)}, f32[2,2,32,1024]{3,2,1,0:T(8,128)S(1)}, f32[3,32,1024]{2,1,0:T(8,128)S(1)}) custom-call(f32[8,8,128]{2,1,0:T(8,128)S(1)} %get-tuple-element.41.values, f32[2,32,1024]{2,1,0:T(8,128)S(1)} %collective-permute-done.2.p_low, f32[2,32,1024]{2,1,0:T(8,128)S(1)} %collective-permute-done.3.p_high, ...), custom_call_target="tpu_custom_call" | custom-call | flops 8388608 | bytes 65536 | tf_op jit(solution)/shard_map/rim/pallas_call | solution.py:583
  30.9 0.0 collective-permute-done.4.q_low
  31.0 1.0 %collective-permute-done.5.q_high = f32[2,16,1024]{2,1,0:T(8,128)S(1)} collective-permute-done((f32[2,16,1024]{2,1,0:T(8,128)S(1)}, f32[2,16,1024]{2,1,0:T(8,128)S(1)}, u32[]{:S(2)}, u32[]{:S(2)}) %collective-permute-start.5) | collective-permute-done | bytes 131104 | tf_op jit(solution)/shard_map/ppermute | solution.py:493
  31.9 0.1 most.1
  32.0 1.4 %collective-permute-done.6.r_low = f32[2,16,1024]{2,1,0:T(8,128)S(1)} collective-permute-done((f32[2,16,1024]{2,1,0:T(8,128)S(1)}, f32[2,16,1024]{2,1,0:T(8,128)S(1)}, u32[]{:S(2)}, u32[]{:S(2)}) %collective-permute-start.6) | collective-permute-done | bytes 131104 | tf_op jit(solution)/shard_map/ppermute | solution.py:493
  33.4 1.5 %collective-permute-done.7.r_high = f32[2,16,1024]{2,1,0:T(8,128)S(1)} collective-permute-done((f32[2,16,1024]{2,1,0:T(8,128)S(1)}, f32[2,16,1024]{2,1,0:T(8,128)S(1)}, u32[]{:S(2)}, u32[]{:S(2)}) %collective-permute-start.7) | collective-permute-done | bytes 131104 | tf_op jit(solution)/shard_map/ppermute | solution.py:493
  34.9 0.1 last.1
  35.0 1.5 %collective-permute-start.11 = (f32[3,32,256]{2,1,0:T(8,128)S(1)}, f32[3,32,256]{2,1,0:T(8,128)S(1)}, u32[]{:S(2)}, u32[]{:S(2)}) collective-permute-start(f32[3,32,256]{2,1,0:T(8,128)S(1)} %get-tuple-element.78), channel_id=1, source_target_pairs={{0,24},{8,16},{16,8},{24,0},{1,25},{9,17},{17,9},{25,1},{2,26},{10... | collective-permute-start | bytes 294920 | tf_op jit(solution)/shard_map/ppermute | solution.py:606
  36.5 0.5 %collective-permute-start.9 = (f32[3,32,256]{2,1,0:T(8,128)S(1)}, f32[3,32,256]{2,1,0:T(8,128)S(1)}, u32[]{:S(2)}, u32[]{:S(2)}) collective-permute-start(f32[3,32,256]{2,1,0:T(8,128)S(1)} %get-tuple-element.76), channel_id=1, source_target_pairs={{0,8},{8,0},{16,24},{24,16},{1,9},{9,1},{17,25},{25,17},{2,10},{10... | collective-permute-start | bytes 294920 | tf_op jit(solution)/shard_map/ppermute | solution.py:606
  37.0 1.5 %collective-permute-start.8 = (f32[3,16,256]{2,1,0:T(8,128)S(1)}, f32[3,16,256]{2,1,0:T(8,128)S(1)}, u32[]{:S(2)}, u32[]{:S(2)}) collective-permute-start(f32[3,16,256]{2,1,0:T(8,128)S(1)} %get-tuple-element.74), channel_id=1, source_target_pairs={{0,16},{8,24},{16,0},{24,8},{1,17},{9,25},{17,1},{25,9},{2,18},{10... | collective-permute-start | bytes 147464 | tf_op jit(solution)/shard_map/ppermute | solution.py:606
  38.6 0.5 %collective-permute-start.10 = (f32[3,16,256]{2,1,0:T(8,128)S(1)}, f32[3,16,256]{2,1,0:T(8,128)S(1)}, u32[]{:S(2)}, u32[]{:S(2)}) collective-permute-start(f32[3,16,256]{2,1,0:T(8,128)S(1)} %get-tuple-element.77), channel_id=1, source_target_pairs={{0,16},{8,24},{16,0},{24,8},{1,17},{9,25},{17,1},{25,9},{2,18},{10... | collective-permute-start | bytes 147464 | tf_op jit(solution)/shard_map/ppermute | solution.py:606
  39.1 1.6 %place.1 = (f32[16,32,1024]{2,1,0:T(8,128)}, f32[16,32,1024]{2,1,0:T(8,128)}) custom-call(f32[2,2,16,8,1024]{4,3,2,1,0:T(8,128)S(1)} %get-tuple-element.51.new, f32[2,2,32,1024]{3,2,1,0:T(8,128)S(1)} %get-tuple-element.62.ring, f32[2,2,16,1024]{3,2,1,0:T(8,128)S(1)} %get-tuple-element.65.inner, ...), custom_call_target="tpu_custom_call", output_to_operand_aliasing={{0}: (4, {}), {1}: (5, {})} | custom-call | flops 4194304 | bytes 65536 | tf_op jit(solution)/shard_map/place/pallas_call | solution.py:626
  40.7 0.4 collective-permute-done.8.half
  41.1 1.5 %collective-permute-done.10.pieces_and_rest_2_ = f32[3,16,256]{2,1,0:T(8,128)S(1)} collective-permute-done((f32[3,16,256]{2,1,0:T(8,128)S(1)}, f32[3,16,256]{2,1,0:T(8,128)S(1)}, u32[]{:S(2)}, u32[]{:S(2)}) %collective-permute-start.10) | collective-permute-done | bytes 49184 | tf_op jit(solution)/shard_map/ppermute | solution.py:606
  42.6 0.0 collective-permute-done.11.pieces_and_rest_3_
  42.6 0.0 collective-permute-done.9.pieces_and_rest_1_
  42.6 0.7 %shade.1 = f32[4,32,256]{2,1,0:T(8,128)} custom-call(f32[8,8,128]{2,1,0:T(8,128)S(1)} %get-tuple-element.41.values, f32[3,16,256]{2,1,0:T(8,128)S(1)} %collective-permute-done.8.half, f32[3,32,256]{2,1,0:T(8,128)S(1)} %get-tuple-element.75.pieces_and_rest_0_, f32[3,32,256]{2,1,0:T(8,128)S(1)} %collective-permute-done.9.pieces_and_rest_1_, ...), custom_call_target="tpu_custom_call" | custom-call | flops 1048576 | bytes 65536 | tf_op jit(solution)/shard_map/shade/pallas_call | solution.py:638
  (1 shorter events, 0.0 us)
Async XLA Ops:
  0.6 1.6 %copy-start = (f32[16,32,1024]{2,1,0:T(8,128)S(1)}, f32[16,32,1024]{2,1,0:T(8,128)}, u32[]{:S(2)}) copy-start(f32[16,32,1024]{2,1,0:T(8,128)} %sub.5) | copy-start | bytes 6291460
  2.2 1.6 %copy-start.2 = (f32[16,32,1024]{2,1,0:T(8,128)S(1)}, f32[16,32,1024]{2,1,0:T(8,128)}, u32[]{:S(2)}) copy-start(f32[16,32,1024]{2,1,0:T(8,128)} %cat.5) | copy-start | bytes 6291460
  4.3 9.8 %collective-permute-start = (f32[2,2,16,1024]{3,2,1,0:T(8,128)S(1)}, f32[2,2,16,1024]{3,2,1,0:T(8,128)S(1)}, u32[]{:S(2)}, u32[]{:S(2)}) collective-permute-start(f32[2,2,16,1024]{3,2,1,0:T(8,128)S(1)} %get-tuple-element.47.own_high), channel_id=1, source_target_pairs={{0,1},{1,2},{2,3},{3,4},{4,5},{5,6},{6,7},{7,0},{8,9},{9,10},{10,1... | collective-permute-start | bytes 786440 | tf_op jit(solution)/shard_map/ppermute | solution.py:493
  4.8 17.3 %copy-start.1 = (f32[16,32,1024]{2,1,0:T(8,128)S(1)}, f32[16,32,1024]{2,1,0:T(8,128)}, u32[]{:S(2)}) copy-start(f32[16,32,1024]{2,1,0:T(8,128)} %sub.5) | copy-start | bytes 6291460
  4.8 17.3 %copy-start.3 = (f32[16,32,1024]{2,1,0:T(8,128)S(1)}, f32[16,32,1024]{2,1,0:T(8,128)}, u32[]{:S(2)}) copy-start(f32[16,32,1024]{2,1,0:T(8,128)} %cat.5) | copy-start | bytes 6291460
  4.8 11.7 %collective-permute-start.1 = (f32[2,2,16,1024]{3,2,1,0:T(8,128)S(1)}, f32[2,2,16,1024]{3,2,1,0:T(8,128)S(1)}, u32[]{:S(2)}, u32[]{:S(2)}) collective-permute-start(f32[2,2,16,1024]{3,2,1,0:T(8,128)S(1)} %get-tuple-element.48.own_low), channel_id=1, source_target_pairs={{0,7},{1,0},{2,1},{3,2},{4,3},{5,4},{6,5},{7,6},{8,15},{9,8},{10,9... | collective-permute-start | bytes 786440 | tf_op jit(solution)/shard_map/ppermute | solution.py:493
  10.1 10.1 %collective-permute-start.2 = (f32[2,32,1024]{2,1,0:T(8,128)S(1)}, f32[2,32,1024]{2,1,0:T(8,128)S(1)}, u32[]{:S(2)}, u32[]{:S(2)}) collective-permute-start(f32[2,32,1024]{2,1,0:T(8,128)S(1)} %get-tuple-element.52.up), channel_id=1, source_target_pairs={{0,8},{8,16},{16,24},{24,0},{1,9},{9,17},{17,25},{25,1},{2,10},{10... | collective-permute-start | bytes 786440 | tf_op jit(solution)/shard_map/ppermute | solution.py:493
  12.0 18.1 %collective-permute-start.3 = (f32[2,32,1024]{2,1,0:T(8,128)S(1)}, f32[2,32,1024]{2,1,0:T(8,128)S(1)}, u32[]{:S(2)}, u32[]{:S(2)}) collective-permute-start(f32[2,32,1024]{2,1,0:T(8,128)S(1)} %get-tuple-element.53.down), channel_id=1, source_target_pairs={{0,24},{8,0},{16,8},{24,16},{1,25},{9,1},{17,9},{25,17},{2,26},{10... | collective-permute-start | bytes 786440 | tf_op jit(solution)/shard_map/ppermute | solution.py:493
  13.1 17.9 %collective-permute-start.4 = (f32[2,16,1024]{2,1,0:T(8,128)S(1)}, f32[2,16,1024]{2,1,0:T(8,128)S(1)}, u32[]{:S(2)}, u32[]{:S(2)}) collective-permute-start(f32[2,16,1024]{2,1,0:T(8,128)S(1)} %get-tuple-element.43.q_up), channel_id=1, source_target_pairs={{0,8},{8,16},{16,24},{24,0},{1,9},{9,17},{17,25},{25,1},{2,10},{10... | collective-permute-start | bytes 393224 | tf_op jit(solution)/shard_map/ppermute | solution.py:493
  14.1 17.8 %collective-permute-start.5 = (f32[2,16,1024]{2,1,0:T(8,128)S(1)}, f32[2,16,1024]{2,1,0:T(8,128)S(1)}, u32[]{:S(2)}, u32[]{:S(2)}) collective-permute-start(f32[2,16,1024]{2,1,0:T(8,128)S(1)} %get-tuple-element.44.q_down), channel_id=1, source_target_pairs={{0,24},{8,0},{16,8},{24,16},{1,25},{9,1},{17,9},{25,17},{2,26},{10... | collective-permute-start | bytes 393224 | tf_op jit(solution)/shard_map/ppermute | solution.py:493
  16.6 16.8 %collective-permute-start.6 = (f32[2,16,1024]{2,1,0:T(8,128)S(1)}, f32[2,16,1024]{2,1,0:T(8,128)S(1)}, u32[]{:S(2)}, u32[]{:S(2)}) collective-permute-start(f32[2,16,1024]{2,1,0:T(8,128)S(1)} %get-tuple-element.66), channel_id=1, source_target_pairs={{0,8},{8,16},{16,24},{24,0},{1,9},{9,17},{17,25},{25,1},{2,10},{10... | collective-permute-start | bytes 393224 | tf_op jit(solution)/shard_map/ppermute | solution.py:493
  20.2 14.7 %collective-permute-start.7 = (f32[2,16,1024]{2,1,0:T(8,128)S(1)}, f32[2,16,1024]{2,1,0:T(8,128)S(1)}, u32[]{:S(2)}, u32[]{:S(2)}) collective-permute-start(f32[2,16,1024]{2,1,0:T(8,128)S(1)} %get-tuple-element.67), channel_id=1, source_target_pairs={{0,24},{8,0},{16,8},{24,16},{1,25},{9,1},{17,9},{25,17},{2,26},{10... | collective-permute-start | bytes 393224 | tf_op jit(solution)/shard_map/ppermute | solution.py:493
  35.0 7.6 %collective-permute-start.11 = (f32[3,32,256]{2,1,0:T(8,128)S(1)}, f32[3,32,256]{2,1,0:T(8,128)S(1)}, u32[]{:S(2)}, u32[]{:S(2)}) collective-permute-start(f32[3,32,256]{2,1,0:T(8,128)S(1)} %get-tuple-element.78), channel_id=1, source_target_pairs={{0,24},{8,16},{16,8},{24,0},{1,25},{9,17},{17,9},{25,1},{2,26},{10... | collective-permute-start | bytes 294920 | tf_op jit(solution)/shard_map/ppermute | solution.py:606
  36.5 6.1 %collective-permute-start.9 = (f32[3,32,256]{2,1,0:T(8,128)S(1)}, f32[3,32,256]{2,1,0:T(8,128)S(1)}, u32[]{:S(2)}, u32[]{:S(2)}) collective-permute-start(f32[3,32,256]{2,1,0:T(8,128)S(1)} %get-tuple-element.76), channel_id=1, source_target_pairs={{0,8},{8,0},{16,24},{24,16},{1,9},{9,1},{17,25},{25,17},{2,10},{10... | collective-permute-start | bytes 294920 | tf_op jit(solution)/shard_map/ppermute | solution.py:606
  37.0 4.1 %collective-permute-start.8 = (f32[3,16,256]{2,1,0:T(8,128)S(1)}, f32[3,16,256]{2,1,0:T(8,128)S(1)}, u32[]{:S(2)}, u32[]{:S(2)}) collective-permute-start(f32[3,16,256]{2,1,0:T(8,128)S(1)} %get-tuple-element.74), channel_id=1, source_target_pairs={{0,16},{8,24},{16,0},{24,8},{1,17},{9,25},{17,1},{25,9},{2,18},{10... | collective-permute-start | bytes 147464 | tf_op jit(solution)/shard_map/ppermute | solution.py:606
  38.6 4.1 %collective-permute-start.10 = (f32[3,16,256]{2,1,0:T(8,128)S(1)}, f32[3,16,256]{2,1,0:T(8,128)S(1)}, u32[]{:S(2)}, u32[]{:S(2)}) collective-permute-start(f32[3,16,256]{2,1,0:T(8,128)S(1)} %get-tuple-element.77), channel_id=1, source_target_pairs={{0,16},{8,24},{16,0},{24,8},{1,17},{9,25},{17,1},{25,9},{2,18},{10... | collective-permute-start | bytes 147464 | tf_op jit(solution)/shard_map/ppermute | solution.py:606
